TPU v7x, 64 devices: a 2x2x8 block of a 4x4x8 slice. The times are simulated.
64 devices in a mesh: dp: 4 (over x, y), tp: 16 (over z, core).
Axes of the slice: x: 2, y: 2, z: 8, core: 2. Of those that a mesh axis runs over, the one named last changes fastest.
The devices are a block of a 4x4x8 slice.
Arguments:
- act_in: bfloat16 [384, 64, 2048], P('dp'), parts along dimension 0
- ln_gain: float32 [2, 2048], replicated
- ln_bias: float32 [2, 2048], replicated
- w_qkv: bfloat16 [2, 2048, 16, 384], P(None, None, 'tp')
- w_out: bfloat16 [2, 2048, 2048], P(None, 'tp')
- w_up: bfloat16 [2, 2048, 8192], P(None, None, 'tp')
- w_down: bfloat16 [2, 8192, 2048], P(None, 'tp')
Outputs:
- output: bfloat16 [384, 64, 2048], P('dp'), parts along dimension 0
There are 4 independent parts. A program takes and returns all parts, laid end to end along the dimension named above; an argument that names none is the same for every part.
All inputs are finite; a program needn't handle non-finite values.
Results may differ from a plain program's by a relative error of at most 0.02.
Values are sent between devices in bfloat16 or wider.
A program may use at most 768 MiB of HBM per device.

v0:
```python
import jax
import jax.numpy as jnp
from jax import lax
from jax.sharding import PartitionSpec as P

LN_EPS = 1e-5
ROPE_BASE = 10000.0


def layer_norm(hidden, gain, bias):
    hidden_f = hidden.astype(jnp.float32)
    row_mean = jnp.mean(hidden_f, axis=-1, keepdims=True)
    centered = hidden_f - row_mean
    row_var = jnp.mean(centered * centered, axis=-1, keepdims=True)
    return (centered * lax.rsqrt(row_var + LN_EPS) * gain + bias).astype(jnp.bfloat16)


def rope_tables(seq_len, head_dim):
    half_dim = head_dim // 2
    inv_freq = ROPE_BASE ** (-2.0 * jnp.arange(half_dim, dtype=jnp.float32) / head_dim)
    angles = jnp.arange(seq_len, dtype=jnp.float32)[:, None] * inv_freq[None, :]
    return jnp.cos(angles), jnp.sin(angles)


def apply_rope(proj, cos_tab, sin_tab):
    half_dim = proj.shape[-1] // 2
    first = proj[..., :half_dim]
    second = proj[..., half_dim:]
    return jnp.concatenate([first * cos_tab - second * sin_tab, second * cos_tab + first * sin_tab], axis=-1)


def layer_partial(hidden, gain, bias, w_qkv, w_out, w_up, w_down):
    batch, seq_len, d_model = hidden.shape
    groups = w_qkv.shape[1]
    attn_width = w_out.shape[0]
    head_dim = (w_qkv.shape[2] - attn_width // groups) // 2
    group_heads = attn_width // (groups * head_dim)
    normed = layer_norm(hidden, gain, bias)
    qkv_proj = jnp.einsum("bsd,dgc->bsgc", normed, w_qkv, preferred_element_type=jnp.float32)
    qkv_proj = qkv_proj.reshape(batch, seq_len, groups, group_heads + 2, head_dim)
    cos_tab, sin_tab = rope_tables(seq_len, head_dim)
    query = apply_rope(qkv_proj[:, :, :, :group_heads], cos_tab[None, :, None, None, :], sin_tab[None, :, None, None, :]).astype(jnp.bfloat16)
    keys = apply_rope(qkv_proj[:, :, :, group_heads], cos_tab[None, :, None, :], sin_tab[None, :, None, :]).astype(jnp.bfloat16)
    values = qkv_proj[:, :, :, group_heads + 1].astype(jnp.bfloat16)
    scores = jnp.einsum("bsgrd,btgd->bgrst", query, keys, preferred_element_type=jnp.float32) * (head_dim ** -0.5)
    positions = jnp.arange(seq_len)
    allowed = positions[:, None] >= positions[None, :]
    scores = jnp.where(allowed, scores, -1e30)
    attn_probs = jax.nn.softmax(scores, axis=-1).astype(jnp.bfloat16)
    context = jnp.einsum("bgrst,btgd->bgrsd", attn_probs, values, preferred_element_type=jnp.float32).astype(jnp.bfloat16)
    out_heads = w_out.reshape(groups, group_heads, head_dim, d_model)
    attn_part = jnp.einsum("bgrsd,grde->bse", context, out_heads, preferred_element_type=jnp.float32)
    up_proj = jnp.einsum("bsd,df->bsf", normed, w_up, preferred_element_type=jnp.float32)
    gelu_out = jax.nn.gelu(up_proj, approximate=False).astype(jnp.bfloat16)
    mlp_part = jnp.einsum("bsf,fe->bse", gelu_out, w_down, preferred_element_type=jnp.float32)
    return attn_part + mlp_part


def solution(mesh):
    def shard_body(act_in, ln_gain, ln_bias, w_qkv, w_out, w_up, w_down):
        hidden = act_in
        for layer_idx in range(ln_gain.shape[0]):
            local_sum = layer_partial(hidden, ln_gain[layer_idx], ln_bias[layer_idx], w_qkv[layer_idx], w_out[layer_idx], w_up[layer_idx], w_down[layer_idx]).astype(jnp.bfloat16)
            reduced = lax.psum(local_sum, "tp")
            hidden = (hidden.astype(jnp.float32) + reduced.astype(jnp.float32)).astype(jnp.bfloat16)
        return hidden

    return jax.shard_map(shard_body, mesh=mesh, in_specs=(P("dp", None, None), P(None, None), P(None, None), P(None, None, "tp", None), P(None, "tp", None), P(None, None, "tp"), P(None, "tp", None)), out_specs=P("dp", None, None), check_vma=False)
```

profile of v0, /device:TPU:21, one launch (start us, length us, event | category | flops | bytes accessed | tf_op | source)
XLA Modules:
  0.0 895.5 jit_solution(6275242856294753370)
XLA Ops:
  6.6 1.4 fusion.268
  9.4 10.0 %convert_reduce_fusion.1 = f32[96,64]{1,0:T(8,128)S(1)} fusion(bf16[96,64,2048]{2,1,0:T(8,128)(2,1)} %param.7), kind=kLoop, calls=%fused_computation.5 | loop fusion | flops 25159680 | bytes 25190400 | tf_op jit(solution)/shard_map/reduce_sum | solution.py:12
  19.4 5.5 copy-done
  24.9 8.3 fusion.8
  33.4 1.4 slice_bitcast_fusion.3
  35.6 18.5 %fusion.117 = f32[96,64,1,3,128]{4,1,3,0,2:T(8,128)S(1)} fusion(bf16[3,128,2048,1]{2,1,0,3:T(8,128)(2,1)S(1)} %bitcast.183, f32[2048]{0:T(1024)S(1)} %bitcast.190, f32[2048]{0:T(1024)S(1)} %bitcast.188, f32[96,64]{1,0:T(8,128)S(1)} %add_rsqrt_fusion.1, f32[96,64]{1,0:T(8,128)S(1)} %broadcast_multiply_fusion.1, bf16[96,64,2048]{2,1,0:T(8,128)(2,1)} %param.7), kind=kOutput, calls=%fused_computation.127 | convolution fusion | flops 9739173888 | bytes 36241408 | tf_op jit(solution)/shard_map/bsd,dgc->bsgc/dot_general | solution.py:39
  56.4 3.1 copy-done.4
  59.4 1.6 fusion.298
  62.2 2.3 fusion.125
  65.4 21.3 %fusion.176 = f32[96,64,2048]{2,1,0:T(8,128)} fusion(f32[96,64,1,3,128]{4,1,3,0,2:T(8,128)} %copy-done.2, f32[96,64,64]{2,1,0:T(8,128)S(1)} %get-tuple-element.22, f32[96,64]{1,0:T(8,128)S(1)} %fusion.123, f32[96,64]{1,0:T(8,128)S(1)} %get-tuple-element.21, pred[64,64]{0,1:T(8,128)(4,1)S(1)} %iota_compare_fusion, bf16[2,128,2048]{2,1,0:T(8,128)(2,1)} %param.11), kind=kOutput, calls=%fused_computation.195 | convolution fusion | flops 3324641280 | bytes 54054912 | tf_op jit(solution)/shard_map/bgrsd,grde->bse/dot_general | solution.py:52
  86.8 61.6 %add_convert_fusion.1 = bf16[96,64,2048]{2,1,0:T(8,128)(2,1)} fusion(f32[96,64,2048]{2,1,0:T(8,128)} %fusion.176, bf16[96,64,2048]{2,1,0:T(8,128)(2,1)} %param.7, f32[2048]{0:T(1024)S(1)} %bitcast.191, f32[2048]{0:T(1024)S(1)} %bitcast.189, f32[96,64]{1,0:T(8,128)S(1)} %add_rsqrt_fusion.1, f32[96,64]{1,0:T(8,128)S(1)} %broadcast_multiply_fusion.1, ...), kind=kOutput, calls=%fused_computation.21 | convolution fusion | flops 26074939392 | bytes 104923136 | tf_op jit(solution)/shard_map/bsf,fe->bse/dot_general | solution.py:55
  150.7 3.2 fusion.296
  153.8 276.3 %all-reduce.3.cloned.1.call-done = bf16[96,64,2048]{2,1,0:T(8,128)(2,1)} async-done(((bf16[96,64,2048]{2,1,0:T(8,128)(2,1)}), bf16[96,64,2048]{2,1,0:T(8,128)(2,1)}) %all-reduce.3.cloned.1.call-update) | async-done | bytes 25165840 | tf_op jit(solution)/shard_map/psum | solution.py:64
  430.2 27.6 %convert_reduce_fusion = (f32[96,64]{1,0:T(8,128)S(1)}, bf16[96,64,2048]{2,1,0:T(8,128)(2,1)}) fusion(bf16[96,64,2048]{2,1,0:T(8,128)(2,1)} %all-reduce.3.cloned.1.call-done, bf16[96,64,2048]{2,1,0:T(8,128)(2,1)} %param.7), kind=kLoop, calls=%fused_computation.2 | loop fusion | flops 75491328 | bytes 75522048 | tf_op jit(solution)/shard_map/reduce_sum | solution.py:12
  457.8 13.6 %fusion.4 = f32[96,64]{1,0:T(8,128)S(1)} fusion(bf16[96,64,2048]{2,1,0:T(8,128)(2,1)} %get-tuple-element.6, f32[96,64]{1,0:T(8,128)S(1)} %broadcast_multiply_fusion), kind=kLoop, calls=%fused_computation.10 | loop fusion | flops 50325504 | bytes 25214976 | tf_op jit(solution)/shard_map/reduce_sum | solution.py:14
  471.4 1.9 copy-done.1
  473.3 16.1 %fusion.114 = f32[96,64,1,3,128]{4,1,0,3,2:T(8,128)} fusion(bf16[3,128,2048,1]{2,1,3,0:T(8,128)(2,1)S(1)} %bitcast.182, f32[2048]{0:T(1024)S(1)} %bitcast.186, f32[2048]{0:T(1024)S(1)} %bitcast.184, f32[96,64]{1,0:T(8,128)S(1)} %add_rsqrt_fusion, f32[96,64]{1,0:T(8,128)S(1)} %broadcast_multiply_fusion, bf16[96,64,2048]{2,1,0:T(8,128)(2,1)S(1)} %copy-done.1), kind=kOutput, calls=%fused_computation.126 | convolution fusion | flops 9739173888 | bytes 36241408 | tf_op jit(solution)/shard_map/bsd,dgc->bsgc/dot_general | solution.py:39
  489.4 2.3 slice_bitcast_fusion
  491.7 4.0 fusion.143
  496.9 2.3 fusion.126
  500.2 21.3 %fusion.170 = f32[96,64,2048]{2,1,0:T(8,128)} fusion(f32[96,64,1,3,128]{4,1,0,3,2:T(8,128)} %fusion.114, f32[96,64,64]{2,1,0:T(8,128)S(1)} %get-tuple-element.24, f32[96,64]{1,0:T(8,128)S(1)} %fusion.124, f32[96,64]{1,0:T(8,128)S(1)} %get-tuple-element.23, pred[64,64]{0,1:T(8,128)(4,1)S(1)} %copy-done.11, bf16[2,128,2048]{2,1,0:T(8,128)(2,1)} %param.11), kind=kOutput, calls=%fused_computation.192 | convolution fusion | flops 3324641280 | bytes 54054912 | tf_op jit(solution)/shard_map/bgrsd,grde->bse/dot_general | solution.py:52
  521.5 61.3 %add_convert_fusion = bf16[96,64,2048]{2,1,0:T(8,128)(2,1)} fusion(f32[96,64,2048]{2,1,0:T(8,128)} %fusion.170, bf16[96,64,2048]{2,1,0:T(8,128)(2,1)} %get-tuple-element.6, f32[2048]{0:T(1024)S(1)} %bitcast.187, f32[2048]{0:T(1024)S(1)} %bitcast.185, f32[96,64]{1,0:T(8,128)S(1)} %add_rsqrt_fusion, f32[96,64]{1,0:T(8,128)S(1)} %broadcast_multiply_fusion, ...), kind=kOutput, calls=%fused_computation.20 | convolution fusion | flops 26074939392 | bytes 104923136 | tf_op jit(solution)/shard_map/bsf,fe->bse/dot_general | solution.py:55
  582.8 276.4 %all-reduce.5.cloned.1.call-done = bf16[96,64,2048]{2,1,0:T(8,128)(2,1)} async-done(((bf16[96,64,2048]{2,1,0:T(8,128)(2,1)}), bf16[96,64,2048]{2,1,0:T(8,128)(2,1)}) %all-reduce.5.cloned.1.call-update) | async-done | bytes 25165840 | tf_op jit(solution)/shard_map/psum | solution.py:64
  859.2 29.2 %fusion.13 = bf16[96,64,2048]{2,1,0:T(8,128)(2,1)} fusion(bf16[96,64,2048]{2,1,0:T(8,128)(2,1)} %get-tuple-element.6, bf16[96,64,2048]{2,1,0:T(8,128)(2,1)} %all-reduce.5.cloned.1.call-done), kind=kLoop, calls=%fused_computation.19 | loop fusion | flops 50331648 | bytes 75497472 | tf_op jit(solution)/shard_map/convert_element_type | solution.py:65
  (46 shorter events, 11.3 us)
Async XLA Ops:
  6.5 423.6 %all-reduce.3.cloned.1.call-start = ((), (), s32[]{:S(2)}) async-start(), calls=%async_computation | async-start | bytes 50331648 | tf_op jit(solution)/shard_map/psum | solution.py:64
  6.6 58.8 %copy-start.10 = (pred[64,64]{0,1:T(8,128)(4,1)}, pred[64,64]{0,1:T(8,128)(4,1)S(1)}, u32[]{:S(2)}) copy-start(pred[64,64]{0,1:T(8,128)(4,1)S(1)} %iota_compare_fusion) | copy-start | bytes 12292
  9.4 15.5 %copy-start = (bf16[96,64,2048]{2,1,0:T(8,128)(2,1)S(1)}, bf16[96,64,2048]{2,1,0:T(8,128)(2,1)}, u32[]{:S(2)}) copy-start(bf16[96,64,2048]{2,1,0:T(8,128)(2,1)} %param.7) | copy-start | bytes 75497472
  24.9 8.5 copy-start.5
  33.3 27.7 %copy-start.6 = (f32[64,64]{1,0:T(8,128)}, f32[64,64]{1,0:T(8,128)S(1)}, u32[]{:S(2)}) copy-start(f32[64,64]{1,0:T(8,128)S(1)} %get-tuple-element.19) | copy-start | bytes 49156
  33.4 27.6 %copy-start.8 = (f32[64,64]{1,0:T(8,128)}, f32[64,64]{1,0:T(8,128)S(1)}, u32[]{:S(2)}) copy-start(f32[64,64]{1,0:T(8,128)S(1)} %get-tuple-element.20) | copy-start | bytes 49156
  54.1 6.9 copy-start.2
  54.1 5.3 copy-start.4
  148.3 1.4 copy-start.3
  148.4 710.8 %all-reduce.5.cloned.1.call-start = ((), (), s32[]{:S(2)}) async-start(), calls=%async_computation.1 | async-start | bytes 50331648 | tf_op jit(solution)/shard_map/psum | solution.py:64
  457.7 15.6 %copy-start.1 = (bf16[96,64,2048]{2,1,0:T(8,128)(2,1)S(1)}, bf16[96,64,2048]{2,1,0:T(8,128)(2,1)}, u32[]{:S(2)}) copy-start(bf16[96,64,2048]{2,1,0:T(8,128)(2,1)} %get-tuple-element.6) | copy-start | bytes 75497472
  457.8 15.6 %copy-start.12 = (f32[1,2048]{1,0:T(1,128)S(1)}, f32[1,2048]{1,0:T(1,128)}, u32[]{:S(2)}) copy-start(f32[1,2048]{1,0:T(1,128)} %get-tuple-element.15) | copy-start | bytes 24580
  457.8 15.6 %copy-start.13 = (f32[1,2048]{1,0:T(1,128)S(1)}, f32[1,2048]{1,0:T(1,128)}, u32[]{:S(2)}) copy-start(f32[1,2048]{1,0:T(1,128)} %get-tuple-element.17) | copy-start | bytes 24580
  473.3 18.4 %copy-start.7 = (f32[64,64]{1,0:T(8,128)S(1)}, f32[64,64]{1,0:T(8,128)}, u32[]{:S(2)}) copy-start(f32[64,64]{1,0:T(8,128)} %copy-done.6) | copy-start | bytes 49156
  473.3 18.4 %copy-start.9 = (f32[64,64]{1,0:T(8,128)S(1)}, f32[64,64]{1,0:T(8,128)}, u32[]{:S(2)}) copy-start(f32[64,64]{1,0:T(8,128)} %copy-done.8) | copy-start | bytes 49156
  489.4 7.5 copy-start.11
Sparse Core Ops, SparseCore 0:
  148.5 281.6 all-reduce.2
  582.9 276.1 all-reduce.4
where the time goes:
time: 901 us; the launch traced here: 895 us
  waiting for transfers between devices  553 us (61%)
  matrix products  205 us (23%)
  other arithmetic  99 us (11%)
  local copies, waits for them, and re-layouts  25.1 us (3%)
  between operations  14 us (2%)
    psum x2, waiting for transfers between devices, shard_body(): reduced = lax.psum(local_sum, 'tp')  553 us
    dot_general x2, matrix products, layer_partial(): jnp.einsum('bsf,fe->bse', gelu_out, w_down, preferred_element_type=jnp.fl...  123 us
    dot_general x2, matrix products, layer_partial(): jnp.einsum('bgrsd,grde->bse', context, out_heads, preferred_element_type=...  42.6 us
    reduce_sum x2, other arithmetic, layer_norm(): row_mean = jnp.mean(hidden_f, axis=-1, keepdims=True)  37.5 us
    dot_general x2, matrix products, layer_partial(): jnp.einsum('bsd,dgc->bsgc', normed, w_qkv, preferred_element_type=jnp.flo...  34.6 us
    convert_element_type x1, other arithmetic, shard_body(): (hidden.astype(jnp.float32) + reduced.astype(jnp.float32)).astype(jnp.bfl...  29.2 us
    reduce_sum x2, other arithmetic, layer_norm(): row_var = jnp.mean(centered * centered, axis=-1, keepdims=True)  21.9 us
  transfers between devices with their start and end apart: 2, of which 2 were waited for; matrix products, arithmetic and copies ran while one was open for 0% of the time, Pallas kernels for 0%

commit v1 on v0

v1 whole, which is shorter than its diff:
```python
import functools
import math

import jax
import jax.numpy as jnp
from jax import lax
from jax.experimental import pallas as pl
from jax.experimental.pallas import tpu as pltpu
from jax.sharding import PartitionSpec as P

LN_EPS = 1e-5
ROPE_BASE = 10000.0
MESH = pl.DeviceIdType.MESH
BF16 = jnp.bfloat16
F32 = jnp.float32
LANES = 128
UP, Q, K, V, DOWN, OUT = range(6)


def norm_rows(hidden_f, gain, bias):
    row_mean = jnp.mean(hidden_f, axis=-1, keepdims=True)
    centered = hidden_f - row_mean
    row_var = jnp.mean(centered * centered, axis=-1, keepdims=True)
    return (centered * lax.rsqrt(row_var + LN_EPS) * gain + bias).astype(BF16)


def rope(heads, cos, sin):
    return (heads * cos + pltpu.roll(heads, heads.shape[-1] // 2, 1) * sin).astype(BF16)


def gelu(values):
    return (0.5 * values * (1.0 + lax.erf(values * math.sqrt(0.5)))).astype(BF16)


def attend(query, keys, values, seq_len):
    rows, head_dim = query.shape
    scores = lax.dot_general(query, keys, (((1,), (1,)), ((), ())), preferred_element_type=F32) * (head_dim ** -0.5)
    row = lax.broadcasted_iota(jnp.int32, (rows, rows), 0)
    col = lax.broadcasted_iota(jnp.int32, (rows, rows), 1)
    allowed = (row >= col) & (row // seq_len == col // seq_len)
    scores = jnp.where(allowed, scores, -1e30)
    weights = jnp.exp(scores - jnp.max(scores, axis=-1, keepdims=True))
    probs = (weights / jnp.sum(weights, axis=-1, keepdims=True)).astype(BF16)
    return jnp.dot(probs, values, preferred_element_type=F32).astype(BF16)


def branches(normed, qkv_w, up_w, cos_ref, sin_ref, ctx, act, seq_len):
    head_dim = cos_ref.shape[1]
    for head in range(ctx.shape[1] // head_dim):
        cols = pl.ds(3 * head_dim * head, 3 * head_dim)
        proj = jnp.dot(normed[...], qkv_w[:, cols], preferred_element_type=F32)
        query = rope(proj[:, :head_dim], cos_ref[...], sin_ref[...])
        keys = rope(proj[:, head_dim : 2 * head_dim], cos_ref[...], sin_ref[...])
        values = proj[:, 2 * head_dim :].astype(BF16)
        ctx[:, pl.ds(head * head_dim, head_dim)] = attend(query, keys, values, seq_len)
    step = 512
    for first in range(0, act.shape[1], step):
        cols = pl.ds(first, step)
        act[:, cols] = gelu(jnp.dot(normed[...], up_w[:, cols], preferred_element_type=F32))


class Place:
    def __init__(self, n_dp, n_tp):
        side = math.isqrt(n_dp)
        assert side * side == n_dp and side % 2 == 0 and n_tp % 4 == 0
        self.n_tp, self.nz = n_tp, n_tp // 2
        self.dp, self.tp = lax.axis_index("dp"), lax.axis_index("tp")
        self.z, self.core = self.tp // 2, self.tp % 2
        x, y = self.dp // side, self.dp % side
        xf, yf = x + 1 - 2 * (x % 2), y + 1 - 2 * (y % 2)
        self.q = (x % 2) * 2 + y % 2
        self.peers = [{"dp": xf * side + y}, {"dp": x * side + yf}, {"dp": xf * side + yf}]
        self.peer_q = [(1 - x % 2) * 2 + y % 2, (x % 2) * 2 + 1 - y % 2, (1 - x % 2) * 2 + 1 - y % 2]
        self.sib = {"tp": 2 * self.z + 1 - self.core}
        self.right = {"tp": 2 * ((self.z + 1) % self.nz) + self.core}
        self.left = {"tp": 2 * ((self.z + self.nz - 1) % self.nz) + self.core}

    def meet(self):
        barrier = pltpu.get_barrier_semaphore()
        others = [self.sib, self.right, self.left, *self.peers]
        for other in others:
            pl.semaphore_signal(barrier, inc=1, device_id=other, device_id_type=MESH)
        pl.semaphore_wait(barrier, len(others))


def remote(src, dst, send_sem, recv_sem, device):
    return pltpu.make_async_remote_copy(src_ref=src, dst_ref=dst, send_sem=send_sem, recv_sem=recv_sem, device_id=device, device_id_type=MESH)


def piece(kind, source, n_tp, cols, rows):
    if kind == UP:
        return cols.at[source]
    if kind == DOWN:
        return rows.at[source]
    if kind == OUT:
        return rows.at[n_tp + source // 4]
    return cols.at[n_tp + 3 * (source // 4) + kind - Q]


def first_kernel(n_dp, n_tp, x, gains, biases, cos_ref, sin_ref, qkv, out_w, up, down,
                 y1, nall, gcols, grows,
                 qkv_v, out_v, up_v, down_v, xbuf, normed, ctx, act, own, sib_out, sib_in, ring_r, ring_l, nown, st_cols, st_rows,
                 w_sem, x_sem, sib_send, sib_recv, r_send, r_recv, l_send, l_recv,
                 st_sem, own_sem, loc_sem, wr_recv, wr_send, ws_send, ws_recv, n_send, n_recv, n_loc):
    me = Place(n_dp, n_tp)
    nz, core, z, q = me.nz, me.core, me.z, me.q
    n_seq, seq_len, d_model = x.shape
    per = n_seq // n_tp
    half = per // 2
    steps = nz * half

    first_w = [pltpu.make_async_copy(src.at[0], dst, w_sem.at[i]) for i, (src, dst) in enumerate(((qkv, qkv_v), (up, up_v), (out_w, out_v), (down, down_v)))]

    def owner_seq(zo, co, j):
        return per * (2 * zo + co) + j

    def tile_seqs(i):
        s, j = i // half, i % half
        zr, zl = (z + 2 * nz - 1 - s) % nz, (z + 1 + s) % nz
        return [owner_seq(zr, core, j), owner_seq(zl, core, half + j), owner_seq(zr, 1 - core, j), owner_seq(zl, 1 - core, half + j)]

    def fetch(i):
        for place, seq in enumerate(tile_seqs(i)):
            pltpu.make_async_copy(x.at[seq], xbuf.at[i % 3, place], x_sem.at[i % 3]).start()

    fetch(0)
    for copy in first_w:
        copy.start()
    head_dim = out_w.shape[1]
    loads = {UP: (up.at[1, :, pl.ds(pl.multiple_of(q * LANES, LANES), LANES)], st_cols.at[UP]),
             DOWN: (down.at[1, pl.ds(pl.multiple_of(q * LANES, LANES), LANES), :], st_rows.at[0]),
             OUT: (out_w.at[1], st_rows.at[1])}
    for kind in (Q, K, V):
        loads[kind] = (qkv.at[1, :, pl.ds((kind - Q) * head_dim, head_dim)], st_cols.at[kind])
    kinds = (UP, DOWN, Q, K, V, OUT)
    loads = {kind: pltpu.make_async_copy(*loads[kind], st_sem.at[kind]) for kind in kinds}
    for kind in kinds:
        loads[kind].start()
    me.meet()

    def has(kind, source):
        return source >= 0 if kind in (UP, DOWN) else source % 4 == q

    def staged(kind):
        return st_rows.at[kind - DOWN] if kind >= DOWN else st_cols.at[kind]

    def first_hops(kind):
        src, dst = staged(kind), piece(kind, me.tp, n_tp, gcols, grows)
        return [remote(src, dst, own_sem.at[0, kind], wr_recv.at[0, 0, kind], me.right),
                remote(src, dst, own_sem.at[1, kind], wr_recv.at[1, 0, kind], me.left),
                remote(src, dst, own_sem.at[2, kind], ws_recv.at[z, kind], me.sib),
                pltpu.make_async_copy(src, dst, loc_sem.at[kind])]

    for kind in kinds:
        loads[kind].wait()

        @pl.when(has(kind, me.tp))
        def _():
            for copy in first_hops(kind):
                copy.start()

    for i in range(half):
        ring_r[i] = jnp.zeros(ring_r.shape[1:], BF16)
        ring_l[i] = jnp.zeros(ring_l.shape[1:], BF16)

    def send_sib(i):
        return remote(sib_out.at[i % 2], sib_in.at[i % 4], sib_send.at[i % 2], sib_recv.at[i % 4], me.sib)

    def send_r(i):
        return remote(ring_r.at[i], ring_r.at[i + half], r_send.at[i], r_recv.at[i + half], me.right)

    def send_l(i):
        return remote(ring_l.at[i], ring_l.at[i + half], l_send.at[i], l_recv.at[i + half], me.left)

    def send_n(seq, peer):
        return remote(nown.at[seq], nall.at[seq, q], n_send.at[peer, seq], n_recv.at[peer, seq], me.peers[peer])

    def wait_n(seq, peer):
        return remote(nown.at[seq], nall.at[seq, me.peer_q[peer]], n_send.at[peer, seq], n_recv.at[peer, seq], me.peers[peer])

    def keep_n(seq):
        return pltpu.make_async_copy(nown.at[seq], nall.at[seq, q], n_loc.at[seq])

    for copy in first_w:
        copy.wait()

    def compute(i):
        slot = i % 3
        pltpu.make_async_copy(x.at[pl.ds(0, 4)], xbuf.at[slot], x_sem.at[slot]).wait()

        @pl.when(i + 1 < steps)
        def _():
            fetch(i + 1)

        rows = 16

        def norm(k, carry):
            at = pl.ds(pl.multiple_of(k % (seq_len // rows) * rows, rows), rows)
            tile = xbuf[slot, k // (seq_len // rows), at, :].astype(F32)
            normed[pl.ds(pl.multiple_of(k * rows, rows), rows), :] = norm_rows(tile, gains[pl.ds(0, 1), :], biases[pl.ds(0, 1), :])
            return carry

        lax.fori_loop(0, 4 * seq_len // rows, norm, 0, unroll=2)
        branches(normed, qkv_v, up_v, cos_ref, sin_ref, ctx, act, seq_len)

        @pl.when(i >= 2)
        def _():
            send_sib(i - 2).wait_send()

        step = 512
        for first in range(0, d_model, step):
            cols = pl.ds(first, step)
            part = jnp.dot(ctx[...], out_v[:, cols], preferred_element_type=F32) + jnp.dot(act[...], down_v[:, cols], preferred_element_type=F32)
            own[i % 2, :, cols] = part[: 2 * seq_len]
            sib_out[i % 2, :, cols] = part[2 * seq_len :].astype(BF16)
        send_sib(i).start()

    def finish(i):
        send_sib(i).wait_recv()

        @pl.when(i >= half)
        def _():
            send_r(i - half).wait_recv()
            send_l(i - half).wait_recv()

        last = i >= steps - half

        @pl.when(jnp.logical_not(last))
        def _():
            for side, ring in enumerate((ring_r, ring_l)):
                at = pl.ds(side * seq_len, seq_len)
                ring[i] = (own[i % 2, at, :] + sib_in[i % 4, at, :].astype(F32) + ring[i].astype(F32)).astype(BF16)
            send_r(i).start()
            send_l(i).start()

        @pl.when(last)
        def _():
            rows = 16
            for side, ring in enumerate((ring_r, ring_l)):
                seq = side * half + i % half

                def close(k, carry):
                    at = pl.ds(pl.multiple_of(k * rows, rows), rows)
                    both = pl.ds(pl.multiple_of(side * seq_len + k * rows, rows), rows)
                    update = (own[i % 2, both, :] + sib_in[i % 4, both, :].astype(F32) + ring[i, at, :].astype(F32)).astype(BF16)
                    hidden = (xbuf[i % 3, side, at, :].astype(F32) + update.astype(F32)).astype(BF16)
                    y1[seq, at, :] = hidden
                    nown[seq, at, :] = norm_rows(hidden.astype(F32), gains[pl.ds(1, 1), :], biases[pl.ds(1, 1), :])
                    return carry

                lax.fori_loop(0, seq_len // rows, close, 0)
                for peer in range(3):
                    send_n(seq, peer).start()
                keep_n(seq).start()

    def turn(i, carry):
        @pl.when(i < steps)
        def _():
            compute(i)

        @pl.when(i >= 1)
        def _():
            finish(i - 1)

        return carry

    lax.fori_loop(0, steps + 1, turn, 0)

    hops = (nz // 2 - core, nz // 2 - 1 + core)
    to = (me.right, me.left)

    def source_of(side, s):
        zs = (z + nz - s) % nz if side == 0 else (z + s) % nz
        return 2 * zs + core

    def onward(side, s, kind):
        at = piece(kind, source_of(side, s), n_tp, gcols, grows)
        return remote(at, at, wr_send.at[side, s - 1, kind], wr_recv.at[side, s, kind], to[side])

    def arrival(side, s, kind):
        at = piece(kind, source_of(side, s), n_tp, gcols, grows)
        return remote(at, at, wr_send.at[side, s - 1, kind], wr_recv.at[side, s - 1, kind], to[side])

    def across(side, s, kind):
        source = source_of(side, s)
        at = piece(kind, source, n_tp, gcols, grows)
        return remote(at, at, ws_send.at[side, s - 1, kind], ws_recv.at[source // 2, kind], me.sib)

    for s in range(1, nz // 2 + 1):
        for kind in kinds:
            for side in range(2):
                @pl.when(has(kind, source_of(side, s)) & (s <= hops[side]))
                def _():
                    arrival(side, s, kind).wait_recv()

                    @pl.when(s < hops[side])
                    def _():
                        onward(side, s, kind).start()

                    across(side, s, kind).start()

    def drain(i, carry):
        send_r(i).wait_send()
        send_l(i).wait_send()
        return carry

    lax.fori_loop(0, steps - half, drain, 0)
    send_sib(steps - 2).wait_send()
    send_sib(steps - 1).wait_send()
    for seq in range(per):
        for peer in range(3):
            send_n(seq, peer).wait_send()
            wait_n(seq, peer).wait_recv()
        keep_n(seq).wait()
    for kind in kinds:
        @pl.when(has(kind, me.tp))
        def _():
            right, left, sib, local = first_hops(kind)
            right.wait_send()
            left.wait_send()
            sib.wait_send()
            local.wait()

        for s in range(1, nz // 2 + 1):
            for side in range(2):
                @pl.when(has(kind, source_of(side, s)) & (s <= hops[side]))
                def _():
                    @pl.when(s < hops[side])
                    def _():
                        onward(side, s, kind).wait_send()

                    across(side, s, kind).wait_send()

        for zs in range(nz):
            source = 2 * zs + 1 - core

            @pl.when(has(kind, source))
            def _():
                at = piece(kind, source, n_tp, gcols, grows)
                remote(at, at, own_sem.at[2, kind], ws_recv.at[zs, kind], me.sib).wait_recv()


def second_kernel(n_dp, n_tp, y1, nall, gcols, grows, cos_ref, sin_ref, out,
                  qkv_v, out_v, up_v, down_v, nbuf, normed, ctx, act, own, part_out, part_in, ybuf,
                  w_sem, n_sem, p_send, p_recv, own_send, loc_sem, r_recv, f_send, s_send, s_recv):
    me = Place(n_dp, n_tp)
    nz, core, z, q = me.nz, me.core, me.z, me.q
    per, members, seq_len, d_model = nall.shape
    head_dim = cos_ref.shape[1]

    def fetch(i):
        return pltpu.make_async_copy(nall.at[i], nbuf.at[i % 2], n_sem.at[i % 2])

    fetch(0).start()
    n_cols, n_rows = gcols.shape[0], grows.shape[0]
    loads = []
    for i in range(n_cols - n_tp):
        loads.append((gcols.at[n_tp + i], qkv_v.at[:, pl.ds(i * LANES, LANES)]))
    for i in range(n_tp):
        loads.append((gcols.at[i], up_v.at[:, pl.ds(i * LANES, LANES)]))
    for i in range(n_rows - n_tp):
        loads.append((grows.at[n_tp + i], out_v.at[pl.ds(i * LANES, LANES), :]))
    for i in range(n_tp):
        loads.append((grows.at[i], down_v.at[pl.ds(i * LANES, LANES), :]))
    loads = [pltpu.make_async_copy(src, dst, w_sem.at[i]) for i, (src, dst) in enumerate(loads)]
    for copy in loads:
        copy.start()
    me.meet()
    for copy in loads:
        copy.wait()

    def send_part(i, peer):
        return remote(part_out.at[i % 2, me.peer_q[peer]], part_in.at[i, peer], p_send.at[i % 2, peer], p_recv.at[i, peer], me.peers[peer])

    def seq_of(zs, co, i):
        return per * (2 * zs + co) + i

    def first_hops(i):
        src, dst = ybuf.at[i], out.at[seq_of(z, core, i)]
        return [remote(src, dst, own_send.at[0, i], r_recv.at[0, i, 0], me.right),
                remote(src, dst, own_send.at[1, i], r_recv.at[1, i, 0], me.left),
                remote(src, dst, own_send.at[2, i], s_recv.at[z, i], me.sib),
                pltpu.make_async_copy(src, dst, loc_sem.at[i])]

    to = (me.right, me.left)

    def hops(side, i):
        longer = (i + core) % 2
        return nz // 2 - longer if side == 0 else nz // 2 - 1 + longer

    def z_of(side, s):
        return (z + nz - s) % nz if side == 0 else (z + s) % nz

    def arrival(side, i, s):
        at = out.at[seq_of(z_of(side, s), core, i)]
        return remote(at, at, f_send.at[side, i, s - 1], r_recv.at[side, i, s - 1], to[side])

    def onward(side, i, s):
        at = out.at[seq_of(z_of(side, s), core, i)]
        return remote(at, at, f_send.at[side, i, s - 1], r_recv.at[side, i, s], to[side])

    def across(side, i, s):
        at = out.at[seq_of(z_of(side, s), core, i)]
        return remote(at, at, s_send.at[side, i, s - 1], s_recv.at[z_of(side, s), i], me.sib)

    def compute(i):
        fetch(i).wait()

        @pl.when(i + 1 < per)
        def _():
            fetch(i + 1).start()

        for member in range(members):
            normed[pl.ds(member * seq_len, seq_len), :] = nbuf[i % 2, member]
        branches(normed, qkv_v, up_v, cos_ref, sin_ref, ctx, act, seq_len)

        @pl.when(i >= 2)
        def _():
            for peer in range(3):
                send_part(i - 2, peer).wait_send()

        step = 512
        for first in range(0, d_model, step):
            cols = pl.ds(first, step)
            part = jnp.dot(ctx[...], out_v[:, cols], preferred_element_type=F32) + jnp.dot(act[...], down_v[:, cols], preferred_element_type=F32)
            for member in range(members):
                rows = part[member * seq_len : (member + 1) * seq_len]
                part_out[i % 2, member, :, cols] = rows.astype(BF16)

                @pl.when(q == member)
                def _():
                    own[i % 2, :, cols] = rows
        for peer in range(3):
            send_part(i, peer).start()

    def finish(i):
        for peer in range(3):
            send_part(i, peer).wait_recv()
        total = own[i % 2]
        for peer in range(3):
            total = total + part_in[i, peer].astype(F32)
        ybuf[i] = (y1[i].astype(F32) + total.astype(BF16).astype(F32)).astype(BF16)
        for copy in first_hops(i):
            copy.start()

    def turn(t, carry):
        @pl.when(t < per)
        def _():
            compute(t)

        @pl.when((t >= 1) & (t <= per))
        def _():
            finish(t - 1)

        for s in range(1, nz // 2 + 1):
            i = t - 1 - s

            @pl.when((i >= 0) & (i < per))
            def _():
                for side in range(2):
                    @pl.when(s <= hops(side, i))
                    def _():
                        arrival(side, i, s).wait_recv()

                        @pl.when(s < hops(side, i))
                        def _():
                            onward(side, i, s).start()

                        across(side, i, s).start()

        return carry

    lax.fori_loop(0, per + 1 + nz // 2, turn, 0)

    for peer in range(3):
        send_part(per - 2, peer).wait_send()
        send_part(per - 1, peer).wait_send()

    def drain(i, carry):
        right, left, sib, local = first_hops(i)
        right.wait_send()
        left.wait_send()
        sib.wait_send()
        local.wait()
        for s in range(1, nz // 2 + 1):
            for side in range(2):
                @pl.when(s <= hops(side, i))
                def _():
                    @pl.when(s < hops(side, i))
                    def _():
                        onward(side, i, s).wait_send()

                    across(side, i, s).wait_send()
        for zs in range(nz):
            at = out.at[seq_of(zs, 1 - core, i)]
            remote(at, at, own_send.at[2, i], s_recv.at[zs, i], me.sib).wait_recv()
        return carry

    lax.fori_loop(0, per, drain, 0)


def rope_rows(seq_len, head_dim, copies):
    half_dim = head_dim // 2
    inv_freq = ROPE_BASE ** (-2.0 * jnp.arange(half_dim, dtype=F32) / head_dim)
    angles = jnp.arange(seq_len, dtype=F32)[:, None] * inv_freq[None, :]
    cos, sin = jnp.cos(angles), jnp.sin(angles)
    return jnp.tile(jnp.concatenate([cos, cos], 1), (copies, 1)), jnp.tile(jnp.concatenate([-sin, sin], 1), (copies, 1))


def solution(mesh):
    n_dp, n_tp = mesh.shape["dp"], mesh.shape["tp"]
    nz = n_tp // 2
    any_spec = pl.BlockSpec(memory_space=pl.ANY)
    vmem_spec = pl.BlockSpec(memory_space=pltpu.VMEM)
    dma = pltpu.SemaphoreType.DMA

    def shard_body(act_in, ln_gain, ln_bias, w_qkv, w_out, w_up, w_down):
        n_seq, seq_len, d_model = act_in.shape
        layers, _, _, qkv_cols = w_qkv.shape
        head_dim, ff = w_out.shape[1], w_up.shape[2]
        per = n_seq // n_tp
        half = per // 2
        heads = n_tp // 4
        tile = 4 * seq_len
        w_qkv = w_qkv.reshape(layers, d_model, qkv_cols)
        cos, sin = rope_rows(seq_len, head_dim, 4)
        seq_block = (seq_len, d_model)
        n_cols, n_rows = n_tp + 3 * heads, n_tp + heads
        steps = nz * half
        y1, nall, gcols, grows = pl.pallas_call(
            functools.partial(first_kernel, n_dp, n_tp),
            name="layer_one",
            out_shape=(jax.ShapeDtypeStruct((per, *seq_block), BF16), jax.ShapeDtypeStruct((per, 4, *seq_block), BF16),
                       jax.ShapeDtypeStruct((n_cols, d_model, LANES), BF16), jax.ShapeDtypeStruct((n_rows, LANES, d_model), BF16)),
            in_specs=[any_spec] + [vmem_spec] * 4 + [any_spec] * 4,
            out_specs=(vmem_spec, any_spec, any_spec, any_spec),
            scratch_shapes=[
                pltpu.VMEM((d_model, qkv_cols), BF16), pltpu.VMEM((head_dim, d_model), BF16), pltpu.VMEM((d_model, ff), BF16), pltpu.VMEM((ff, d_model), BF16),
                pltpu.VMEM((3, 4, *seq_block), BF16), pltpu.VMEM((tile, d_model), BF16), pltpu.VMEM((tile, head_dim), BF16), pltpu.VMEM((tile, ff), BF16),
                pltpu.VMEM((2, 2 * seq_len, d_model), F32), pltpu.VMEM((2, 2 * seq_len, d_model), BF16), pltpu.VMEM((4, 2 * seq_len, d_model), BF16),
                pltpu.VMEM((steps, *seq_block), BF16), pltpu.VMEM((steps, *seq_block), BF16), pltpu.VMEM((per, *seq_block), BF16),
                pltpu.VMEM((4, d_model, LANES), BF16), pltpu.VMEM((2, LANES, d_model), BF16),
                dma((4,)), dma((3,)), dma((2,)), dma((4,)), dma((steps,)), dma((steps,)), dma((steps,)), dma((steps,)),
                dma((6,)), dma((3, 6)), dma((6,)), dma((2, nz // 2, 6)), dma((2, nz // 2, 6)), dma((2, nz // 2, 6)), dma((nz, 6)),
                dma((3, per)), dma((3, per)), dma((per,)),
            ],
            compiler_params=pltpu.CompilerParams(collective_id=1, has_side_effects=True, vmem_limit_bytes=60 * 2**20),
        )(act_in, ln_gain, ln_bias, cos, sin, w_qkv, w_out, w_up, w_down)
        return pl.pallas_call(
            functools.partial(second_kernel, n_dp, n_tp),
            name="layer_two",
            out_shape=jax.ShapeDtypeStruct(act_in.shape, BF16),
            in_specs=[vmem_spec] + [any_spec] * 3 + [vmem_spec] * 2,
            out_specs=any_spec,
            scratch_shapes=[
                pltpu.VMEM((d_model, heads * qkv_cols), BF16), pltpu.VMEM((heads * head_dim, d_model), BF16), pltpu.VMEM((d_model, n_tp * LANES), BF16), pltpu.VMEM((n_tp * LANES, d_model), BF16),
                pltpu.VMEM((2, 4, *seq_block), BF16), pltpu.VMEM((tile, d_model), BF16), pltpu.VMEM((tile, heads * head_dim), BF16), pltpu.VMEM((tile, n_tp * LANES), BF16),
                pltpu.VMEM((2, *seq_block), F32), pltpu.VMEM((2, 4, *seq_block), BF16), pltpu.VMEM((per, 3, *seq_block), BF16), pltpu.VMEM((per, *seq_block), BF16),
                dma((n_cols + n_rows,)), dma((2,)), dma((2, 3)), dma((per, 3)), dma((3, per)), dma((per,)),
                dma((2, per, nz // 2)), dma((2, per, nz // 2)), dma((2, per, nz // 2)), dma((nz, per)),
            ],
            compiler_params=pltpu.CompilerParams(collective_id=2, has_side_effects=True, vmem_limit_bytes=60 * 2**20),
        )(y1, nall, gcols, grows, cos, sin)

    return jax.shard_map(shard_body, mesh=mesh, in_specs=(P("dp", None, None), P(None, None), P(None, None), P(None, None, "tp", None), P(None, "tp", None), P(None, None, "tp"), P(None, "tp", None)), out_specs=P("dp", None, None), check_vma=False)
```

time: 901 us -> 479 us (0.53)
  waiting for transfers between devices: 553 us -> 0 us
  Pallas kernels: 0 us -> 457 us
  matrix products: 205 us -> 0 us
  other arithmetic: 99 us -> 0.24 us
  between operations: 14 us -> 0.03 us
    psum x2 -> x0, waiting for transfers between devices: 553 us -> none  [shard_body(): reduced = lax.psum(local_sum, 'tp')]
    pallas_call x0 -> x2, Pallas kernels: none -> 457 us  [the longest x1 293 us: shard_body(): pl.pallas_call(functools.partial(first_kernel, n_dp, n_tp), name='layer_o...]
    dot_general x8 -> x0, matrix products: 205 us -> none  [the longest x2 123 us: layer_partial(): jnp.einsum('bsf,fe->bse', gelu_out, w_down, preferred_element_type=jnp.fl...]
    reduce_sum x6 -> x0, other arithmetic: 61.4 us -> none  [the longest x2 37.5 us: layer_norm(): row_mean = jnp.mean(hidden_f, axis=-1, keepdims=True)]
    convert_element_type x1 -> x0, other arithmetic: 29.2 us -> none  [shard_body(): (hidden.astype(jnp.float32) + reduced.astype(jnp.float32)).astype(jnp.bfl...]
    unnamed x28 -> x1, local copies, waits for them, and re-layouts: 11.8 us -> 21 us
  transfers between devices with their start and end apart: 2 -> 0, of which waited for: 2 -> 0; matrix products, arithmetic and copies ran while one was open for 0% -> 0% of each run, Pallas kernels for 0% -> 0%
where the time goes in v1:
time: 479 us
  Pallas kernels  457 us (95%)
  local copies, waits for them, and re-layouts  22.3 us (5%)
    pallas_call x1, Pallas kernels, shard_body(): pl.pallas_call(functools.partial(first_kernel, n_dp, n_tp), name='layer_o...  293 us
    pallas_call x1, Pallas kernels, shard_body(): pl.pallas_call(functools.partial(second_kernel, n_dp, n_tp), name='layer_...  163 us
    unnamed x1, local copies, waits for them, and re-layouts  21 us

profile of v1, /device:TPU:21, one launch (start us, length us, event | category | flops | bytes accessed | tf_op | source)
XLA Modules:
  0.0 479.1 jit_solution(12601689065284909634)
XLA Ops:
  0.0 0.1 fusion.2
  0.2 0.1 pad_maximum_fusion
  0.3 0.7 tile.8
  0.9 0.7 tile.20
  1.6 293.0 %layer_one.1 = (bf16[6,64,2048]{2,1,0:T(8,128)(2,1)}, bf16[6,4,64,2048]{3,2,1,0:T(8,128)(2,1)}, bf16[28,2048,128]{2,1,0:T(8,128)(2,1)}, bf16[20,128,2048]{2,1,0:T(8,128)(2,1)}) custom-call(bf16[96,64,2048]{2,1,0:T(8,128)(2,1)} %x.1, f32[2,2048]{1,0:T(2,128)} %gains.1, f32[2,2048]{1,0:T(2,128)} %biases.1, f32[256,128]{1,0:T(8,128)} %bitcast.4, ...), custom_call_target="tpu_custom_call" | custom-call | tf_op jit(solution)/shard_map/layer_one/pallas_call | solution.py:530
  294.6 163.5 %layer_two.1 = bf16[96,64,2048]{2,1,0:T(8,128)(2,1)} custom-call(bf16[6,64,2048]{2,1,0:T(8,128)(2,1)} %get-tuple-element.9.y1, bf16[6,4,64,2048]{3,2,1,0:T(8,128)(2,1)} %get-tuple-element.10.nall, bf16[28,2048,128]{2,1,0:T(8,128)(2,1)} %get-tuple-element.11.gcols, bf16[20,128,2048]{2,1,0:T(8,128)(2,1)} %get-tuple-element.12.grows, f32[256,128]{1,0:T(8,128)} %bitcast.5, ...), custom_call_target="tpu_custom_call" | custom-call | tf_op jit(solution)/shard_map/layer_two/pallas_call | solution.py:549
  458.1 21.0 %copy.9 = bf16[96,64,2048]{2,1,0:T(8,128)(2,1)} copy(bf16[96,64,2048]{2,1,0:T(8,128)(2,1)} %layer_two.1) | data formatting | bytes 50331648
  (1 shorter events, 0.0 us)

commit v2 on v1

v2 whole, which is shorter than its diff:
```python
import functools
import math

import jax
import jax.numpy as jnp
from jax import lax
from jax.experimental import pallas as pl
from jax.experimental.pallas import tpu as pltpu
from jax.sharding import PartitionSpec as P

LN_EPS = 1e-5
ROPE_BASE = 10000.0
MESH = pl.DeviceIdType.MESH
BF16 = jnp.bfloat16
F32 = jnp.float32
LANES = 128
UP, Q, K, V, DOWN, OUT = range(6)


def norm_rows(hidden_f, gain, bias):
    row_mean = jnp.mean(hidden_f, axis=-1, keepdims=True)
    centered = hidden_f - row_mean
    row_var = jnp.mean(centered * centered, axis=-1, keepdims=True)
    return (centered * lax.rsqrt(row_var + LN_EPS) * gain + bias).astype(BF16)


def rope(heads, cos, sin):
    return (heads * cos + pltpu.roll(heads, heads.shape[-1] // 2, 1) * sin).astype(BF16)


def gelu(values):
    return (0.5 * values * (1.0 + lax.erf(values * math.sqrt(0.5)))).astype(BF16)


def attend(query, keys, values, seq_len):
    rows, head_dim = query.shape
    scores = lax.dot_general(query, keys, (((1,), (1,)), ((), ())), preferred_element_type=F32) * (head_dim ** -0.5)
    row = lax.broadcasted_iota(jnp.int32, (rows, rows), 0)
    col = lax.broadcasted_iota(jnp.int32, (rows, rows), 1)
    allowed = (row >= col) & (row // seq_len == col // seq_len)
    scores = jnp.where(allowed, scores, -1e30)
    weights = jnp.exp(scores - jnp.max(scores, axis=-1, keepdims=True))
    probs = (weights / jnp.sum(weights, axis=-1, keepdims=True)).astype(BF16)
    return jnp.dot(probs, values, preferred_element_type=F32).astype(BF16)


def context_of(proj, cos_ref, sin_ref, seq_len):
    head_dim = cos_ref.shape[1]
    query = rope(proj[:, :head_dim], cos_ref[...], sin_ref[...])
    keys = rope(proj[:, head_dim : 2 * head_dim], cos_ref[...], sin_ref[...])
    return attend(query, keys, proj[:, 2 * head_dim :].astype(BF16), seq_len)


def head_context(normed, qkv_w, cos_ref, sin_ref, seq_len):
    return context_of(jnp.dot(normed, qkv_w, preferred_element_type=F32), cos_ref, sin_ref, seq_len)


class Place:
    def __init__(self, n_dp, n_tp):
        side = math.isqrt(n_dp)
        assert side * side == n_dp and side % 2 == 0 and n_tp % 4 == 0
        self.n_tp, self.nz = n_tp, n_tp // 2
        self.dp, self.tp = lax.axis_index("dp"), lax.axis_index("tp")
        self.z, self.core = self.tp // 2, self.tp % 2
        x, y = self.dp // side, self.dp % side
        xf, yf = x + 1 - 2 * (x % 2), y + 1 - 2 * (y % 2)
        self.q = (x % 2) * 2 + y % 2
        self.peers = [{"dp": xf * side + y}, {"dp": x * side + yf}, {"dp": xf * side + yf}]
        self.peer_q = [(1 - x % 2) * 2 + y % 2, (x % 2) * 2 + 1 - y % 2, (1 - x % 2) * 2 + 1 - y % 2]
        self.sib = {"tp": 2 * self.z + 1 - self.core}
        self.right = {"tp": 2 * ((self.z + 1) % self.nz) + self.core}
        self.left = {"tp": 2 * ((self.z + self.nz - 1) % self.nz) + self.core}

    def others(self):
        return [self.sib, self.right, self.left, *self.peers]

    def greet(self):
        barrier = pltpu.get_barrier_semaphore()
        for other in self.others():
            pl.semaphore_signal(barrier, inc=1, device_id=other, device_id_type=MESH)

    def meet(self):
        pl.semaphore_wait(pltpu.get_barrier_semaphore(), len(self.others()))


def remote(src, dst, send_sem, recv_sem, device):
    return pltpu.make_async_remote_copy(src_ref=src, dst_ref=dst, send_sem=send_sem, recv_sem=recv_sem, device_id=device, device_id_type=MESH)


def piece(kind, source, n_tp, cols, rows):
    if kind == UP:
        return cols.at[source]
    if kind == DOWN:
        return rows.at[source]
    head = source // 8 * 2 + source % 2
    if kind == OUT:
        return rows.at[n_tp + head]
    return cols.at[n_tp + 3 * head + kind - Q]


def first_kernel(n_dp, n_tp, x, gains, biases, cos_ref, sin_ref, qkv, out_w, up, down,
                 y1, nout, accout, gcols, grows,
                 qkv_v, out_v, up_v, down_v, xbuf, normed, ctx, act, own, sib_out, sib_in, ring_r, ring_l, nall, acc, st_cols, st_rows,
                 w_sem, x_sem, sib_send, sib_recv, r_send, r_recv, l_send, l_recv,
                 st_sem, own_sem, loc_sem, wr_recv, wr_send, ws_send, ws_recv, n_send, n_recv, slab_sem, nout_sem, acc_sem):
    me = Place(n_dp, n_tp)
    me.greet()
    nz, core, z, q = me.nz, me.core, me.z, me.q
    n_seq, seq_len, d_model = x.shape
    head_dim, ff = out_w.shape[1], up.shape[2]
    per = n_seq // n_tp
    half = per // 2
    steps = nz * half
    tile = 4 * seq_len

    first_w = [pltpu.make_async_copy(src.at[0], dst, w_sem.at[i]) for i, (src, dst) in
               enumerate(((qkv, qkv_v.at[:, pl.ds(0, qkv.shape[2])]), (up, up_v), (out_w, out_v.at[pl.ds(0, head_dim)]), (down, down_v)))]

    def owner_seq(zo, co, j):
        return per * (2 * zo + co) + j

    def tile_seqs(i):
        s, j = i // half, i % half
        zr, zl = (z + 2 * nz - 1 - s) % nz, (z + 1 + s) % nz
        return [owner_seq(zr, core, j), owner_seq(zl, core, half + j), owner_seq(zr, 1 - core, j), owner_seq(zl, 1 - core, half + j)]

    def fetch(i):
        for place, seq in enumerate(tile_seqs(i)):
            pltpu.make_async_copy(x.at[seq], xbuf.at[i % 3, place], x_sem.at[i % 3]).start()

    fetch(0)
    for copy in first_w[:2]:
        copy.start()
    loads = {UP: (up.at[1, :, pl.ds(pl.multiple_of(q * LANES, LANES), LANES)], st_cols.at[UP]),
             DOWN: (down.at[1, pl.ds(pl.multiple_of(q * LANES, LANES), LANES), :], st_rows.at[0]),
             OUT: (out_w.at[1], st_rows.at[1])}
    for kind in (Q, K, V):
        loads[kind] = (qkv.at[1, :, pl.ds((kind - Q) * head_dim, head_dim)], st_cols.at[kind])
    kinds = (Q, K, V, OUT, UP, DOWN)
    loads = {kind: pltpu.make_async_copy(*loads[kind], st_sem.at[kind]) for kind in kinds}
    loads[UP].start()
    for copy in first_w[2:]:
        copy.start()
    for kind in kinds:
        if kind != UP:
            loads[kind].start()

    def has(kind, source):
        return source >= 0 if kind in (UP, DOWN) else (source // 2 + 2 * (source % 2)) % 4 == q

    def staged(kind):
        return st_rows.at[kind - DOWN] if kind >= DOWN else st_cols.at[kind]

    def first_hops(kind):
        src, dst = staged(kind), piece(kind, me.tp, n_tp, gcols, grows)
        return [remote(src, dst, own_sem.at[0, kind], wr_recv.at[0, 0, kind], me.right),
                remote(src, dst, own_sem.at[1, kind], wr_recv.at[1, 0, kind], me.left),
                remote(src, dst, own_sem.at[2, kind], ws_recv.at[z, kind], me.sib),
                pltpu.make_async_copy(src, dst, loc_sem.at[kind])]

    def send_first(kind):
        loads[kind].wait()

        @pl.when(has(kind, me.tp))
        def _():
            for copy in first_hops(kind):
                copy.start()

    for i in range(half):
        ring_r[i] = jnp.zeros(ring_r.shape[1:], BF16)
        ring_l[i] = jnp.zeros(ring_l.shape[1:], BF16)

    def send_sib(i):
        return remote(sib_out.at[i % 2], sib_in.at[i % 4], sib_send.at[i % 2], sib_recv.at[i % 4], me.sib)

    def send_r(i):
        return remote(ring_r.at[i], ring_r.at[i + half], r_send.at[i], r_recv.at[i + half], me.right)

    def send_l(i):
        return remote(ring_l.at[i], ring_l.at[i + half], l_send.at[i], l_recv.at[i + half], me.left)

    def rows_of(member):
        return pl.ds(pl.multiple_of(member * seq_len, seq_len), seq_len)

    def send_n(seq, peer):
        at = nall.at[seq, rows_of(q)]
        return remote(at, at, n_send.at[peer, seq], n_recv.at[peer, seq], me.peers[peer])

    def wait_n(seq, peer):
        at = nall.at[seq, rows_of(me.peer_q[peer])]
        return remote(at, at, n_send.at[peer, seq], n_recv.at[peer, seq], me.peers[peer])

    def compute(i, waits=()):
        slot = i % 3
        pltpu.make_async_copy(x.at[pl.ds(0, 4)], xbuf.at[slot], x_sem.at[slot]).wait()

        @pl.when(i + 1 < steps)
        def _():
            fetch(i + 1)

        @pl.when(i >= 2)
        def _():
            send_sib(i - 2).wait_send()

        for member in range(4):
            normed[pl.ds(member * seq_len, seq_len), :] = norm_rows(xbuf[slot, member].astype(F32), gains[pl.ds(0, 1), :], biases[pl.ds(0, 1), :])
        for copy in waits[:2]:
            copy.wait()
        ctx[...] = head_context(normed[...], qkv_v[:, : 3 * head_dim], cos_ref, sin_ref, seq_len)
        act[...] = gelu(jnp.dot(normed[...], up_v[...], preferred_element_type=F32))
        for copy in waits[2:]:
            copy.wait()
        step = 512
        for first in range(0, d_model, step):
            cols = pl.ds(first, step)
            part = jnp.dot(ctx[...], out_v[:head_dim, cols], preferred_element_type=F32) + jnp.dot(act[...], down_v[:, cols], preferred_element_type=F32)
            own[i % 2, :, cols] = part[: 2 * seq_len]
            sib_out[i % 2, :, cols] = part[2 * seq_len :].astype(BF16)

    def finish(i):
        send_sib(i).wait_recv()

        @pl.when(i >= half)
        def _():
            send_r(i - half).wait_recv()
            send_l(i - half).wait_recv()

        last = i >= steps - half

        @pl.when(jnp.logical_not(last))
        def _():
            for side, ring in enumerate((ring_r, ring_l)):
                at = pl.ds(side * seq_len, seq_len)
                ring[i] = (own[i % 2, at, :] + sib_in[i % 4, at, :].astype(F32) + ring[i].astype(F32)).astype(BF16)
            send_r(i).start()
            send_l(i).start()

        @pl.when(i == steps - half - 1)
        def _():
            for kind in kinds:
                if kind != UP:
                    send_first(kind)

        @pl.when(last)
        def _():
            rows = 16
            for side, ring in enumerate((ring_r, ring_l)):
                seq = side * half + i % half

                def close(k, carry):
                    at = pl.ds(pl.multiple_of(k * rows, rows), rows)
                    both = pl.ds(pl.multiple_of(side * seq_len + k * rows, rows), rows)
                    update = (own[i % 2, both, :] + sib_in[i % 4, both, :].astype(F32) + ring[i, at, :].astype(F32)).astype(BF16)
                    hidden = (xbuf[i % 3, side, at, :].astype(F32) + update.astype(F32)).astype(BF16)
                    y1[seq, at, :] = hidden
                    mine = pl.ds(pl.multiple_of(q * seq_len + k * rows, rows), rows)
                    nall[seq, mine, :] = norm_rows(hidden.astype(F32), gains[pl.ds(1, 1), :], biases[pl.ds(1, 1), :])
                    return carry

                lax.fori_loop(0, seq_len // rows, close, 0)
                for peer in range(3):
                    send_n(seq, peer).start()

    compute(0, first_w)
    me.meet()
    send_first(UP)
    send_sib(0).start()

    def turn(i, carry):
        @pl.when(i < steps)
        def _():
            compute(i)
            send_sib(i).start()

        finish(i - 1)
        return carry

    lax.fori_loop(1, steps + 1, turn, 0)

    to = (me.right, me.left)

    def hops(side, kind):
        longer = (core + kind) % 2
        return nz // 2 - longer if side == 0 else nz // 2 - 1 + longer

    def z_at(side, s):
        return (z + nz - s) % nz if side == 0 else (z + s) % nz

    def source_of(side, s):
        return 2 * z_at(side, s) + core

    def onward(side, s, kind):
        at = piece(kind, source_of(side, s), n_tp, gcols, grows)
        return remote(at, at, wr_send.at[side, s - 1, kind], wr_recv.at[side, s, kind], to[side])

    def arrival(side, s, kind):
        at = piece(kind, source_of(side, s), n_tp, gcols, grows)
        return remote(at, at, wr_send.at[side, s - 1, kind], wr_recv.at[side, s - 1, kind], to[side])

    def across(side, s, kind):
        source = source_of(side, s)
        at = piece(kind, source, n_tp, gcols, grows)
        return remote(at, at, ws_send.at[side, s - 1, kind], ws_recv.at[source // 2, kind], me.sib)

    def take(side, s, kind):
        @pl.when(has(kind, source_of(side, s)) & (s <= hops(side, kind)))
        def _():
            arrival(side, s, kind).wait_recv()

            @pl.when(s < hops(side, kind))
            def _():
                onward(side, s, kind).start()

            across(side, s, kind).start()

    def from_sib(zs, kind):
        source = 2 * zs + 1 - core

        @pl.when(has(kind, source))
        def _():
            at = piece(kind, source, n_tp, gcols, grows)
            remote(at, at, own_sem.at[2, kind], ws_recv.at[zs, kind], me.sib).wait_recv()

    width = 2 * LANES

    def slab_loads(number, zs):
        slot = number % 2
        copies = []
        for c in range(2):
            copies.append((gcols.at[2 * zs + c], up_v.at[:, pl.ds(slot * width + c * LANES, LANES)], slab_sem.at[slot, c]))
            copies.append((grows.at[2 * zs + c], down_v.at[pl.ds(slot * width + c * LANES, LANES), :], slab_sem.at[slot, 2 + c]))
        return [pltpu.make_async_copy(*copy) for copy in copies]

    def head_loads(first):
        copies = []
        for n in range(2):
            for i in range(3):
                copies.append((gcols.at[n_tp + 3 * (first + n) + i], qkv_v.at[:, pl.ds((3 * n + i) * head_dim, head_dim)], slab_sem.at[2, 4 * n + i]))
            copies.append((grows.at[n_tp + first + n], out_v.at[pl.ds(n * head_dim, head_dim)], slab_sem.at[2, 4 * n + 3]))
        return [pltpu.make_async_copy(*copy) for copy in copies]

    def pair(p):
        return p, half + p

    def slab_pair(number, p):
        mine = pl.ds(number % 2 * width, width)
        hidden = [gelu(jnp.dot(nall[i], up_v[:, mine], preferred_element_type=F32)) for i in pair(p)]
        step = 512
        for first in range(0, d_model, step):
            cols = pl.ds(first, step)
            for i, rows in zip(pair(p), hidden):
                part = jnp.dot(rows, down_v[mine, cols], preferred_element_type=F32)
                acc[i, :, cols] = part if number == 0 else acc[i, :, cols] + part

    def head_pair(p):
        contexts = []
        for i in pair(p):
            proj = jnp.dot(nall[i], qkv_v[...], preferred_element_type=F32)
            contexts.append(jnp.concatenate([context_of(proj[:, 3 * head_dim * n : 3 * head_dim * (n + 1)], cos_ref, sin_ref, seq_len) for n in range(2)], axis=1))
        step = 512
        for first in range(0, d_model, step):
            cols = pl.ds(first, step)
            for i, rows in zip(pair(p), contexts):
                acc[i, :, cols] += jnp.dot(rows, out_v[:, cols], preferred_element_type=F32)

    def pairs(body):
        def one(p, carry):
            body(p)
            return carry

        lax.fori_loop(0, half, one, 0)

    order = [(0, 0), (0, 1), (1, 1)]

    def start_slab(number):
        zs = z_at(*order[number])
        for kind in (UP, DOWN):
            from_sib(zs, kind)
            if number == 0:
                first_hops(kind)[3].wait()
        for copy in slab_loads(number, zs):
            copy.start()

    def wait_slab(number):
        for copy in slab_loads(number, z_at(*order[number])):
            copy.wait()

    def take_all(stages, kinds):
        for s in stages:
            for kind in kinds:
                for side in range(2):
                    take(side, s, kind)

    def await_pair(p):
        for i in pair(p):
            for peer in range(3):
                wait_n(i, peer).wait_recv()
            pltpu.make_async_copy(nall.at[i], nout.at[i], nout_sem.at[i]).start()

    def slab(number):
        wait_slab(number)
        pairs(functools.partial(slab_pair, number))

    attn = (Q, K, V, OUT)
    take_all([1, 2], attn)
    start_slab(0)
    take_all([1], [UP, DOWN])
    wait_slab(0)
    await_pair(0)
    slab_pair(0, 0)
    take_all([3], attn)
    await_pair(1)
    slab_pair(0, 1)
    take_all([2], [UP])
    await_pair(2)
    slab_pair(0, 2)
    start_slab(1)
    take_all([2], [DOWN])
    take_all([4], attn)
    for kind in attn:
        @pl.when(has(kind, me.tp))
        def _():
            first_hops(kind)[3].wait()

        for zs in range(nz):
            from_sib(zs, kind)
    for copy in head_loads(0):
        copy.start()
    start_slab(2)
    for copy in head_loads(0):
        copy.wait()
    head_pair(0)
    take_all([3], [UP])
    head_pair(1)
    take_all([3], [DOWN])
    head_pair(2)
    slab(1)
    wait_slab(2)

    def last_part(p):
        slab_pair(2, p)
        for i in pair(p):
            pltpu.make_async_copy(acc.at[i], accout.at[i], acc_sem.at[i]).start()

    pairs(last_part)
    take_all([4], [UP, DOWN])

    def drain(i, carry):
        send_r(i).wait_send()
        send_l(i).wait_send()
        return carry

    lax.fori_loop(0, steps - half, drain, 0)
    send_sib(steps - 2).wait_send()
    send_sib(steps - 1).wait_send()
    for seq in range(per):
        for peer in range(3):
            send_n(seq, peer).wait_send()
        pltpu.make_async_copy(nall.at[seq], nout.at[seq], nout_sem.at[seq]).wait()
        pltpu.make_async_copy(acc.at[seq], accout.at[seq], acc_sem.at[seq]).wait()
    for kind in kinds:
        @pl.when(has(kind, me.tp))
        def _():
            for copy in first_hops(kind)[:3]:
                copy.wait_send()

        for s in range(1, nz // 2 + 1):
            for side in range(2):
                @pl.when(has(kind, source_of(side, s)) & (s <= hops(side, kind)))
                def _():
                    @pl.when(s < hops(side, kind))
                    def _():
                        onward(side, s, kind).wait_send()

                    across(side, s, kind).wait_send()
    for side, s in late_slabs(nz):
        for kind in (UP, DOWN):
            from_sib(z_at(side, s), kind)


def late_slabs(nz):
    return [(side, s) for s in range(2, nz // 2) for side in range(2)] + [(0, nz // 2)]


def second_kernel(n_dp, n_tp, y1, cos_ref, sin_ref, nout, accout, gcols, grows, out,
                  qkv_v, out_v, up_v, down_v, nbuf, ctx, act, accbuf, own, part_out, part_in,
                  w_sem, n_sem, a_sem, p_send, p_recv, own_send, r_recv, f_send, s_send, s_recv):
    me = Place(n_dp, n_tp)
    me.greet()
    nz, core, z, q = me.nz, me.core, me.z, me.q
    per, tile, d_model = nout.shape
    members = 4
    seq_len = tile // members

    def z_of(side, s):
        return (z + nz - s) % nz if side == 0 else (z + s) % nz

    def fetch(i):
        return [pltpu.make_async_copy(nout.at[i], nbuf.at[i % 2], n_sem.at[i % 2]),
                pltpu.make_async_copy(accout.at[i], accbuf.at[i % 2], a_sem.at[i % 2])]

    for copy in fetch(0):
        copy.start()
    head_dim = cos_ref.shape[1]
    firsts, seconds = [], []
    for n in range(2):
        head = grows.shape[0] - n_tp - 2 + n
        for i in range(3):
            firsts.append((gcols.at[n_tp + 3 * head + i], qkv_v.at[:, pl.ds((3 * n + i) * head_dim, head_dim)]))
        seconds.append((grows.at[n_tp + head], out_v.at[pl.ds(n * head_dim, head_dim)]))
    for n, (side, s) in enumerate(late_slabs(nz)):
        for c in range(2):
            source, at = 2 * z_of(side, s) + c, pl.ds((2 * n + c) * LANES, LANES)
            firsts.append((gcols.at[source], up_v.at[:, at]))
            seconds.append((grows.at[source], down_v.at[at, :]))
    loads = [pltpu.make_async_copy(src, dst, w_sem.at[i]) for i, (src, dst) in enumerate(firsts + seconds)]
    firsts, seconds = loads[: len(firsts)], loads[len(firsts) :]
    for copy in loads:
        copy.start()

    def send_part(i, peer):
        at = pl.ds(pl.multiple_of(me.peer_q[peer] * seq_len, seq_len), seq_len)
        return remote(part_out.at[i % 4, at], part_in.at[i, peer], p_send.at[i % 4, peer], p_recv.at[i, peer], me.peers[peer])

    def seq_of(zs, co, i):
        return per * (2 * zs + co) + i

    def first_hops(i):
        at = out.at[seq_of(z, core, i)]
        return [remote(at, at, own_send.at[0, i], r_recv.at[0, i, 0], me.right),
                remote(at, at, own_send.at[1, i], r_recv.at[1, i, 0], me.left),
                remote(at, at, own_send.at[2, i], s_recv.at[z, i], me.sib)]

    to = (me.right, me.left)

    def hops(side, i):
        longer = (i + core) % 2
        return nz // 2 - longer if side == 0 else nz // 2 - 1 + longer

    def arrival(side, i, s):
        at = out.at[seq_of(z_of(side, s), core, i)]
        return remote(at, at, f_send.at[side, i, s - 1], r_recv.at[side, i, s - 1], to[side])

    def onward(side, i, s):
        at = out.at[seq_of(z_of(side, s), core, i)]
        return remote(at, at, f_send.at[side, i, s - 1], r_recv.at[side, i, s], to[side])

    def across(side, i, s):
        at = out.at[seq_of(z_of(side, s), core, i)]
        return remote(at, at, s_send.at[side, i, s - 1], s_recv.at[z_of(side, s), i], me.sib)

    def when_first(i, copies):
        @pl.when(i == 0)
        def _():
            for copy in copies:
                copy.wait()

    def compute(i):
        for copy in fetch(i):
            copy.wait()

        @pl.when(i + 1 < per)
        def _():
            for copy in fetch(i + 1):
                copy.start()

        @pl.when(i >= 4)
        def _():
            for peer in range(3):
                send_part(i - 4, peer).wait_send()

        when_first(i, firsts)
        proj = jnp.dot(nbuf[i % 2], qkv_v[...], preferred_element_type=F32)
        ctx[...] = jnp.concatenate([context_of(proj[:, 3 * head_dim * n : 3 * head_dim * (n + 1)], cos_ref, sin_ref, seq_len) for n in range(2)], axis=1)
        act[...] = gelu(jnp.dot(nbuf[i % 2], up_v[...], preferred_element_type=F32))
        when_first(i, seconds)
        step = 512
        for first in range(0, d_model, step):
            cols = pl.ds(first, step)
            part = accbuf[i % 2, :, cols] + jnp.dot(act[...], down_v[:, cols], preferred_element_type=F32)
            part += jnp.dot(ctx[...], out_v[:, cols], preferred_element_type=F32)
            accbuf[i % 2, :, cols] = part
            part_out[i % 4, :, cols] = part.astype(BF16)

        @pl.when(i == 0)
        def _():
            me.meet()

        for peer in range(3):
            send_part(i, peer).start()
        own[i % 4] = accbuf[i % 2, pl.ds(pl.multiple_of(q * seq_len, seq_len), seq_len), :]

    def finish(i):
        for peer in range(3):
            send_part(i, peer).wait_recv()
        total = own[i % 4]
        for peer in range(3):
            total = total + part_in[i, peer].astype(F32)
        out[seq_of(z, core, i)] = (y1[i].astype(F32) + total.astype(BF16).astype(F32)).astype(BF16)
        for copy in first_hops(i):
            copy.start()

    def pass_on(i, s):
        for side in range(2):
            @pl.when(s <= hops(side, i))
            def _():
                arrival(side, i, s).wait_recv()

                @pl.when(s < hops(side, i))
                def _():
                    onward(side, i, s).start()

                across(side, i, s).start()

    def stage(name):
        i, s = int(name[0]), int(name[1])
        if s == 0:
            finish(i)
        else:
            pass_on(i, s)

    assert (per, nz) == (6, 8)
    beside = {2: "00", 3: "01", 4: "10 02", 5: "11 20"}

    def turn(i, carry):
        compute(i)
        for at, names in beside.items():
            @pl.when(i == at)
            def _():
                for name in names.split():
                    stage(name)

        return carry

    lax.fori_loop(0, per, turn, 0)
    for name in "03 12 30 21 04 13 40 31 22 50 14 41 32 23 51 42 33 52 24 43 34 53 44 54".split():
        stage(name)

    for i in range(per - 4, per):
        for peer in range(3):
            send_part(i, peer).wait_send()

    def drain(i, carry):
        for copy in first_hops(i):
            copy.wait_send()
        for s in range(1, nz // 2 + 1):
            for side in range(2):
                @pl.when(s <= hops(side, i))
                def _():
                    @pl.when(s < hops(side, i))
                    def _():
                        onward(side, i, s).wait_send()

                    across(side, i, s).wait_send()
        for zs in range(nz):
            at = out.at[seq_of(zs, 1 - core, i)]
            remote(at, at, own_send.at[2, i], s_recv.at[zs, i], me.sib).wait_recv()
        return carry

    lax.fori_loop(0, per, drain, 0)


def rope_rows(seq_len, head_dim, copies):
    half_dim = head_dim // 2
    inv_freq = ROPE_BASE ** (-2.0 * jnp.arange(half_dim, dtype=F32) / head_dim)
    angles = jnp.arange(seq_len, dtype=F32)[:, None] * inv_freq[None, :]
    cos, sin = jnp.cos(angles), jnp.sin(angles)
    return jnp.tile(jnp.concatenate([cos, cos], 1), (copies, 1)), jnp.tile(jnp.concatenate([-sin, sin], 1), (copies, 1))


def solution(mesh):
    n_dp, n_tp = mesh.shape["dp"], mesh.shape["tp"]
    nz = n_tp // 2
    any_spec = pl.BlockSpec(memory_space=pl.ANY)
    vmem_spec = pl.BlockSpec(memory_space=pltpu.VMEM)
    dma = pltpu.SemaphoreType.DMA

    def shard_body(act_in, ln_gain, ln_bias, w_qkv, w_out, w_up, w_down):
        n_seq, seq_len, d_model = act_in.shape
        layers, _, _, qkv_cols = w_qkv.shape
        head_dim, ff = w_out.shape[1], w_up.shape[2]
        per = n_seq // n_tp
        half = per // 2
        heads = n_tp // 4
        tile = 4 * seq_len
        w_qkv = w_qkv.reshape(layers, d_model, qkv_cols)
        cos, sin = rope_rows(seq_len, head_dim, 4)
        seq_block = (seq_len, d_model)
        n_cols, n_rows = n_tp + 3 * heads, n_tp + heads
        steps = nz * half
        n_late = 2 * len(late_slabs(nz)) * LANES
        y1, nout, accout, gcols, grows = pl.pallas_call(
            functools.partial(first_kernel, n_dp, n_tp),
            name="layer_one",
            out_shape=(jax.ShapeDtypeStruct((per, *seq_block), BF16), jax.ShapeDtypeStruct((per, tile, d_model), BF16), jax.ShapeDtypeStruct((per, tile, d_model), F32),
                       jax.ShapeDtypeStruct((n_cols, d_model, LANES), BF16), jax.ShapeDtypeStruct((n_rows, LANES, d_model), BF16)),
            in_specs=[any_spec] + [vmem_spec] * 4 + [any_spec] * 4,
            out_specs=(vmem_spec, any_spec, any_spec, any_spec, any_spec),
            scratch_shapes=[
                pltpu.VMEM((d_model, 2 * qkv_cols), BF16), pltpu.VMEM((2 * head_dim, d_model), BF16), pltpu.VMEM((d_model, ff), BF16), pltpu.VMEM((ff, d_model), BF16),
                pltpu.VMEM((3, 4, *seq_block), BF16), pltpu.VMEM((tile, d_model), BF16), pltpu.VMEM((tile, head_dim), BF16), pltpu.VMEM((tile, ff), BF16),
                pltpu.VMEM((2, 2 * seq_len, d_model), F32), pltpu.VMEM((2, 2 * seq_len, d_model), BF16), pltpu.VMEM((4, 2 * seq_len, d_model), BF16),
                pltpu.VMEM((steps, *seq_block), BF16), pltpu.VMEM((steps, *seq_block), BF16), pltpu.VMEM((per, tile, d_model), BF16), pltpu.VMEM((per, tile, d_model), F32),
                pltpu.VMEM((4, d_model, LANES), BF16), pltpu.VMEM((2, LANES, d_model), BF16),
                dma((4,)), dma((3,)), dma((2,)), dma((4,)), dma((steps,)), dma((steps,)), dma((steps,)), dma((steps,)),
                dma((6,)), dma((3, 6)), dma((6,)), dma((2, nz // 2, 6)), dma((2, nz // 2, 6)), dma((2, nz // 2, 6)), dma((nz, 6)),
                dma((3, per)), dma((3, per)), dma((3, 8)), dma((per,)), dma((per,)),
            ],
            compiler_params=pltpu.CompilerParams(collective_id=1, has_side_effects=True, vmem_limit_bytes=63 * 2**20),
        )(act_in, ln_gain, ln_bias, cos, sin, w_qkv, w_out, w_up, w_down)
        return pl.pallas_call(
            functools.partial(second_kernel, n_dp, n_tp),
            name="layer_two",
            out_shape=pltpu.VMEM(act_in.shape, BF16),
            in_specs=[vmem_spec] * 3 + [any_spec] * 4,
            out_specs=vmem_spec,
            scratch_shapes=[
                pltpu.VMEM((d_model, 2 * qkv_cols), BF16), pltpu.VMEM((2 * head_dim, d_model), BF16), pltpu.VMEM((d_model, n_late), BF16), pltpu.VMEM((n_late, d_model), BF16),
                pltpu.VMEM((2, tile, d_model), BF16), pltpu.VMEM((tile, 2 * head_dim), BF16), pltpu.VMEM((tile, n_late), BF16), pltpu.VMEM((2, tile, d_model), F32), pltpu.VMEM((4, *seq_block), F32),
                pltpu.VMEM((4, tile, d_model), BF16), pltpu.VMEM((per, 3, *seq_block), BF16),
                dma((2 * n_late // LANES + 8,)), dma((2,)), dma((2,)), dma((4, 3)), dma((per, 3)), dma((3, per)),
                dma((2, per, nz // 2)), dma((2, per, nz // 2)), dma((2, per, nz // 2)), dma((nz, per)),
            ],
            compiler_params=pltpu.CompilerParams(collective_id=2, has_side_effects=True, vmem_limit_bytes=38 * 2**20),
        )(y1, cos, sin, nout, accout, gcols, grows)

    return jax.shard_map(shard_body, mesh=mesh, in_specs=(P("dp", None, None), P(None, None), P(None, None), P(None, None, "tp", None), P(None, "tp", None), P(None, None, "tp"), P(None, "tp", None)), out_specs=P("dp", None, None), check_vma=False)
```

time: 479 us -> 440 us (0.919)
  Pallas kernels: 457 us -> 429 us
  local copies, waits for them, and re-layouts: 22.3 us -> 10.3 us
    pallas_call x1, Pallas kernels: 293 us -> 268 us  [shard_body(): pl.pallas_call(functools.partial(first_kernel, n_dp, n_tp), name='layer_o...]
    unnamed x1, local copies, waits for them, and re-layouts: 21 us -> 8.92 us
where the time goes in v2:
time: 440 us
  Pallas kernels  429 us (98%)
  local copies, waits for them, and re-layouts  10.3 us (2%)
    pallas_call x1, Pallas kernels, shard_body(): pl.pallas_call(functools.partial(first_kernel, n_dp, n_tp), name='layer_o...  268 us
    pallas_call x1, Pallas kernels, shard_body(): pl.pallas_call(functools.partial(second_kernel, n_dp, n_tp), name='layer_...  161 us
    unnamed x1, local copies, waits for them, and re-layouts  8.92 us

profile of v2, /device:TPU:21, one launch (start us, length us, event | category | flops | bytes accessed | tf_op | source)
XLA Modules:
  0.0 439.6 jit_solution(17367542690822443387)
XLA Ops:
  0.0 0.1 fusion.2
  0.2 0.1 pad_maximum_fusion
  0.3 0.7 tile.8
  0.9 0.7 tile.20
  1.6 268.1 %layer_one.1 = (bf16[6,64,2048]{2,1,0:T(8,128)(2,1)}, bf16[6,256,2048]{2,1,0:T(8,128)(2,1)}, f32[6,256,2048]{2,1,0:T(8,128)}, bf16[28,2048,128]{2,1,0:T(8,128)(2,1)}, bf16[20,128,2048]{2,1,0:T(8,128)(2,1)}) custom-call(bf16[96,64,2048]{2,1,0:T(8,128)(2,1)} %x.1, f32[2,2048]{1,0:T(2,128)} %gains.1, f32[2,2048]{1,0:T(2,128)} %biases.1, f32[256,128]{1,0:T(8,128)} %bitcast.4, ...), custom_call_target="tpu_custom_call" | custom-call | tf_op jit(solution)/shard_map/layer_one/pallas_call | solution.py:692
  269.7 160.9 %layer_two.1 = bf16[96,64,2048]{2,1,0:T(8,128)(2,1)S(1)} custom-call(bf16[6,64,2048]{2,1,0:T(8,128)(2,1)} %get-tuple-element.10.y1, f32[256,128]{1,0:T(8,128)} %bitcast.5, f32[256,128]{1,0:T(8,128)} %bitcast.7, bf16[6,256,2048]{2,1,0:T(8,128)(2,1)} %get-tuple-element.11.nout, f32[6,256,2048]{2,1,0:T(8,128)} %get-tuple-element.12.accout, ...), custom_call_target="tpu_custom_call" | custom-call | tf_op jit(solution)/shard_map/layer_two/pallas_call | solution.py:711
  430.7 8.9 %copy.9 = bf16[96,64,2048]{2,1,0:T(8,128)(2,1)} copy(bf16[96,64,2048]{2,1,0:T(8,128)(2,1)S(1)} %layer_two.1) | data formatting | bytes 50331648
  (1 shorter events, 0.0 us)

commit v3 on v0

v3 whole, which is shorter than its diff:
```python
import functools
import math

import jax
import jax.numpy as jnp
import numpy as np
from jax import lax
from jax.experimental import pallas as pl
from jax.experimental.pallas import tpu as pltpu
from jax.sharding import PartitionSpec as P

LN_EPS = 1e-5
ROPE_BASE = 10000.0
MESH = pl.DeviceIdType.MESH
BF16 = jnp.bfloat16
F32 = jnp.float32
LANES = 128
UP, Q, K, V, DOWN, OUT = range(6)


def norm_rows(hidden_f, gain, bias):
    row_mean = jnp.mean(hidden_f, axis=-1, keepdims=True)
    centered = hidden_f - row_mean
    row_var = jnp.mean(centered * centered, axis=-1, keepdims=True)
    return (centered * lax.rsqrt(row_var + LN_EPS) * gain + bias).astype(BF16)


def rope(heads, cos, sin):
    return (heads * cos + pltpu.roll(heads, heads.shape[-1] // 2, 1) * sin).astype(BF16)


def gelu(values):
    return (0.5 * values * (1.0 + lax.erf(values * math.sqrt(0.5)))).astype(BF16)


def attend(query, keys, values, seq_len):
    rows, head_dim = query.shape
    block = 2 * seq_len
    row = lax.broadcasted_iota(jnp.int32, (block, block), 0)
    col = lax.broadcasted_iota(jnp.int32, (block, block), 1)
    allowed = (row >= col) & (row // seq_len == col // seq_len)
    contexts = []
    for first in range(0, rows, block):
        at = slice(first, first + block)
        scores = lax.dot_general(query[at], keys[at], (((1,), (1,)), ((), ())), preferred_element_type=F32) * (head_dim ** -0.5)
        scores = jnp.where(allowed, scores, -1e30)
        weights = jnp.exp(scores - jnp.max(scores, axis=-1, keepdims=True))
        probs = (weights / jnp.sum(weights, axis=-1, keepdims=True)).astype(BF16)
        contexts.append(jnp.dot(probs, values[at], preferred_element_type=F32).astype(BF16))
    return jnp.concatenate(contexts, axis=0)


def context_of(proj, cos_ref, sin_ref, seq_len):
    head_dim = cos_ref.shape[1]
    query = rope(proj[:, :head_dim], cos_ref[...], sin_ref[...])
    keys = rope(proj[:, head_dim : 2 * head_dim], cos_ref[...], sin_ref[...])
    return attend(query, keys, proj[:, 2 * head_dim :].astype(BF16), seq_len)


def head_context(normed, qkv_w, cos_ref, sin_ref, seq_len):
    return context_of(jnp.dot(normed, qkv_w, preferred_element_type=F32), cos_ref, sin_ref, seq_len)


class Place:
    def __init__(self, n_dp, n_tp):
        side = math.isqrt(n_dp)
        assert side * side == n_dp and side % 2 == 0 and n_tp % 4 == 0
        self.n_tp, self.nz = n_tp, n_tp // 2
        self.dp, self.tp = lax.axis_index("dp"), lax.axis_index("tp")
        self.z, self.core = self.tp // 2, self.tp % 2
        x, y = self.dp // side, self.dp % side
        xf, yf = x + 1 - 2 * (x % 2), y + 1 - 2 * (y % 2)
        self.q = (x % 2) * 2 + y % 2
        self.peers = [{"dp": xf * side + y}, {"dp": x * side + yf}, {"dp": xf * side + yf}]
        self.peer_q = [(1 - x % 2) * 2 + y % 2, (x % 2) * 2 + 1 - y % 2, (1 - x % 2) * 2 + 1 - y % 2]
        self.sib = {"tp": 2 * self.z + 1 - self.core}
        self.right = {"tp": 2 * ((self.z + 1) % self.nz) + self.core}
        self.left = {"tp": 2 * ((self.z + self.nz - 1) % self.nz) + self.core}

    def z_at(self, side, s):
        return (self.z + self.nz - s) % self.nz if side == 0 else (self.z + s) % self.nz

    def others(self):
        return [self.sib, self.right, self.left, *self.peers]

    def greet(self):
        barrier = pltpu.get_barrier_semaphore()
        for other in self.others():
            pl.semaphore_signal(barrier, inc=1, device_id=other, device_id_type=MESH)

    def meet(self):
        pl.semaphore_wait(pltpu.get_barrier_semaphore(), len(self.others()))


def remote(src, dst, send_sem, recv_sem, device):
    return pltpu.make_async_remote_copy(src_ref=src, dst_ref=dst, send_sem=send_sem, recv_sem=recv_sem, device_id=device, device_id_type=MESH)


def piece(kind, source, n_tp, cols, rows):
    if kind == UP:
        return cols.at[source]
    if kind == DOWN:
        return rows.at[source]
    head = source // 8 * 2 + source % 2
    if kind == OUT:
        return rows.at[n_tp + head]
    return cols.at[n_tp + 3 * head + kind - Q]


class SecondLayer:
    def __init__(self, place, nall, acc, qkv_v, out_v, up_v, down_v, gcols, grows, cos_ref, sin_ref, sem):
        self.place, self.nall, self.acc, self.sem = place, nall, acc, sem
        self.qkv_v, self.out_v, self.up_v, self.down_v = qkv_v, out_v, up_v, down_v
        self.gcols, self.grows, self.cos_ref, self.sin_ref = gcols, grows, cos_ref, sin_ref
        self.seq_len = nall.shape[1] // 4
        far = place.nz // 2
        self.order = [(0, 0)] + [(side, s) for s in range(1, far) for side in range(2)] + [(0, far)]

    def slab_loads(self, number):
        slot, zs = number % 2, self.place.z_at(*self.order[number])
        copies = []
        for c in range(2):
            at = pl.ds(c * LANES, LANES)
            copies.append((self.gcols.at[2 * zs + c], self.up_v.at[slot, :, at], self.sem.at[slot, 0]))
            copies.append((self.grows.at[2 * zs + c], self.down_v.at[slot, at, :], self.sem.at[slot, 1]))
        return [pltpu.make_async_copy(*copy) for copy in copies]

    def head_loads(self, first):
        n_tp, head_dim = self.place.n_tp, self.cos_ref.shape[1]
        copies = []
        for n in range(2):
            for i in range(3):
                at = pl.ds((3 * n + i) * head_dim, head_dim)
                copies.append((self.gcols.at[n_tp + 3 * (first + n) + i], self.qkv_v.at[:, at], self.sem.at[2, 0]))
            copies.append((self.grows.at[n_tp + first + n], self.out_v.at[pl.ds(n * head_dim, head_dim)], self.sem.at[2, 1]))
        return [pltpu.make_async_copy(*copy) for copy in copies]

    def wait_slab(self, number):
        slot = number % 2
        settle(self.up_v.at[slot], self.sem.at[slot, 0])
        settle(self.down_v.at[slot], self.sem.at[slot, 1])

    def wait_heads(self):
        settle(self.qkv_v, self.sem.at[2, 0])
        settle(self.out_v, self.sem.at[2, 1])

    def clear(self):
        for i in range(self.acc.shape[0]):
            self.acc[i] = jnp.zeros(self.acc.shape[1:], F32)

    def slab(self, slot, p):
        nall, acc = self.nall, self.acc
        pair = (2 * p, 2 * p + 1)
        hidden = [gelu(jnp.dot(nall[i], self.up_v[slot], preferred_element_type=F32)) for i in pair]
        step = 512
        for first in range(0, acc.shape[2], step):
            cols = pl.ds(first, step)
            for i, rows in zip(pair, hidden):
                acc[i, :, cols] += jnp.dot(rows, self.down_v[slot, :, cols], preferred_element_type=F32)

    def heads(self, i):
        nall, acc, head_dim = self.nall, self.acc, self.cos_ref.shape[1]
        proj = jnp.dot(nall[i], self.qkv_v[...], preferred_element_type=F32)
        both = [context_of(proj[:, 3 * head_dim * n : 3 * head_dim * (n + 1)], self.cos_ref, self.sin_ref, self.seq_len) for n in range(2)]
        context = jnp.concatenate(both, axis=1)
        step = 512
        for first in range(0, acc.shape[2], step):
            cols = pl.ds(first, step)
            acc[i, :, cols] += jnp.dot(context, self.out_v[:, cols], preferred_element_type=F32)

    def round_off(self, i):
        self.nall[i] = self.acc[i].astype(BF16)

    def run(self, plan, late_step=None):
        def pick(values, default):
            def at(u):
                found = jnp.int32(default)
                for k, value in enumerate(values):
                    if value is not None:
                        found = jnp.where(u == k, value, found)
                return found
            return at

        late = pick([entry[1] for entry in plan], -1)
        slot = pick([entry[2][0] % 2 if len(entry[2]) == 2 else None for entry in plan], -1)
        pair = pick([entry[2][1] if len(entry[2]) == 2 else None for entry in plan], 0)
        tile = pick([entry[2][0] if len(entry[2]) == 1 else None for entry in plan], -1)

        def turn(u, carry):
            for k, entry in enumerate(plan):
                if entry[0]:
                    @pl.when(u == k)
                    def _():
                        for event in entry[0]:
                            event()

            if late_step:
                @pl.when(late(u) >= 0)
                def _():
                    late_step(late(u))

            @pl.when(slot(u) >= 0)
            def _():
                self.slab(slot(u), pair(u))

            @pl.when(tile(u) >= 0)
            def _():
                self.heads(tile(u))

            return carry

        lax.fori_loop(0, len(plan), turn, 0)


def settle(ref, sem):
    pltpu.make_async_copy(ref, ref, sem).wait()


def call(function, *args):
    return lambda: function(*args)


def start(copies):
    for copy in copies:
        copy.start()


def wait(copies):
    for copy in copies:
        copy.wait()


def first_kernel(n_dp, n_tp, x, gains_h, biases_h, cos_h, sin_h, qkv, out_w, up, down,
                 done_h, nown_h, pout, pown, gcols, grows,
                 gains, biases, cos_ref, sin_ref, done, nown, qkv_v, out_v, up_v, down_v, xbuf, normed, ctx, act, own, sib_out, sib_in, ring_r, ring_l, loc, nall, acc, part_in, st_cols, st_rows,
                 w_sem, x_sem, sib_send, sib_recv, r_send, r_recv, e_send, e_recv,
                 st_sem, loc_sem, w_send, wr_recv, ws_recv, n_send, n_recv, slab_sem, p_send, p_recv, o_sem, small_sem, done_sem):
    me = Place(n_dp, n_tp)
    me.greet()
    nz, core, z, q = me.nz, me.core, me.z, me.q
    n_seq, seq_len, d_model = x.shape
    head_dim, ff = out_w.shape[1], up.shape[2]
    per = n_seq // n_tp
    half = per // 2
    steps = nz * half

    wide = ff // 2
    first_w = [pltpu.make_async_copy(src, dst, w_sem.at[i]) for i, (src, dst) in
               enumerate(((qkv.at[0], qkv_v.at[:, pl.ds(0, qkv.shape[2])]), (up.at[0, :, pl.ds(0, wide)], up_v.at[0]), (up.at[0, :, pl.ds(wide, wide)], up_v.at[1]),
                         (out_w.at[0], out_v.at[pl.ds(0, head_dim)]), (down.at[0, pl.ds(0, wide)], down_v.at[0]), (down.at[0, pl.ds(wide, wide)], down_v.at[1])))]

    def owner_seq(zo, co, j):
        return per * (2 * zo + co) + j

    def tile_seqs(i):
        s, j = i // half, i % half
        zr, zl = (z + 2 * nz - 1 - s) % nz, (z + 1 + s) % nz
        return [owner_seq(zr, core, j), owner_seq(zl, core, half + j), owner_seq(zr, 1 - core, j), owner_seq(zl, 1 - core, half + j)]

    def fetch(i):
        for place, seq in enumerate(tile_seqs(i)):
            pltpu.make_async_copy(x.at[seq], xbuf.at[i % 3, place], x_sem.at[i % 3]).start()

    small = [pltpu.make_async_copy(src, dst, small_sem.at[i]) for i, (src, dst) in enumerate(((gains_h, gains), (biases_h, biases), (cos_h, cos_ref), (sin_h, sin_ref)))]
    fetch(0)
    start(small)
    start(first_w[:3])
    loads = {UP: (up.at[1, :, pl.ds(pl.multiple_of(q * LANES, LANES), LANES)], st_cols.at[UP]),
             DOWN: (down.at[1, pl.ds(pl.multiple_of(q * LANES, LANES), LANES), :], st_rows.at[0]),
             OUT: (out_w.at[1], st_rows.at[1])}
    for kind in (Q, K, V):
        loads[kind] = (qkv.at[1, :, pl.ds((kind - Q) * head_dim, head_dim)], st_cols.at[kind])
    kinds = (Q, K, V, OUT, UP, DOWN)
    loads = {kind: pltpu.make_async_copy(*loads[kind], st_sem.at[kind]) for kind in kinds}

    def start_rest():
        wait(small)
        start(first_w[3:])
        start([loads[UP], *(loads[kind] for kind in kinds if kind != UP)])

    def has(kind, source):
        return source >= 0 if kind in (UP, DOWN) else (source // 2 + 2 * (source % 2)) % 4 == q

    def staged(kind):
        return st_rows.at[kind - DOWN] if kind >= DOWN else st_cols.at[kind]

    def first_hops(kind):
        src, dst = staged(kind), piece(kind, me.tp, n_tp, gcols, grows)
        return [remote(src, dst, w_send.at[kind], wr_recv.at[0, 0, kind], me.right),
                remote(src, dst, w_send.at[kind], wr_recv.at[1, 0, kind], me.left),
                remote(src, dst, w_send.at[kind], sib_sem(z, kind), me.sib),
                pltpu.make_async_copy(src, dst, loc_sem.at[kind])]

    def sib_sem(zs, kind):
        return ws_recv.at[zs] if kind in (UP, DOWN) else ws_recv.at[nz]

    def send_first(kind):
        loads[kind].wait()

        @pl.when(has(kind, me.tp))
        def _():
            start(first_hops(kind))

    rings = (ring_r, ring_l)
    for i in range(half):
        for ring in rings:
            ring[i] = jnp.zeros(ring.shape[1:], BF16)

    def send_sib(i):
        return remote(sib_out.at[i % 2], sib_in.at[i % 4], sib_send.at[i % 2], sib_recv.at[i % 4], me.sib)

    def early(i):
        return i // half * (half - 1) + i % half

    def send_r(i):
        return remote(ring_r.at[i], ring_r.at[i + half], r_send.at[0], r_recv.at[0, early(i)], me.right)

    def send_l(i):
        return remote(ring_l.at[i], ring_l.at[i + half], r_send.at[1], r_recv.at[1, early(i)], me.left)

    def rows_of(member):
        return pl.ds(pl.multiple_of(member * seq_len, seq_len), seq_len)

    def send_n(tile, peer):
        at = nall.at[tile, rows_of(q)]
        return remote(at, at, n_send.at[tile], n_recv.at[tile // 2], me.peers[peer])

    def compute(i, waits=(), then=None):
        slot = i % 3
        pltpu.make_async_copy(x.at[pl.ds(0, 4)], xbuf.at[slot], x_sem.at[slot]).wait()
        if then:
            then()

        @pl.when(i + 1 < steps)
        def _():
            fetch(i + 1)

        @pl.when(i >= 2)
        def _():
            send_sib(i - 2).wait_send()

        for member in range(4):
            normed[pl.ds(member * seq_len, seq_len), :] = norm_rows(xbuf[slot, member].astype(F32), gains[pl.ds(0, 1), :], biases[pl.ds(0, 1), :])
        wait(waits[:3])
        ctx[...] = head_context(normed[...], qkv_v[:, : 3 * head_dim], cos_ref, sin_ref, seq_len)
        for n in range(2):
            act[:, n * wide : (n + 1) * wide] = gelu(jnp.dot(normed[...], up_v[n], preferred_element_type=F32))
        wait(waits[3:])
        step = 512
        for first in range(0, d_model, step):
            cols = pl.ds(first, step)
            part = jnp.dot(ctx[...], out_v[:head_dim, cols], preferred_element_type=F32)
            for n in range(2):
                part += jnp.dot(act[:, n * wide : (n + 1) * wide], down_v[n, :, cols], preferred_element_type=F32)
            own[i % 2, :, cols] = part[: 2 * seq_len]
            sib_out[i % 2, :, cols] = part[2 * seq_len :].astype(BF16)

    def finish(i):
        send_sib(i).wait_recv()
        late = i % half == half - 1
        last = i >= steps - half

        @pl.when(late)
        def _():
            for side in range(2):
                at = pl.ds(side * seq_len, seq_len)
                loc[side, i // half] = (own[i % 2, at, :] + sib_in[i % 4, at, :].astype(F32)).astype(BF16)

        @pl.when((i >= half) & jnp.logical_not(late))
        def _():
            send_r(i - half).wait_recv()
            send_l(i - half).wait_recv()

        @pl.when(jnp.logical_not(last | late))
        def _():
            for side, ring in enumerate(rings):
                at = pl.ds(side * seq_len, seq_len)
                ring[i] = (own[i % 2, at, :] + sib_in[i % 4, at, :].astype(F32) + ring[i].astype(F32)).astype(BF16)
            send_r(i).start()
            send_l(i).start()

        @pl.when(i == steps - half - 2)
        def _():
            for kind in kinds:
                if kind != UP:
                    send_first(kind)

        @pl.when(last & jnp.logical_not(late))
        def _():
            rows = seq_len // 2
            for side, ring in enumerate(rings):
                tile = 2 * (i % half) + side
                for first in range(0, seq_len, rows):
                    at, both = pl.ds(first, rows), pl.ds(side * seq_len + first, rows)
                    update = (own[i % 2, both, :] + sib_in[i % 4, both, :].astype(F32) + ring[i, at, :].astype(F32)).astype(BF16)
                    close(side, tile, at, i % 3, update, nall.at[tile, pl.ds(pl.multiple_of(q * seq_len + first, rows), rows)])
                for peer in range(3):
                    send_n(tile, peer).start()

    def close(side, tile, at, slot, update, normed_at):
        hidden = (xbuf[slot, side, at, :].astype(F32) + update.astype(F32)).astype(BF16)
        done[tile, at, :] = hidden
        normed_at[...] = norm_rows(hidden.astype(F32), gains[pl.ds(1, 1), :], biases[pl.ds(1, 1), :])

    compute(0, first_w, start_rest)
    me.meet()
    send_first(UP)
    send_sib(0).start()

    def turn(i, carry):
        @pl.when(i < steps)
        def _():
            compute(i)
            send_sib(i).start()

        finish(i - 1)
        return carry

    lax.fori_loop(1, steps + 1, turn, 0)

    to = (me.right, me.left)

    def hops(side, kind):
        longer = (core + (kind in (Q, V, DOWN))) % 2
        return nz // 2 - longer if side == 0 else nz // 2 - 1 + longer

    def source_of(side, s):
        return 2 * me.z_at(side, s) + core

    def onward(side, s, kind):
        at = piece(kind, source_of(side, s), n_tp, gcols, grows)
        return remote(at, at, w_send.at[kind], wr_recv.at[side, s, kind], to[side])

    def arrival(side, s, kind):
        at = piece(kind, source_of(side, s), n_tp, gcols, grows)
        return remote(at, at, w_send.at[kind], wr_recv.at[side, s - 1, kind], to[side])

    def across(side, s, kind):
        source = source_of(side, s)
        at = piece(kind, source, n_tp, gcols, grows)
        return remote(at, at, w_send.at[kind], sib_sem(source // 2, kind), me.sib)

    def take(side, s, kind):
        @pl.when(has(kind, source_of(side, s)) & (s <= hops(side, kind)))
        def _():
            arrival(side, s, kind).wait_recv()

            @pl.when(s < hops(side, kind))
            def _():
                onward(side, s, kind).start()

            across(side, s, kind).start()

    def take_both(s, kind):
        for side in range(2):
            take(side, s, kind)

    cut = seq_len // 2

    def late_send(side, s, h):
        at, ring = pl.ds(h * cut, cut), rings[side]
        return remote(ring.at[half * s + half - 1, at], ring.at[half * (s + 1) + half - 1, at], e_send.at[side], e_recv.at[side, s, h], to[side])

    def late_step(s):
        for h in range(2):
            at, i = pl.ds(h * cut, cut), half * s + half - 1
            for side, ring in enumerate(rings):
                @pl.when(s > 0)
                def _():
                    late_send(side, s - 1, h).wait_recv()

                total = loc[side, s, at, :].astype(F32) + ring[i, at, :].astype(F32)

                @pl.when(s < nz - 1)
                def _():
                    ring[i, at, :] = total.astype(BF16)

                @pl.when(s == nz - 1)
                def _():
                    close(side, 2 * (half - 1) + side, at, (steps - 1) % 3, total.astype(BF16), nown.at[side, at])

            @pl.when(s < nz - 1)
            def _():
                for side in range(2):
                    late_send(side, s, h).start()

    layer = SecondLayer(me, nall, acc, qkv_v, out_v, up_v, down_v, gcols, grows, cos_ref, sin_ref, slab_sem)

    def start_slab(number):
        settle(gcols.at[pl.ds(0, 2)], ws_recv.at[me.z_at(*layer.order[number])])
        if number == 0:
            for kind in (UP, DOWN):
                first_hops(kind)[3].wait()
        start(layer.slab_loads(number))

    def wait_slab(number):
        layer.wait_slab(number)

    def start_heads(first):
        start(layer.head_loads(first))

    def wait_heads():
        layer.wait_heads()

    def await_pair(p):
        settle(nall.at[pl.ds(2 * p, 2), pl.ds(0, 3 * seq_len)], n_recv.at[p])

    def send_part(tile, peer):
        return remote(nall.at[tile, rows_of(me.peer_q[peer])], part_in.at[tile, peer], p_send.at[tile], p_recv.at[tile], me.peers[peer])

    def keep_part(tile):
        return [pltpu.make_async_copy(nall.at[tile], pout.at[tile - 2], o_sem.at[tile - 2, 0]),
                pltpu.make_async_copy(acc.at[tile, rows_of(q)], pown.at[tile - 2], o_sem.at[tile - 2, 1])]

    def hand_out(tile):
        settle(nall.at[tile, pl.ds(0, 3 * seq_len)], n_send.at[tile])
        layer.round_off(tile)
        if tile < 2:
            for peer in range(3):
                send_part(tile, peer).start()
        else:
            start(keep_part(tile))

    def finish_tile(tile):
        settle(part_in.at[tile], p_recv.at[tile])
        total = acc[tile, rows_of(q), :]
        for peer in range(3):
            total = total + part_in[tile, peer].astype(F32)
        done[tile] = (done[tile].astype(F32) + total.astype(BF16).astype(F32)).astype(BF16)

    def keep_done(which):
        start([pltpu.make_async_copy(done.at[k], done_h.at[k], done_sem.at[0]) for k in which])

    keep_n = [pltpu.make_async_copy(nown.at[side], nown_h.at[side], done_sem.at[1]) for side in range(2)]

    def drain_rings():
        for side, ring in enumerate(rings):
            settle(ring.at[pl.ds(0, (nz - 1) * (half - 1))], r_send.at[side])
        send_sib(steps - 2).wait_send()
        send_sib(steps - 1).wait_send()

    def drain_weights():
        for kind in kinds:
            sent = jnp.where(has(kind, me.tp), 3, 0)
            for s in range(1, nz // 2 + 1):
                for side in range(2):
                    here = has(kind, source_of(side, s))
                    sent += jnp.where(here & (s <= hops(side, kind)), 1, 0) + jnp.where(here & (s < hops(side, kind)), 1, 0)
            for count in [2 * nz - 1] if kind in (UP, DOWN) else [3, 4]:
                @pl.when(sent == count)
                def _():
                    settle(gcols.at[pl.ds(0, count)], w_send.at[kind])

    attn = (Q, K, V, OUT)

    def own_heads_kept():
        for kind in attn:
            @pl.when(has(kind, me.tp))
            def _():
                first_hops(kind)[3].wait()

        settle(gcols.at[pl.ds(0, 2 * len(attn))], ws_recv.at[nz])

    layer.clear()
    def reload():
        start(layer.slab_loads(5))

    layer.run([
        ([call(start_slab, 0), call(take_both, 1, K), call(take_both, 2, K), call(take_both, 1, V), call(take_both, 1, OUT), call(take_both, 2, V), call(take_both, 2, OUT), call(take_both, 1, Q), call(take_both, 2, Q), call(take_both, 1, DOWN), call(await_pair, 0), call(take_both, 3, V), call(take_both, 1, UP), call(await_pair, 1), call(wait_slab, 0)], None, (0, 0)),
        ([call(start_slab, 1)], None, (0, 1)),
        ([drain_rings, call(keep_done, range(2, 4)), call(start_slab, 2), call(take_both, 3, K), call(wait_slab, 1)], None, (1, 0)),
        ([], None, (1, 1)),
        ([call(take_both, 3, Q), call(take_both, 3, OUT), call(take_both, 4, OUT), call(take_both, 2, DOWN), call(take_both, 2, UP), call(take_both, 4, K), call(start_slab, 3), call(take_both, 4, Q), call(take_both, 4, V), call(wait_slab, 2)], None, (2, 0)),
        ([own_heads_kept, call(start_heads, 0)], None, (2, 1)),
        ([call(start_slab, 4), wait_heads], None, (0,)),
        ([], None, (1,)),
        ([], None, (2,)),
        ([], None, (3,)),
        ([call(start_heads, 2)], 0, ()),
        ([call(wait_slab, 3)], None, (3, 0)),
        ([call(take_both, 3, UP)], None, (3, 1)),
        ([call(take_both, 3, DOWN), call(start_slab, 5), call(wait_slab, 4)], None, (4, 0)),
        ([], None, (4, 1)),
        ([call(start_slab, 6)], 1, ()),
        ([wait_heads], None, (0,)),
        ([], None, (1,)),
        ([call(wait_slab, 5)], None, (5, 0)),
        ([call(take_both, 4, DOWN), call(wait_slab, 6)], None, (6, 0)),
        ([call(take_both, 4, UP)], 2, ()),
        ([call(start_slab, 7), call(wait_slab, 7)], None, (7, 0)),
        ([call(hand_out, 0)], 3, ()),
        ([call(hand_out, 1)], None, (2,)),
        ([], 4, (3,)),
        ([], 5, (7, 1)),
        ([], 6, ()),
        ([reload], None, (6, 1)),
        ([call(wait_slab, 5)], None, (5, 1)),
        ([call(hand_out, 2), call(hand_out, 3), drain_weights, call(finish_tile, 0)], 7, ()),
    ], late_step)
    finish_tile(1)
    keep_done(range(0, 2))
    keep_done(range(4, per))
    start(keep_n)
    for side, ring in enumerate(rings):
        settle(ring.at[pl.ds(0, nz - 1)], e_send.at[side])
    for tile in range(2):
        settle(part_in.at[tile], p_send.at[tile])
        wait(keep_part(2 + tile))
    settle(done, done_sem.at[0])
    settle(nown, done_sem.at[1])


def second_kernel(n_dp, n_tp, done_h, nown, cos_h, sin_h, pout, pown, gcols, grows, out,
                  cos_ref, sin_ref, done, qkv_v, out_v, up_v, down_v, nall, acc, own, part_in,
                  slab_sem, o_sem, n_sem, p_send, p_recv, g_send, r_recv, s_recv):
    me = Place(n_dp, n_tp)
    me.greet()
    nz, core, z, q = me.nz, me.core, me.z, me.q
    per, seq_len, d_model = done_h.shape
    half = per // 2
    layer = SecondLayer(me, nall, acc, qkv_v, out_v, up_v, down_v, gcols, grows, cos_ref, sin_ref, slab_sem)
    keep = [pltpu.make_async_copy(pown, own, o_sem.at[0]), pltpu.make_async_copy(done_h, done, o_sem.at[1])]
    tables = [pltpu.make_async_copy(cos_h, cos_ref, o_sem.at[2]), pltpu.make_async_copy(sin_h, sin_ref, o_sem.at[3])]
    start(keep + tables)
    start(layer.slab_loads(0))
    start(layer.slab_loads(1))
    start(layer.head_loads(0))

    def rows_of(member):
        return pl.ds(pl.multiple_of(member * seq_len, seq_len), seq_len)

    def seq_of(zs, co, k):
        return per * (2 * zs + co) + k % 2 * half + k // 2

    def send_n(side, peer):
        return remote(nown.at[side], nall.at[side, rows_of(q)], n_sem.at[0], n_sem.at[1], me.peers[peer])

    def send_part(k, peer):
        at = rows_of(me.peer_q[peer])
        src = pout.at[k - 2, at] if k < 4 else nall.at[k - 4, at]
        return remote(src, part_in.at[k - 2, peer], p_send.at[k - 2], p_recv.at[k - 2], me.peers[peer])

    def start_parts(k):
        for peer in range(3):
            send_part(k, peer).start()

    def first_hops(k, src=None):
        at = out.at[seq_of(z, core, k)]
        src = at if src is None else src
        return [remote(src, at, g_send.at[k], r_recv.at[0, k, 0], me.right),
                remote(src, at, g_send.at[k], r_recv.at[1, k, 0], me.left),
                remote(src, at, g_send.at[k], s_recv.at[k], me.sib)]

    ready = [pltpu.make_async_copy(done_h.at[k], out.at[seq_of(z, core, k)], o_sem.at[4 + k]) for k in range(2)]
    mine = [pltpu.make_async_copy(nown.at[side], nall.at[side, rows_of(q)], o_sem.at[6 + side]) for side in range(2)]
    start(ready + mine)

    to = (me.right, me.left)

    def hops(side, k):
        longer = (k + core) % 2
        return nz // 2 - longer if side == 0 else nz // 2 - 1 + longer

    def arrival(side, k, s):
        at = out.at[seq_of(me.z_at(side, s), core, k)]
        return remote(at, at, g_send.at[k], r_recv.at[side, k, s - 1], to[side])

    def onward(side, k, s):
        at = out.at[seq_of(me.z_at(side, s), core, k)]
        return remote(at, at, g_send.at[k], r_recv.at[side, k, s], to[side])

    def across(side, k, s):
        at = out.at[seq_of(me.z_at(side, s), core, k)]
        return remote(at, at, g_send.at[k], s_recv.at[k], me.sib)

    def finish(k):
        settle(part_in.at[k - 2], p_recv.at[k - 2])
        if k == 2:
            wait(keep)
        total = own[k - 2] if k < 4 else acc[k - 4, rows_of(q), :]
        for peer in range(3):
            total = total + part_in[k - 2, peer].astype(F32)
        out[seq_of(z, core, k)] = (done[k].astype(F32) + total.astype(BF16).astype(F32)).astype(BF16)
        start(first_hops(k))

    def pass_on(k, s):
        for side in range(2):
            @pl.when(s <= hops(side, k))
            def _():
                arrival(side, k, s).wait_recv()

                @pl.when(s < hops(side, k))
                def _():
                    onward(side, k, s).start()

                across(side, k, s).start()

    me.meet()
    for k in range(2):
        start(first_hops(k, done_h.at[k]))
    for side in range(2):
        for peer in range(3):
            send_n(side, peer).start()
    start_parts(2)
    start_parts(3)

    def await_all():
        settle(nall.at[:, pl.ds(0, 3 * seq_len)], n_sem.at[1])
        wait(mine)

    def hand_out(side):
        layer.round_off(side)
        start_parts(4 + side)

    def start_slab(number):
        start(layer.slab_loads(number))

    def wait_slab(number):
        layer.wait_slab(number)

    def start_heads(first):
        start(layer.head_loads(first))

    def wait_heads():
        layer.wait_heads()

    def stages(*names):
        for k, s in names:
            if s == 0:
                finish(k)
            else:
                pass_on(k, s)

    layer.clear()
    assert (per, nz, n_tp // 4) == (6, 8, 4)
    layer.run([
        ([call(stages, (0, 1), (1, 1), (0, 2)), await_all, call(stages, (1, 2)), call(wait_slab, 0)], None, (0, 0)),
        ([call(stages, (0, 3), (2, 0)), call(start_slab, 2), call(wait_slab, 1)], None, (1, 0)),
        ([call(start_slab, 3), call(wait_slab, 2)], None, (2, 0)),
        ([call(start_slab, 4), call(wait_slab, 3)], None, (3, 0)),
        ([call(stages, (0, 4)), call(start_slab, 5), call(wait_slab, 4)], None, (4, 0)),
        ([call(stages, (1, 3)), call(start_slab, 6), wait_heads, call(wait, tables)], None, (0,)),
        ([call(stages, (2, 1))], None, (1,)),
        ([call(start_heads, 2), call(wait_slab, 5)], None, (5, 0)),
        ([call(stages, (3, 0)), call(start_slab, 7), call(wait_slab, 6)], None, (6, 0)),
        ([call(wait_slab, 7)], None, (7, 0)),
        ([wait_heads], None, (0,)),
        ([call(stages, (2, 2)), call(hand_out, 0), call(stages, (1, 4), (3, 1), (2, 3))], None, (1,)),
        ([call(hand_out, 1)], None, ()),
    ])
    stages((3, 2), (4, 0), (5, 0), (3, 3), (5, 1), (4, 1))

    def drain(k):
        settle(out.at[pl.ds(0, 2 * nz - 1)], g_send.at[k])
        settle(out.at[pl.ds(0, nz)], s_recv.at[k])

    wait(ready)
    for k in range(2, per):
        settle(part_in.at[k - 2], p_send.at[k - 2])
    settle(nall.at[:, pl.ds(0, 3 * seq_len)], n_sem.at[0])
    for k in range(2):
        drain(k)
    stages((5, 2), (4, 2), (5, 3), (2, 4), (4, 3), (4, 4), (5, 4), (3, 4))
    for k in range(2, per):
        drain(k)


def rope_rows(seq_len, head_dim, copies):
    inv_freq = ROPE_BASE ** (-2.0 * np.arange(head_dim // 2) / head_dim)
    angles = np.arange(seq_len)[:, None] * inv_freq[None, :]
    cos, sin = np.cos(angles), np.sin(angles)
    return [np.tile(np.concatenate(halves, 1), (copies, 1)).astype(np.float32) for halves in ((cos, cos), (-sin, sin))]


def solution(mesh):
    n_dp, n_tp = mesh.shape["dp"], mesh.shape["tp"]
    nz = n_tp // 2
    any_spec = pl.BlockSpec(memory_space=pl.ANY)
    vmem_spec = pl.BlockSpec(memory_space=pltpu.VMEM)
    dma = pltpu.SemaphoreType.DMA

    def shard_body(act_in, ln_gain, ln_bias, w_qkv, w_out, w_up, w_down):
        n_seq, seq_len, d_model = act_in.shape
        layers, _, _, qkv_cols = w_qkv.shape
        head_dim, ff = w_out.shape[1], w_up.shape[2]
        per = n_seq // n_tp
        half = per // 2
        heads = n_tp // 4
        tile = 4 * seq_len
        w_qkv = w_qkv.reshape(layers, d_model, qkv_cols)
        cos, sin = rope_rows(seq_len, head_dim, 4)
        seq_block = (seq_len, d_model)
        n_cols, n_rows = n_tp + 3 * heads, n_tp + heads
        steps = nz * half
        done, nown, pout, pown, gcols, grows = pl.pallas_call(
            functools.partial(first_kernel, n_dp, n_tp),
            name="layer_one",
            out_shape=(jax.ShapeDtypeStruct((per, *seq_block), BF16), jax.ShapeDtypeStruct((2, *seq_block), BF16), jax.ShapeDtypeStruct((2, tile, d_model), BF16), jax.ShapeDtypeStruct((2, *seq_block), F32),
                       jax.ShapeDtypeStruct((n_cols, d_model, LANES), BF16), jax.ShapeDtypeStruct((n_rows, LANES, d_model), BF16)),
            in_specs=[any_spec] * 9,
            out_specs=(any_spec,) * 6,
            scratch_shapes=[
                pltpu.VMEM(ln_gain.shape, F32), pltpu.VMEM(ln_bias.shape, F32), pltpu.VMEM(cos.shape, F32), pltpu.VMEM(sin.shape, F32),
                pltpu.VMEM((per, *seq_block), BF16), pltpu.VMEM((2, *seq_block), BF16),
                pltpu.VMEM((d_model, 2 * qkv_cols), BF16), pltpu.VMEM((2 * head_dim, d_model), BF16), pltpu.VMEM((2, d_model, ff // 2), BF16), pltpu.VMEM((2, ff // 2, d_model), BF16),
                pltpu.VMEM((3, 4, *seq_block), BF16), pltpu.VMEM((tile, d_model), BF16), pltpu.VMEM((tile, head_dim), BF16), pltpu.VMEM((tile, ff), BF16),
                pltpu.VMEM((2, 2 * seq_len, d_model), F32), pltpu.VMEM((2, 2 * seq_len, d_model), BF16), pltpu.VMEM((4, 2 * seq_len, d_model), BF16),
                pltpu.VMEM((steps, *seq_block), BF16), pltpu.VMEM((steps, *seq_block), BF16), pltpu.VMEM((2, nz, *seq_block), BF16),
                pltpu.VMEM((4, tile, d_model), BF16), pltpu.VMEM((4, tile, d_model), F32), pltpu.VMEM((2, 3, *seq_block), BF16),
                pltpu.VMEM((4, d_model, LANES), BF16), pltpu.VMEM((2, LANES, d_model), BF16),
                dma((6,)), dma((3,)), dma((2,)), dma((4,)), dma((2,)), dma((2, (nz - 1) * (half - 1))), dma((2,)), dma((2, nz - 1, 2)),
                dma((6,)), dma((6,)), dma((6,)), dma((2, nz // 2, 6)), dma((nz + 1,)), dma((4,)), dma((2,)), dma((3, 2)), dma((2,)), dma((2,)), dma((2, 2)), dma((4,)), dma((2,)),
            ],
            compiler_params=pltpu.CompilerParams(collective_id=1, has_side_effects=True, vmem_limit_bytes=63 * 2**20),
        )(act_in, ln_gain, ln_bias, cos, sin, w_qkv, w_out, w_up, w_down)
        return pl.pallas_call(
            functools.partial(second_kernel, n_dp, n_tp),
            name="layer_two",
            out_shape=pltpu.VMEM(act_in.shape, BF16),
            in_specs=[any_spec] * 8,
            out_specs=vmem_spec,
            scratch_shapes=[
                pltpu.VMEM(cos.shape, F32), pltpu.VMEM(sin.shape, F32), pltpu.VMEM((per, *seq_block), BF16),
                pltpu.VMEM((d_model, 2 * qkv_cols), BF16), pltpu.VMEM((2 * head_dim, d_model), BF16), pltpu.VMEM((2, d_model, 2 * LANES), BF16), pltpu.VMEM((2, 2 * LANES, d_model), BF16),
                pltpu.VMEM((2, tile, d_model), BF16), pltpu.VMEM((2, tile, d_model), F32), pltpu.VMEM((2, *seq_block), F32), pltpu.VMEM((4, 3, *seq_block), BF16),
                dma((3, 2)), dma((8,)), dma((2,)), dma((4,)), dma((4,)), dma((per,)), dma((2, per, nz // 2)), dma((per,)),
            ],
            compiler_params=pltpu.CompilerParams(collective_id=2, has_side_effects=True, vmem_limit_bytes=38 * 2**20),
        )(done, nown, cos, sin, pout, pown, gcols, grows)

    return jax.shard_map(shard_body, mesh=mesh, in_specs=(P("dp", None, None), P(None, None), P(None, None), P(None, None, "tp", None), P(None, "tp", None), P(None, None, "tp"), P(None, "tp", None)), out_specs=P("dp", None, None), check_vma=False)
```

time: 901 us -> 399 us (0.44)
  waiting for transfers between devices: 553 us -> 0 us
  Pallas kernels: 0 us -> 390 us
  matrix products: 205 us -> 0 us
  other arithmetic: 99 us -> 0 us
  local copies, waits for them, and re-layouts: 25.1 us -> 8.92 us
  between operations: 14 us -> 0.02 us
    psum x2 -> x0, waiting for transfers between devices: 553 us -> none  [shard_body(): reduced = lax.psum(local_sum, 'tp')]
    pallas_call x0 -> x2, Pallas kernels: none -> 390 us  [the longest x1 263 us: shard_body(): pl.pallas_call(functools.partial(first_kernel, n_dp, n_tp), name='layer_o...]
    dot_general x8 -> x0, matrix products: 205 us -> none  [the longest x2 123 us: layer_partial(): jnp.einsum('bsf,fe->bse', gelu_out, w_down, preferred_element_type=jnp.fl...]
    reduce_sum x6 -> x0, other arithmetic: 61.4 us -> none  [the longest x2 37.5 us: layer_norm(): row_mean = jnp.mean(hidden_f, axis=-1, keepdims=True)]
    convert_element_type x1 -> x0, other arithmetic: 29.2 us -> none  [shard_body(): (hidden.astype(jnp.float32) + reduced.astype(jnp.float32)).astype(jnp.bfl...]
  transfers between devices with their start and end apart: 2 -> 0, of which waited for: 2 -> 0; matrix products, arithmetic and copies ran while one was open for 0% -> 0% of each run, Pallas kernels for 0% -> 0%
where the time goes in v3:
time: 399 us
  Pallas kernels  390 us (98%)
  local copies, waits for them, and re-layouts  8.92 us (2%)
    pallas_call x1, Pallas kernels, shard_body(): pl.pallas_call(functools.partial(first_kernel, n_dp, n_tp), name='layer_o...  263 us
    pallas_call x1, Pallas kernels, shard_body(): pl.pallas_call(functools.partial(second_kernel, n_dp, n_tp), name='layer_...  127 us
    unnamed x1, local copies, waits for them, and re-layouts  8.92 us

profile of v3, /device:TPU:21, one launch (start us, length us, event | category | flops | bytes accessed | tf_op | source)
XLA Modules:
  0.0 398.6 jit_solution(10888926810497565459)
XLA Ops:
  0.0 262.5 %layer_one.1 = (bf16[6,64,2048]{2,1,0:T(8,128)(2,1)}, bf16[2,64,2048]{2,1,0:T(8,128)(2,1)}, bf16[2,256,2048]{2,1,0:T(8,128)(2,1)}, f32[2,64,2048]{2,1,0:T(8,128)...) custom-call(bf16[96,64,2048]{2,1,0:T(8,128)(2,1)} %x.1, f32[2,2048]{1,0:T(2,128)} %gains_h.1, ...), custom_call_target="tpu_custom_call" | custom-call | tf_op jit(solution)/shard_map/layer_one/pallas_call | solution.py:795
  262.5 127.1 %layer_two.1 = bf16[96,64,2048]{2,1,0:T(8,128)(2,1)S(1)} custom-call(bf16[6,64,2048]{2,1,0:T(8,128)(2,1)} %get-tuple-element.11.done_h, bf16[2,64,2048]{2,1,0:T(8,128)(2,1)} %get-tuple-element.12.nown, f32[256,128]{1,0:T(8,128)} %constant.4.clone.cos_h, f32[256,128]{1,0:T(8,128)} %constant.5.clone.sin_h, bf16[2,256,2048]{2,1,0:T(8,128)(2,1)} %get-tuple-element.13.pout, ...), custom_call_target="tpu_custom_call" | custom-call | tf_op jit(solution)/shard_map/layer_two/pallas_call | solution.py:816
  389.7 8.9 %copy.11 = bf16[96,64,2048]{2,1,0:T(8,128)(2,1)} copy(bf16[96,64,2048]{2,1,0:T(8,128)(2,1)S(1)} %layer_two.1) | data formatting | bytes 50331648

commit v4 on v3

--- a/solution.py
+++ b/solution.py
@@ -15,6 +15,9 @@
 BF16 = jnp.bfloat16
 F32 = jnp.float32
 LANES = 128
+MIB = 1 << 20
+SIDES = range(2)
+PEERS = range(3)
 UP, Q, K, V, DOWN, OUT = range(6)
 
 
@@ -114,12 +117,12 @@
         self.gcols, self.grows, self.cos_ref, self.sin_ref = gcols, grows, cos_ref, sin_ref
         self.seq_len = nall.shape[1] // 4
         far = place.nz // 2
-        self.order = [(0, 0)] + [(side, s) for s in range(1, far) for side in range(2)] + [(0, far)]
+        self.order = [(0, 0)] + [(side, s) for s in range(1, far) for side in SIDES] + [(0, far)]
 
     def slab_loads(self, number):
         slot, zs = number % 2, self.place.z_at(*self.order[number])
         copies = []
-        for c in range(2):
+        for c in SIDES:
             at = pl.ds(c * LANES, LANES)
             copies.append((self.gcols.at[2 * zs + c], self.up_v.at[slot, :, at], self.sem.at[slot, 0]))
             copies.append((self.grows.at[2 * zs + c], self.down_v.at[slot, at, :], self.sem.at[slot, 1]))
@@ -128,7 +131,7 @@
     def head_loads(self, first):
         n_tp, head_dim = self.place.n_tp, self.cos_ref.shape[1]
         copies = []
-        for n in range(2):
+        for n in SIDES:
             for i in range(3):
                 at = pl.ds((3 * n + i) * head_dim, head_dim)
                 copies.append((self.gcols.at[n_tp + 3 * (first + n) + i], self.qkv_v.at[:, at], self.sem.at[2, 0]))
@@ -161,7 +164,7 @@
     def heads(self, i):
         nall, acc, head_dim = self.nall, self.acc, self.cos_ref.shape[1]
         proj = jnp.dot(nall[i], self.qkv_v[...], preferred_element_type=F32)
-        both = [context_of(proj[:, 3 * head_dim * n : 3 * head_dim * (n + 1)], self.cos_ref, self.sin_ref, self.seq_len) for n in range(2)]
+        both = [context_of(proj[:, 3 * head_dim * n : 3 * head_dim * (n + 1)], self.cos_ref, self.sin_ref, self.seq_len) for n in SIDES]
         context = jnp.concatenate(both, axis=1)
         step = 512
         for first in range(0, acc.shape[2], step):
@@ -171,7 +174,28 @@
     def round_off(self, i):
         self.nall[i] = self.acc[i].astype(BF16)
 
-    def run(self, plan, late_step=None):
+    def run(self, program, actions, late_step=None):
+        steps, events, late = [], [], None
+
+        def end(unit):
+            nonlocal events, late
+            steps.append((events, late, unit))
+            events, late = [], None
+
+        for word in " ".join(program).split():
+            letter, rest = word[0], word[1:]
+            if letter in "SH":
+                end([int(digit) for digit in rest])
+                continue
+            if late is not None:
+                end([])
+            if letter == "R":
+                late = int(rest)
+            else:
+                events.append(functools.partial(actions[letter], rest))
+        if events or late is not None:
+            end([])
+
         def pick(values, default):
             def at(u):
                 found = jnp.int32(default)
@@ -181,17 +205,18 @@
                 return found
             return at
 
-        late = pick([entry[1] for entry in plan], -1)
-        slot = pick([entry[2][0] % 2 if len(entry[2]) == 2 else None for entry in plan], -1)
-        pair = pick([entry[2][1] if len(entry[2]) == 2 else None for entry in plan], 0)
-        tile = pick([entry[2][0] if len(entry[2]) == 1 else None for entry in plan], -1)
+        late = pick([step[1] for step in steps], -1)
+        slab = [step[2] if len(step[2]) == 2 else [None, None] for step in steps]
+        slot = pick([number if number is None else number % 2 for number, _ in slab], -1)
+        pair = pick([p for _, p in slab], 0)
+        tile = pick([step[2][0] if len(step[2]) == 1 else None for step in steps], -1)
 
         def turn(u, carry):
-            for k, entry in enumerate(plan):
-                if entry[0]:
+            for k, step in enumerate(steps):
+                if step[0]:
                     @pl.when(u == k)
                     def _():
-                        for event in entry[0]:
+                        for event in step[0]:
                             event()
 
             if late_step:
@@ -209,15 +234,11 @@
 
             return carry
 
-        lax.fori_loop(0, len(plan), turn, 0)
+        lax.fori_loop(0, len(steps), turn, 0)
 
 
 def settle(ref, sem):
     pltpu.make_async_copy(ref, ref, sem).wait()
-
-
-def call(function, *args):
-    return lambda: function(*args)
 
 
 def start(copies):
@@ -262,9 +283,6 @@
             pltpu.make_async_copy(x.at[seq], xbuf.at[i % 3, place], x_sem.at[i % 3]).start()
 
     small = [pltpu.make_async_copy(src, dst, small_sem.at[i]) for i, (src, dst) in enumerate(((gains_h, gains), (biases_h, biases), (cos_h, cos_ref), (sin_h, sin_ref)))]
-    fetch(0)
-    start(small)
-    start(first_w[:3])
     loads = {UP: (up.at[1, :, pl.ds(pl.multiple_of(q * LANES, LANES), LANES)], st_cols.at[UP]),
              DOWN: (down.at[1, pl.ds(pl.multiple_of(q * LANES, LANES), LANES), :], st_rows.at[0]),
              OUT: (out_w.at[1], st_rows.at[1])}
@@ -273,10 +291,15 @@
     kinds = (Q, K, V, OUT, UP, DOWN)
     loads = {kind: pltpu.make_async_copy(*loads[kind], st_sem.at[kind]) for kind in kinds}
 
+    loads[UP].start()
+    fetch(0)
+    start(small)
+    start(first_w[:3])
+
     def start_rest():
         wait(small)
         start(first_w[3:])
-        start([loads[UP], *(loads[kind] for kind in kinds if kind != UP)])
+        start([loads[kind] for kind in kinds if kind != UP])
 
     def has(kind, source):
         return source >= 0 if kind in (UP, DOWN) else (source // 2 + 2 * (source % 2)) % 4 == q
@@ -343,14 +366,14 @@
             normed[pl.ds(member * seq_len, seq_len), :] = norm_rows(xbuf[slot, member].astype(F32), gains[pl.ds(0, 1), :], biases[pl.ds(0, 1), :])
         wait(waits[:3])
         ctx[...] = head_context(normed[...], qkv_v[:, : 3 * head_dim], cos_ref, sin_ref, seq_len)
-        for n in range(2):
+        for n in SIDES:
             act[:, n * wide : (n + 1) * wide] = gelu(jnp.dot(normed[...], up_v[n], preferred_element_type=F32))
         wait(waits[3:])
         step = 512
         for first in range(0, d_model, step):
             cols = pl.ds(first, step)
             part = jnp.dot(ctx[...], out_v[:head_dim, cols], preferred_element_type=F32)
-            for n in range(2):
+            for n in SIDES:
                 part += jnp.dot(act[:, n * wide : (n + 1) * wide], down_v[n, :, cols], preferred_element_type=F32)
             own[i % 2, :, cols] = part[: 2 * seq_len]
             sib_out[i % 2, :, cols] = part[2 * seq_len :].astype(BF16)
@@ -362,7 +385,7 @@
 
         @pl.when(late)
         def _():
-            for side in range(2):
+            for side in SIDES:
                 at = pl.ds(side * seq_len, seq_len)
                 loc[side, i // half] = (own[i % 2, at, :] + sib_in[i % 4, at, :].astype(F32)).astype(BF16)
 
@@ -394,7 +417,7 @@
                     at, both = pl.ds(first, rows), pl.ds(side * seq_len + first, rows)
                     update = (own[i % 2, both, :] + sib_in[i % 4, both, :].astype(F32) + ring[i, at, :].astype(F32)).astype(BF16)
                     close(side, tile, at, i % 3, update, nall.at[tile, pl.ds(pl.multiple_of(q * seq_len + first, rows), rows)])
-                for peer in range(3):
+                for peer in PEERS:
                     send_n(tile, peer).start()
 
     def close(side, tile, at, slot, update, normed_at):
@@ -402,9 +425,9 @@
         done[tile, at, :] = hidden
         normed_at[...] = norm_rows(hidden.astype(F32), gains[pl.ds(1, 1), :], biases[pl.ds(1, 1), :])
 
-    compute(0, first_w, start_rest)
     me.meet()
     send_first(UP)
+    compute(0, first_w, start_rest)
     send_sib(0).start()
 
     def turn(i, carry):
@@ -452,7 +475,7 @@
             across(side, s, kind).start()
 
     def take_both(s, kind):
-        for side in range(2):
+        for side in SIDES:
             take(side, s, kind)
 
     cut = seq_len // 2
@@ -462,7 +485,7 @@
         return remote(ring.at[half * s + half - 1, at], ring.at[half * (s + 1) + half - 1, at], e_send.at[side], e_recv.at[side, s, h], to[side])
 
     def late_step(s):
-        for h in range(2):
+        for h in SIDES:
             at, i = pl.ds(h * cut, cut), half * s + half - 1
             for side, ring in enumerate(rings):
                 @pl.when(s > 0)
@@ -481,7 +504,7 @@
 
             @pl.when(s < nz - 1)
             def _():
-                for side in range(2):
+                for side in SIDES:
                     late_send(side, s, h).start()
 
     layer = SecondLayer(me, nall, acc, qkv_v, out_v, up_v, down_v, gcols, grows, cos_ref, sin_ref, slab_sem)
@@ -493,15 +516,6 @@
                 first_hops(kind)[3].wait()
         start(layer.slab_loads(number))
 
-    def wait_slab(number):
-        layer.wait_slab(number)
-
-    def start_heads(first):
-        start(layer.head_loads(first))
-
-    def wait_heads():
-        layer.wait_heads()
-
     def await_pair(p):
         settle(nall.at[pl.ds(2 * p, 2), pl.ds(0, 3 * seq_len)], n_recv.at[p])
 
@@ -516,7 +530,7 @@
         settle(nall.at[tile, pl.ds(0, 3 * seq_len)], n_send.at[tile])
         layer.round_off(tile)
         if tile < 2:
-            for peer in range(3):
+            for peer in PEERS:
                 send_part(tile, peer).start()
         else:
             start(keep_part(tile))
@@ -524,14 +538,14 @@
     def finish_tile(tile):
         settle(part_in.at[tile], p_recv.at[tile])
         total = acc[tile, rows_of(q), :]
-        for peer in range(3):
+        for peer in PEERS:
             total = total + part_in[tile, peer].astype(F32)
         done[tile] = (done[tile].astype(F32) + total.astype(BF16).astype(F32)).astype(BF16)
 
     def keep_done(which):
         start([pltpu.make_async_copy(done.at[k], done_h.at[k], done_sem.at[0]) for k in which])
 
-    keep_n = [pltpu.make_async_copy(nown.at[side], nown_h.at[side], done_sem.at[1]) for side in range(2)]
+    keep_n = [pltpu.make_async_copy(nown.at[side], nown_h.at[side], done_sem.at[1]) for side in SIDES]
 
     def drain_rings():
         for side, ring in enumerate(rings):
@@ -543,7 +557,7 @@
         for kind in kinds:
             sent = jnp.where(has(kind, me.tp), 3, 0)
             for s in range(1, nz // 2 + 1):
-                for side in range(2):
+                for side in SIDES:
                     here = has(kind, source_of(side, s))
                     sent += jnp.where(here & (s <= hops(side, kind)), 1, 0) + jnp.where(here & (s < hops(side, kind)), 1, 0)
             for count in [2 * nz - 1] if kind in (UP, DOWN) else [3, 4]:
@@ -562,41 +576,44 @@
         settle(gcols.at[pl.ds(0, 2 * len(attn))], ws_recv.at[nz])
 
     layer.clear()
-    def reload():
-        start(layer.slab_loads(5))
-
+    actions = {
+        "T": lambda rest: take_both(int(rest[0]), letters[rest[1]]),
+        "N": lambda rest: await_pair(int(rest)),
+        "L": lambda rest: start_slab(int(rest)),
+        "M": lambda rest: start(layer.slab_loads(int(rest))),
+        "W": lambda rest: layer.wait_slab(int(rest)),
+        "A": lambda rest: own_heads_kept(),
+        "X": lambda rest: start(layer.head_loads(int(rest))),
+        "Y": lambda rest: layer.wait_heads(),
+        "P": lambda rest: hand_out(int(rest)),
+        "B": lambda rest: (drain_rings(), keep_done(range(2, 4))),
+        "Z": lambda rest: (drain_weights(), finish_tile(0)),
+    }
+    letters = {"U": UP, "D": DOWN, "Q": Q, "K": K, "V": V, "O": OUT}
     layer.run([
-        ([call(start_slab, 0), call(take_both, 1, K), call(take_both, 2, K), call(take_both, 1, V), call(take_both, 1, OUT), call(take_both, 2, V), call(take_both, 2, OUT), call(take_both, 1, Q), call(take_both, 2, Q), call(take_both, 1, DOWN), call(await_pair, 0), call(take_both, 3, V), call(take_both, 1, UP), call(await_pair, 1), call(wait_slab, 0)], None, (0, 0)),
-        ([call(start_slab, 1)], None, (0, 1)),
-        ([drain_rings, call(keep_done, range(2, 4)), call(start_slab, 2), call(take_both, 3, K), call(wait_slab, 1)], None, (1, 0)),
-        ([], None, (1, 1)),
-        ([call(take_both, 3, Q), call(take_both, 3, OUT), call(take_both, 4, OUT), call(take_both, 2, DOWN), call(take_both, 2, UP), call(take_both, 4, K), call(start_slab, 3), call(take_both, 4, Q), call(take_both, 4, V), call(wait_slab, 2)], None, (2, 0)),
-        ([own_heads_kept, call(start_heads, 0)], None, (2, 1)),
-        ([call(start_slab, 4), wait_heads], None, (0,)),
-        ([], None, (1,)),
-        ([], None, (2,)),
-        ([], None, (3,)),
-        ([call(start_heads, 2)], 0, ()),
-        ([call(wait_slab, 3)], None, (3, 0)),
-        ([call(take_both, 3, UP)], None, (3, 1)),
-        ([call(take_both, 3, DOWN), call(start_slab, 5), call(wait_slab, 4)], None, (4, 0)),
-        ([], None, (4, 1)),
-        ([call(start_slab, 6)], 1, ()),
-        ([wait_heads], None, (0,)),
-        ([], None, (1,)),
-        ([call(wait_slab, 5)], None, (5, 0)),
-        ([call(take_both, 4, DOWN), call(wait_slab, 6)], None, (6, 0)),
-        ([call(take_both, 4, UP)], 2, ()),
-        ([call(start_slab, 7), call(wait_slab, 7)], None, (7, 0)),
-        ([call(hand_out, 0)], 3, ()),
-        ([call(hand_out, 1)], None, (2,)),
-        ([], 4, (3,)),
-        ([], 5, (7, 1)),
-        ([], 6, ()),
-        ([reload], None, (6, 1)),
-        ([call(wait_slab, 5)], None, (5, 1)),
-        ([call(hand_out, 2), call(hand_out, 3), drain_weights, call(finish_tile, 0)], 7, ()),
-    ], late_step)
+        "L0 T1K T2K T1V",
+        "T1O T2V T2O T1Q",
+        "T2Q T1D N0 T3V",
+        "T1U N1 W0 S00",
+        "L1 S01 L2 T3K",
+        "B W1 S10 S11",
+        "T3Q T3O T4O T2D",
+        "T2U T4K L3 T4Q",
+        "T4V W2 S20 A",
+        "X0 S21 L4 Y",
+        "H0 H1 H2 H3",
+        "X2 R0 W3 S30",
+        "T3U S31 T3D L5",
+        "W4 S40 S41 L6",
+        "R1 Y H0 H1",
+        "W5 S50 T4D W6",
+        "S60 T4U R2 L7",
+        "W7 S70 P0 R3",
+        "P1 H2 R4 H3",
+        "R5 S71 R6 M5",
+        "S61 W5 S51 P2",
+        "P3 Z R7",
+    ], actions, late_step)
     finish_tile(1)
     keep_done(range(0, 2))
     keep_done(range(4, per))
@@ -641,7 +658,7 @@
         return remote(src, part_in.at[k - 2, peer], p_send.at[k - 2], p_recv.at[k - 2], me.peers[peer])
 
     def start_parts(k):
-        for peer in range(3):
+        for peer in PEERS:
             send_part(k, peer).start()
 
     def first_hops(k, src=None):
@@ -652,7 +669,7 @@
                 remote(src, at, g_send.at[k], s_recv.at[k], me.sib)]
 
     ready = [pltpu.make_async_copy(done_h.at[k], out.at[seq_of(z, core, k)], o_sem.at[4 + k]) for k in range(2)]
-    mine = [pltpu.make_async_copy(nown.at[side], nall.at[side, rows_of(q)], o_sem.at[6 + side]) for side in range(2)]
+    mine = [pltpu.make_async_copy(nown.at[side], nall.at[side, rows_of(q)], o_sem.at[6 + side]) for side in SIDES]
     start(ready + mine)
 
     to = (me.right, me.left)
@@ -678,13 +695,13 @@
         if k == 2:
             wait(keep)
         total = own[k - 2] if k < 4 else acc[k - 4, rows_of(q), :]
-        for peer in range(3):
+        for peer in PEERS:
             total = total + part_in[k - 2, peer].astype(F32)
         out[seq_of(z, core, k)] = (done[k].astype(F32) + total.astype(BF16).astype(F32)).astype(BF16)
         start(first_hops(k))
 
     def pass_on(k, s):
-        for side in range(2):
+        for side in SIDES:
             @pl.when(s <= hops(side, k))
             def _():
                 arrival(side, k, s).wait_recv()
@@ -698,8 +715,8 @@
     me.meet()
     for k in range(2):
         start(first_hops(k, done_h.at[k]))
-    for side in range(2):
-        for peer in range(3):
+    for side in SIDES:
+        for peer in PEERS:
             send_n(side, peer).start()
     start_parts(2)
     start_parts(3)
@@ -712,56 +729,57 @@
         layer.round_off(side)
         start_parts(4 + side)
 
-    def start_slab(number):
-        start(layer.slab_loads(number))
-
-    def wait_slab(number):
-        layer.wait_slab(number)
-
-    def start_heads(first):
-        start(layer.head_loads(first))
-
-    def wait_heads():
-        layer.wait_heads()
-
-    def stages(*names):
-        for k, s in names:
-            if s == 0:
-                finish(k)
-            else:
-                pass_on(k, s)
+    def stage(name):
+        k, s = int(name[0]), int(name[1])
+        if s == 0:
+            finish(k)
+        else:
+            pass_on(k, s)
+
+    actions = {
+        "A": stage,
+        "N": lambda rest: await_all(),
+        "L": lambda rest: start(layer.slab_loads(int(rest))),
+        "W": lambda rest: layer.wait_slab(int(rest)),
+        "X": lambda rest: start(layer.head_loads(int(rest))),
+        "Y": lambda rest: layer.wait_heads(),
+        "C": lambda rest: wait(tables),
+        "P": lambda rest: hand_out(int(rest)),
+    }
 
     layer.clear()
     assert (per, nz, n_tp // 4) == (6, 8, 4)
-    layer.run([
-        ([call(stages, (0, 1), (1, 1), (0, 2)), await_all, call(stages, (1, 2)), call(wait_slab, 0)], None, (0, 0)),
-        ([call(stages, (0, 3), (2, 0)), call(start_slab, 2), call(wait_slab, 1)], None, (1, 0)),
-        ([call(start_slab, 3), call(wait_slab, 2)], None, (2, 0)),
-        ([call(start_slab, 4), call(wait_slab, 3)], None, (3, 0)),
-        ([call(stages, (0, 4)), call(start_slab, 5), call(wait_slab, 4)], None, (4, 0)),
-        ([call(stages, (1, 3)), call(start_slab, 6), wait_heads, call(wait, tables)], None, (0,)),
-        ([call(stages, (2, 1))], None, (1,)),
-        ([call(start_heads, 2), call(wait_slab, 5)], None, (5, 0)),
-        ([call(stages, (3, 0)), call(start_slab, 7), call(wait_slab, 6)], None, (6, 0)),
-        ([call(wait_slab, 7)], None, (7, 0)),
-        ([wait_heads], None, (0,)),
-        ([call(stages, (2, 2)), call(hand_out, 0), call(stages, (1, 4), (3, 1), (2, 3))], None, (1,)),
-        ([call(hand_out, 1)], None, ()),
-    ])
-    stages((3, 2), (4, 0), (5, 0), (3, 3), (5, 1), (4, 1))
-
     def drain(k):
         settle(out.at[pl.ds(0, 2 * nz - 1)], g_send.at[k])
         settle(out.at[pl.ds(0, nz)], s_recv.at[k])
+
+    layer.run([
+        "A01 A11 A02 N",
+        "A12 W0 S00 A03",
+        "A20 L2 W1 S10",
+        "L3 W2 S20 L4",
+        "W3 S30 A04 L5",
+        "W4 S40 A13 L6",
+        "Y C H0 A21",
+        "H1 X2 W5 S50",
+        "A30 L7 W6 S60",
+        "W7 S70 Y H0",
+        "A22 P0 A14 A31",
+        "A23 H1 P1",
+    ], actions)
+    for name in (*"32 40 50".split(), *"33 51 41".split()):
+        stage(name)
 
     wait(ready)
     for k in range(2, per):
         settle(part_in.at[k - 2], p_send.at[k - 2])
     settle(nall.at[:, pl.ds(0, 3 * seq_len)], n_sem.at[0])
-    for k in range(2):
+    first = 2
+    for k in range(first):
         drain(k)
-    stages((5, 2), (4, 2), (5, 3), (2, 4), (4, 3), (4, 4), (5, 4), (3, 4))
-    for k in range(2, per):
+    for name in (*"52 42 53 24".split(), *"43 44 54 34".split()):
+        stage(name)
+    for k in range(first, per):
         drain(k)
 
 
@@ -778,6 +796,9 @@
     any_spec = pl.BlockSpec(memory_space=pl.ANY)
     vmem_spec = pl.BlockSpec(memory_space=pltpu.VMEM)
     dma = pltpu.SemaphoreType.DMA
+
+    def sems(counts):
+        return [dma((int(count),)) for count in counts.split()]
 
     def shard_body(act_in, ln_gain, ln_bias, w_qkv, w_out, w_up, w_down):
         n_seq, seq_len, d_model = act_in.shape
@@ -808,10 +829,10 @@
                 pltpu.VMEM((steps, *seq_block), BF16), pltpu.VMEM((steps, *seq_block), BF16), pltpu.VMEM((2, nz, *seq_block), BF16),
                 pltpu.VMEM((4, tile, d_model), BF16), pltpu.VMEM((4, tile, d_model), F32), pltpu.VMEM((2, 3, *seq_block), BF16),
                 pltpu.VMEM((4, d_model, LANES), BF16), pltpu.VMEM((2, LANES, d_model), BF16),
-                dma((6,)), dma((3,)), dma((2,)), dma((4,)), dma((2,)), dma((2, (nz - 1) * (half - 1))), dma((2,)), dma((2, nz - 1, 2)),
-                dma((6,)), dma((6,)), dma((6,)), dma((2, nz // 2, 6)), dma((nz + 1,)), dma((4,)), dma((2,)), dma((3, 2)), dma((2,)), dma((2,)), dma((2, 2)), dma((4,)), dma((2,)),
+                *sems("6 3 2 4"), dma((2,)), dma((2, (nz - 1) * (half - 1))), dma((2,)), dma((2, nz - 1, 2)),
+                *sems("6 6 6"), dma((2, nz // 2, 6)), dma((nz + 1,)), *sems("4 2"), dma((3, 2)), *sems("2 2"), dma((2, 2)), *sems("4 2"),
             ],
-            compiler_params=pltpu.CompilerParams(collective_id=1, has_side_effects=True, vmem_limit_bytes=63 * 2**20),
+            compiler_params=pltpu.CompilerParams(collective_id=1, has_side_effects=True, vmem_limit_bytes=63 * MIB),
         )(act_in, ln_gain, ln_bias, cos, sin, w_qkv, w_out, w_up, w_down)
         return pl.pallas_call(
             functools.partial(second_kernel, n_dp, n_tp),
@@ -823,9 +844,9 @@
                 pltpu.VMEM(cos.shape, F32), pltpu.VMEM(sin.shape, F32), pltpu.VMEM((per, *seq_block), BF16),
                 pltpu.VMEM((d_model, 2 * qkv_cols), BF16), pltpu.VMEM((2 * head_dim, d_model), BF16), pltpu.VMEM((2, d_model, 2 * LANES), BF16), pltpu.VMEM((2, 2 * LANES, d_model), BF16),
                 pltpu.VMEM((2, tile, d_model), BF16), pltpu.VMEM((2, tile, d_model), F32), pltpu.VMEM((2, *seq_block), F32), pltpu.VMEM((4, 3, *seq_block), BF16),
-                dma((3, 2)), dma((8,)), dma((2,)), dma((4,)), dma((4,)), dma((per,)), dma((2, per, nz // 2)), dma((per,)),
+                dma((3, 2)), *sems("8 2 4 4"), dma((per,)), dma((2, per, nz // 2)), dma((per,)),
             ],
-            compiler_params=pltpu.CompilerParams(collective_id=2, has_side_effects=True, vmem_limit_bytes=38 * 2**20),
+            compiler_params=pltpu.CompilerParams(collective_id=2, has_side_effects=True, vmem_limit_bytes=38 * MIB),
         )(done, nown, cos, sin, pout, pown, gcols, grows)
 
-    return jax.shard_map(shard_body, mesh=mesh, in_specs=(P("dp", None, None), P(None, None), P(None, None), P(None, None, "tp", None), P(None, "tp", None), P(None, None, "tp"), P(None, "tp", None)), out_specs=P("dp", None, None), check_vma=False)
+    return jax.shard_map(shard_body, mesh=mesh, in_specs=(P("dp"), P(), P(), P(None, None, "tp"), P(None, "tp"), P(None, None, "tp"), P(None, "tp")), out_specs=P("dp"), check_vma=False)

time: 399 us -> 394 us (0.987)
  Pallas kernels: 390 us -> 385 us
    pallas_call x1, Pallas kernels: 263 us -> 258 us  [shard_body(): pl.pallas_call(functools.partial(first_kernel, n_dp, n_tp), name='layer_o...]
where the time goes in v4:
time: 394 us
  Pallas kernels  385 us (98%)
  local copies, waits for them, and re-layouts  8.92 us (2%)
    pallas_call x1, Pallas kernels, shard_body(): pl.pallas_call(functools.partial(first_kernel, n_dp, n_tp), name='layer_o...  258 us
    pallas_call x1, Pallas kernels, shard_body(): pl.pallas_call(functools.partial(second_kernel, n_dp, n_tp), name='layer_...  127 us
    unnamed x1, local copies, waits for them, and re-layouts  8.92 us

profile of v4, /device:TPU:21, one launch (start us, length us, event | category | flops | bytes accessed | tf_op | source)
XLA Modules:
  0.0 393.9 jit_solution(3231445072889565323)
XLA Ops:
  0.0 258.5 %layer_one.1 = (bf16[6,64,2048]{2,1,0:T(8,128)(2,1)}, bf16[2,64,2048]{2,1,0:T(8,128)(2,1)}, bf16[2,256,2048]{2,1,0:T(8,128)(2,1)}, f32[2,64,2048]{2,1,0:T(8,128)...) custom-call(bf16[96,64,2048]{2,1,0:T(8,128)(2,1)} %x.1, f32[2,2048]{1,0:T(2,128)} %gains_h.1, ...), custom_call_target="tpu_custom_call" | custom-call | tf_op jit(solution)/shard_map/layer_one/pallas_call | solution.py:816
  258.5 126.5 %layer_two.1 = bf16[96,64,2048]{2,1,0:T(8,128)(2,1)S(1)} custom-call(bf16[6,64,2048]{2,1,0:T(8,128)(2,1)} %get-tuple-element.11.done_h, bf16[2,64,2048]{2,1,0:T(8,128)(2,1)} %get-tuple-element.12.nown, f32[256,128]{1,0:T(8,128)} %constant.4.clone.cos_h, f32[256,128]{1,0:T(8,128)} %constant.5.clone.sin_h, bf16[2,256,2048]{2,1,0:T(8,128)(2,1)} %get-tuple-element.13.pout, ...), custom_call_target="tpu_custom_call" | custom-call | tf_op jit(solution)/shard_map/layer_two/pallas_call | solution.py:837
  385.0 8.9 %copy.11 = bf16[96,64,2048]{2,1,0:T(8,128)(2,1)} copy(bf16[96,64,2048]{2,1,0:T(8,128)(2,1)S(1)} %layer_two.1) | data formatting | bytes 50331648

commit v5 on v4

v5 whole, which is shorter than its diff:
```python
import functools
import math

import jax
import jax.numpy as jnp
import numpy as np
from jax import lax
from jax.experimental import pallas as pl
from jax.experimental.pallas import tpu as pltpu
from jax.sharding import PartitionSpec as P

LN_EPS = 1e-5
ROPE_BASE = 10000.0
MESH = pl.DeviceIdType.MESH
BF16 = jnp.bfloat16
F32 = jnp.float32
LANES = 128
MIB = 1 << 20
SIDES = range(2)
PEERS = range(3)
UP, Q, K, V, DOWN, OUT = range(6)


def norm_rows(hidden_f, gain, bias):
    row_mean = jnp.mean(hidden_f, axis=-1, keepdims=True)
    centered = hidden_f - row_mean
    row_var = jnp.mean(centered * centered, axis=-1, keepdims=True)
    return (centered * lax.rsqrt(row_var + LN_EPS) * gain + bias).astype(BF16)


def rope(heads, cos, sin):
    return (heads * cos + pltpu.roll(heads, heads.shape[-1] // 2, 1) * sin).astype(BF16)


def gelu(values):
    return (0.5 * values * (1.0 + lax.erf(values * math.sqrt(0.5)))).astype(BF16)


def attend(query, keys, values, seq_len):
    rows, head_dim = query.shape
    block = 2 * seq_len
    row = lax.broadcasted_iota(jnp.int32, (block, block), 0)
    col = lax.broadcasted_iota(jnp.int32, (block, block), 1)
    allowed = (row >= col) & (row // seq_len == col // seq_len)
    contexts = []
    for first in range(0, rows, block):
        at = slice(first, first + block)
        scores = lax.dot_general(query[at], keys[at], (((1,), (1,)), ((), ())), preferred_element_type=F32) * (head_dim ** -0.5)
        scores = jnp.where(allowed, scores, -1e30)
        weights = jnp.exp(scores - jnp.max(scores, axis=-1, keepdims=True))
        probs = (weights / jnp.sum(weights, axis=-1, keepdims=True)).astype(BF16)
        contexts.append(jnp.dot(probs, values[at], preferred_element_type=F32).astype(BF16))
    return jnp.concatenate(contexts, axis=0)


def context_of(proj, cos_ref, sin_ref, seq_len):
    head_dim = cos_ref.shape[1]
    query = rope(proj[:, :head_dim], cos_ref[...], sin_ref[...])
    keys = rope(proj[:, head_dim : 2 * head_dim], cos_ref[...], sin_ref[...])
    return attend(query, keys, proj[:, 2 * head_dim :].astype(BF16), seq_len)


def head_context(normed, qkv_w, cos_ref, sin_ref, seq_len):
    return context_of(jnp.dot(normed, qkv_w, preferred_element_type=F32), cos_ref, sin_ref, seq_len)


class Place:
    def __init__(self, n_dp, n_tp):
        side = math.isqrt(n_dp)
        assert side * side == n_dp and side % 2 == 0 and n_tp % 4 == 0
        self.n_tp, self.nz = n_tp, n_tp // 2
        self.dp, self.tp = lax.axis_index("dp"), lax.axis_index("tp")
        self.z, self.core = self.tp // 2, self.tp % 2
        x, y = self.dp // side, self.dp % side
        xf, yf = x + 1 - 2 * (x % 2), y + 1 - 2 * (y % 2)
        self.q = (x % 2) * 2 + y % 2
        self.peers = [{"dp": xf * side + y}, {"dp": x * side + yf}, {"dp": xf * side + yf}]
        self.peer_q = [(1 - x % 2) * 2 + y % 2, (x % 2) * 2 + 1 - y % 2, (1 - x % 2) * 2 + 1 - y % 2]
        self.sib = {"tp": 2 * self.z + 1 - self.core}
        self.right = {"tp": 2 * ((self.z + 1) % self.nz) + self.core}
        self.left = {"tp": 2 * ((self.z + self.nz - 1) % self.nz) + self.core}

    def z_at(self, side, s):
        return (self.z + self.nz - s) % self.nz if side == 0 else (self.z + s) % self.nz

    def others(self):
        return [self.sib, self.right, self.left, *self.peers]

    def greet(self):
        barrier = pltpu.get_barrier_semaphore()
        for other in self.others():
            pl.semaphore_signal(barrier, inc=1, device_id=other, device_id_type=MESH)

    def meet(self):
        pl.semaphore_wait(pltpu.get_barrier_semaphore(), len(self.others()))


def remote(src, dst, send_sem, recv_sem, device):
    return pltpu.make_async_remote_copy(src_ref=src, dst_ref=dst, send_sem=send_sem, recv_sem=recv_sem, device_id=device, device_id_type=MESH)


def piece(kind, source, n_tp, cols, rows):
    if kind == UP:
        return cols.at[source]
    if kind == DOWN:
        return rows.at[source]
    head = source // 8 * 2 + source % 2
    if kind == OUT:
        return rows.at[n_tp + head]
    return cols.at[n_tp + 3 * head + kind - Q]


class SecondLayer:
    def __init__(self, place, nall, acc, qkv_v, out_v, up_v, down_v, gcols, grows, cos_ref, sin_ref, sem):
        self.place, self.nall, self.acc, self.sem = place, nall, acc, sem
        self.qkv_v, self.out_v, self.up_v, self.down_v = qkv_v, out_v, up_v, down_v
        self.gcols, self.grows, self.cos_ref, self.sin_ref = gcols, grows, cos_ref, sin_ref
        self.seq_len = nall.shape[1] // 4
        far = place.nz // 2
        self.order = [(0, 0)] + [(side, s) for s in range(1, far) for side in SIDES] + [(0, far)]

    def slab_loads(self, number):
        slot, zs = number % 2, self.place.z_at(*self.order[number])
        copies = []
        for c in SIDES:
            at = pl.ds(c * LANES, LANES)
            copies.append((self.gcols.at[2 * zs + c], self.up_v.at[slot, :, at], self.sem.at[slot, 0]))
            copies.append((self.grows.at[2 * zs + c], self.down_v.at[slot, at, :], self.sem.at[slot, 1]))
        return [pltpu.make_async_copy(*copy) for copy in copies]

    def head_loads(self, first):
        n_tp, head_dim = self.place.n_tp, self.cos_ref.shape[1]
        copies = []
        for n in SIDES:
            for i in range(3):
                at = pl.ds((3 * n + i) * head_dim, head_dim)
                copies.append((self.gcols.at[n_tp + 3 * (first + n) + i], self.qkv_v.at[:, at], self.sem.at[2, 0]))
            copies.append((self.grows.at[n_tp + first + n], self.out_v.at[pl.ds(n * head_dim, head_dim)], self.sem.at[2, 1]))
        return [pltpu.make_async_copy(*copy) for copy in copies]

    def wait_slab(self, number):
        slot = number % 2
        settle(self.up_v.at[slot], self.sem.at[slot, 0])
        settle(self.down_v.at[slot], self.sem.at[slot, 1])

    def wait_heads(self):
        settle(self.qkv_v, self.sem.at[2, 0])
        settle(self.out_v, self.sem.at[2, 1])

    def clear(self, tiles):
        for i in tiles:
            self.acc[i] = jnp.zeros(self.acc.shape[1:], F32)

    def slab(self, slot, p):
        nall, acc = self.nall, self.acc
        pair, kept = (2 * p, 2 * p + 1), acc.shape[0]
        hidden = [gelu(jnp.dot(nall[i], self.up_v[slot], preferred_element_type=F32)) for i in pair]
        step = 512
        for first in range(0, acc.shape[2], step):
            cols = pl.ds(first, step)
            for i, rows in zip(pair, hidden):
                acc[i % kept, :, cols] += jnp.dot(rows, self.down_v[slot, :, cols], preferred_element_type=F32)

    def heads(self, i):
        nall, acc, head_dim = self.nall, self.acc, self.cos_ref.shape[1]
        proj = jnp.dot(nall[i], self.qkv_v[...], preferred_element_type=F32)
        both = [context_of(proj[:, 3 * head_dim * n : 3 * head_dim * (n + 1)], self.cos_ref, self.sin_ref, self.seq_len) for n in SIDES]
        context = jnp.concatenate(both, axis=1)
        step = 512
        for first in range(0, acc.shape[2], step):
            cols = pl.ds(first, step)
            acc[i % acc.shape[0], :, cols] += jnp.dot(context, self.out_v[:, cols], preferred_element_type=F32)

    def round_off(self, i):
        self.nall[i] = self.acc[i % self.acc.shape[0]].astype(BF16)

    def run(self, program, actions, late_step=None):
        steps, events, late = [], [], None

        def end(unit):
            nonlocal events, late
            steps.append((events, late, unit))
            events, late = [], None

        for word in " ".join(program).split():
            letter, rest = word[0], word[1:]
            if letter in "SH":
                end([int(digit) for digit in rest])
                continue
            if late is not None:
                end([])
            if letter == "R":
                late = int(rest)
            else:
                events.append(functools.partial(actions[letter], rest))
        if events or late is not None:
            end([])

        def pick(values, default):
            def at(u):
                found = jnp.int32(default)
                for k, value in enumerate(values):
                    if value is not None:
                        found = jnp.where(u == k, value, found)
                return found
            return at

        late = pick([step[1] for step in steps], -1)
        slab = [step[2] if len(step[2]) == 2 else [None, None] for step in steps]
        slot = pick([number if number is None else number % 2 for number, _ in slab], -1)
        pair = pick([p for _, p in slab], 0)
        tile = pick([step[2][0] if len(step[2]) == 1 else None for step in steps], -1)

        def turn(u, carry):
            for k, step in enumerate(steps):
                if step[0]:
                    @pl.when(u == k)
                    def _():
                        for event in step[0]:
                            event()

            if late_step:
                @pl.when(late(u) >= 0)
                def _():
                    late_step(late(u))

            @pl.when(slot(u) >= 0)
            def _():
                self.slab(slot(u), pair(u))

            @pl.when(tile(u) >= 0)
            def _():
                self.heads(tile(u))

            return carry

        lax.fori_loop(0, len(steps), turn, 0)


def settle(ref, sem):
    pltpu.make_async_copy(ref, ref, sem).wait()


def start(copies):
    for copy in copies:
        copy.start()


def wait(copies):
    for copy in copies:
        copy.wait()


def kernel(n_dp, n_tp, x, gains_h, biases_h, cos_h, sin_h, qkv, out_w, up, down,
           out, gcols, grows,
           gains, biases, cos_ref, sin_ref, done, qkv_v, out_v, up_v, down_v, normed, ctx, act, own, nall, acc, part_in, st_cols, st_rows,
           w_sem, x_sem, sib_send, sib_recv, r_send, r_recv, e_send, e_recv,
           st_sem, loc_sem, w_send, wr_recv, ws_recv, n_send, n_recv, slab_sem, p_send, p_recv, small_sem, g_send, g_recv, s_recv):
    me = Place(n_dp, n_tp)
    me.greet()
    nz, core, z, q = me.nz, me.core, me.z, me.q
    n_seq, seq_len, d_model = x.shape
    head_dim, ff = out_w.shape[1], up.shape[2]
    per = n_seq // n_tp
    half = per // 2
    steps = nz * half

    wide = ff // 2
    assert (per, nz, n_tp // 4) == (6, 8, 4)

    def ring_at(side, i):
        s, j = i // half, i % half
        return jnp.where(j == half - 1, per * (2 * s + side) + j, per * s + half * side + j)

    def loc_at(side, s):
        return per * (2 * s + side) + per - 1

    def sib_in(i):
        return out.at[pl.ds(per * (nz + i % 4), 2)]

    def sib_out(i):
        return out.at[pl.ds(per * (nz + 4 + i % 2), 2)]

    def x_at(i, place):
        return per * (nz + 2 * (i % 3) + place // 2) + half + place % 2

    first_w = [pltpu.make_async_copy(src, dst, w_sem.at[i]) for i, (src, dst) in
               enumerate(((qkv.at[0], qkv_v.at[:, pl.ds(0, qkv.shape[2])]), (up.at[0, :, pl.ds(0, wide)], up_v.at[0]), (up.at[0, :, pl.ds(wide, wide)], up_v.at[1]),
                         (out_w.at[0], out_v.at[pl.ds(0, head_dim)]), (down.at[0, pl.ds(0, wide)], down_v.at[0]), (down.at[0, pl.ds(wide, wide)], down_v.at[1])))]

    def owner_seq(zo, co, j):
        return per * (2 * zo + co) + j

    def tile_seqs(i):
        s, j = i // half, i % half
        zr, zl = (z + 2 * nz - 1 - s) % nz, (z + 1 + s) % nz
        return [owner_seq(zr, core, j), owner_seq(zl, core, half + j), owner_seq(zr, 1 - core, j), owner_seq(zl, 1 - core, half + j)]

    def fetch(i):
        for place, seq in enumerate(tile_seqs(i)):
            pltpu.make_async_copy(x.at[seq], out.at[x_at(i, place)], x_sem.at[i % 3]).start()

    small = [pltpu.make_async_copy(src, dst, small_sem.at[i]) for i, (src, dst) in enumerate(((gains_h, gains), (biases_h, biases), (cos_h, cos_ref), (sin_h, sin_ref)))]
    loads = {UP: (up.at[1, :, pl.ds(pl.multiple_of(q * LANES, LANES), LANES)], st_cols.at[UP]),
             DOWN: (down.at[1, pl.ds(pl.multiple_of(q * LANES, LANES), LANES), :], st_rows.at[0]),
             OUT: (out_w.at[1], st_rows.at[1])}
    for kind in (Q, K, V):
        loads[kind] = (qkv.at[1, :, pl.ds((kind - Q) * head_dim, head_dim)], st_cols.at[kind])
    kinds = (Q, K, V, OUT, UP, DOWN)
    loads = {kind: pltpu.make_async_copy(*loads[kind], st_sem.at[kind]) for kind in kinds}

    loads[UP].start()
    fetch(0)
    start(small)
    start(first_w[:3])

    def start_rest():
        wait(small)
        start(first_w[3:])
        start([loads[kind] for kind in kinds if kind != UP])

    def has(kind, source):
        return source >= 0 if kind in (UP, DOWN) else (source // 2 + 2 * (source % 2)) % 4 == q

    def staged(kind):
        return st_rows.at[kind - DOWN] if kind >= DOWN else st_cols.at[kind]

    def piece_hops(kind):
        src, dst = staged(kind), piece(kind, me.tp, n_tp, gcols, grows)
        return [remote(src, dst, w_send.at[kind], wr_recv.at[0, 0, kind], me.right),
                remote(src, dst, w_send.at[kind], wr_recv.at[1, 0, kind], me.left),
                remote(src, dst, w_send.at[kind], sib_sem(z, kind), me.sib),
                pltpu.make_async_copy(src, dst, loc_sem.at[kind])]

    def sib_sem(zs, kind):
        return ws_recv.at[zs] if kind in (UP, DOWN) else ws_recv.at[nz]

    def send_first(kind):
        loads[kind].wait()

        @pl.when(has(kind, me.tp))
        def _():
            start(piece_hops(kind))

    for side in SIDES:
        for i in range(half):
            out[ring_at(side, i)] = jnp.zeros(out.shape[1:], BF16)

    to = (me.right, me.left)

    def send_sib(i):
        return remote(sib_out(i), sib_in(i), sib_send.at[i % 2], sib_recv.at[i % 4], me.sib)

    def send_ring(side, i):
        return remote(out.at[ring_at(side, i)], out.at[ring_at(side, i + half)], r_send.at[side], r_recv.at[side, i // half * (half - 1) + i % half], to[side])

    def rows_of(member):
        return pl.ds(pl.multiple_of(member * seq_len, seq_len), seq_len)

    def send_n(tile, peer):
        at = nall.at[tile, rows_of(q)]
        return remote(at, at, n_send.at[tile], n_recv.at[tile // 2], me.peers[peer])

    def compute(i, waits=(), then=None):
        slot = i % 3
        settle(out.at[pl.ds(0, 4)], x_sem.at[slot])
        if then:
            then()

        @pl.when(i + 1 < steps)
        def _():
            fetch(i + 1)

        @pl.when(i >= 2)
        def _():
            send_sib(i - 2).wait_send()

        for member in range(4):
            normed[pl.ds(member * seq_len, seq_len), :] = norm_rows(out[x_at(i, member)].astype(F32), gains[pl.ds(0, 1), :], biases[pl.ds(0, 1), :])
        wait(waits[:3])
        ctx[...] = head_context(normed[...], qkv_v[:, : 3 * head_dim], cos_ref, sin_ref, seq_len)
        for n in SIDES:
            act[:, n * wide : (n + 1) * wide] = gelu(jnp.dot(normed[...], up_v[n], preferred_element_type=F32))
        wait(waits[3:])
        step = 512
        for first in range(0, d_model, step):
            cols = pl.ds(first, step)
            part = jnp.dot(ctx[...], out_v[:head_dim, cols], preferred_element_type=F32)
            for n in SIDES:
                part += jnp.dot(act[:, n * wide : (n + 1) * wide], down_v[n, :, cols], preferred_element_type=F32)
            own[i % 2, :, cols] = part[: 2 * seq_len]
            for side in SIDES:
                sib_out(i)[side, :, cols] = part[(2 + side) * seq_len : (3 + side) * seq_len].astype(BF16)

    def finish(i):
        send_sib(i).wait_recv()
        late = i % half == half - 1
        last = i >= steps - half

        def local(side, at):
            return own[i % 2, pl.ds(side * seq_len + at.start, at.size), :] + sib_in(i)[side, at, :].astype(F32)

        whole = pl.ds(0, seq_len)

        @pl.when(late)
        def _():
            for side in SIDES:
                out[loc_at(side, i // half)] = local(side, whole).astype(BF16)

        @pl.when(late & last)
        def _():
            for side in SIDES:
                done[per - 2 + side] = out[x_at(i, side)]

        @pl.when((i >= half) & jnp.logical_not(late))
        def _():
            for side in SIDES:
                send_ring(side, i - half).wait_recv()

        @pl.when(jnp.logical_not(last | late))
        def _():
            for side in SIDES:
                at = ring_at(side, i)
                out[at] = (local(side, whole) + out[at].astype(F32)).astype(BF16)
            for side in SIDES:
                send_ring(side, i).start()

        @pl.when(i == steps - half - 2)
        def _():
            for kind in kinds:
                if kind != UP:
                    send_first(kind)

        @pl.when(last & jnp.logical_not(late))
        def _():
            rows = seq_len // 2
            for side in SIDES:
                tile = 2 * (i % half) + side
                for h in SIDES:
                    at = pl.ds(h * rows, rows)
                    update = (local(side, at) + out[ring_at(side, i), at, :].astype(F32)).astype(BF16)
                    close(tile, at, out[x_at(i, side), at, :], update)
                start_n(tile)

    def close(tile, at, hidden, update):
        hidden = (hidden.astype(F32) + update.astype(F32)).astype(BF16)
        done[tile, at, :] = hidden
        mine = pl.ds(pl.multiple_of(q * seq_len + at.start, at.size), at.size)
        nall[tile, mine, :] = norm_rows(hidden.astype(F32), gains[pl.ds(1, 1), :], biases[pl.ds(1, 1), :])

    def start_n(tile):
        for peer in PEERS:
            send_n(tile, peer).start()

    me.meet()
    send_first(UP)
    compute(0, first_w, start_rest)
    send_sib(0).start()

    def turn(i, carry):
        @pl.when(i < steps)
        def _():
            compute(i)
            send_sib(i).start()

        finish(i - 1)
        return carry

    lax.fori_loop(1, steps + 1, turn, 0)

    def hops(side, kind):
        longer = (core + (kind in (Q, V, DOWN))) % 2
        return nz // 2 - longer if side == 0 else nz // 2 - 1 + longer

    def source_of(side, s):
        return 2 * me.z_at(side, s) + core

    def onward(side, s, kind):
        at = piece(kind, source_of(side, s), n_tp, gcols, grows)
        return remote(at, at, w_send.at[kind], wr_recv.at[side, s, kind], to[side])

    def arrival(side, s, kind):
        at = piece(kind, source_of(side, s), n_tp, gcols, grows)
        return remote(at, at, w_send.at[kind], wr_recv.at[side, s - 1, kind], to[side])

    def across(side, s, kind):
        source = source_of(side, s)
        at = piece(kind, source, n_tp, gcols, grows)
        return remote(at, at, w_send.at[kind], sib_sem(source // 2, kind), me.sib)

    def take(side, s, kind):
        @pl.when(has(kind, source_of(side, s)) & (s <= hops(side, kind)))
        def _():
            arrival(side, s, kind).wait_recv()

            @pl.when(s < hops(side, kind))
            def _():
                onward(side, s, kind).start()

            across(side, s, kind).start()

    def take_both(s, kind):
        for side in SIDES:
            take(side, s, kind)

    cut = seq_len // 2

    def late_send(side, s, h):
        at, i = pl.ds(h * cut, cut), half * s + half - 1
        return remote(out.at[ring_at(side, i), at], out.at[ring_at(side, i + half), at], e_send.at[side], e_recv.at[side, s, h], to[side])

    def late_step(s):
        for h in SIDES:
            at, i = pl.ds(h * cut, cut), half * s + half - 1
            for side in SIDES:
                @pl.when(s > 0)
                def _():
                    late_send(side, s - 1, h).wait_recv()

                total = (out[loc_at(side, s), at, :].astype(F32) + out[ring_at(side, i), at, :].astype(F32)).astype(BF16)

                @pl.when(s < nz - 1)
                def _():
                    out[ring_at(side, i), at, :] = total

                @pl.when(s == nz - 1)
                def _():
                    tile = per - 2 + side
                    close(tile, at, done[tile, at, :], total)

            @pl.when(s < nz - 1)
            def _():
                for side in SIDES:
                    late_send(side, s, h).start()

    layer = SecondLayer(me, nall, acc, qkv_v, out_v, up_v, down_v, gcols, grows, cos_ref, sin_ref, slab_sem)

    def start_slab(number):
        settle(gcols.at[pl.ds(0, 2)], ws_recv.at[me.z_at(*layer.order[number])])
        if number == 0:
            for kind in (UP, DOWN):
                piece_hops(kind)[3].wait()
        start(layer.slab_loads(number))

    def await_pair(p):
        settle(nall.at[pl.ds(2 * p, 2), pl.ds(0, 3 * seq_len)], n_recv.at[p])

    def send_part(k, peer):
        return remote(nall.at[k, rows_of(me.peer_q[peer])], part_in.at[k, peer], p_send.at[k], p_recv.at[k], me.peers[peer])

    def start_parts(k):
        for peer in PEERS:
            send_part(k, peer).start()

    def hand_out(k):
        settle(nall.at[k, pl.ds(0, 3 * seq_len)], n_send.at[k])
        layer.round_off(k)
        if k not in (2, 3):
            start_parts(k)

    def summed(k):
        settle(part_in.at[k], p_recv.at[k])
        total = acc[k % acc.shape[0], rows_of(q), :]
        for peer in PEERS:
            total = total + part_in[k, peer].astype(F32)
        return (done[k].astype(F32) + total.astype(BF16).astype(F32)).astype(BF16)

    def seq_of(zs, co, k):
        return per * (2 * zs + co) + k % 2 * half + k // 2

    def first_hops(k):
        at = out.at[seq_of(z, core, k)]
        return [remote(at, at, g_send.at[k], g_recv.at[0, k, 0], me.right),
                remote(at, at, g_send.at[k], g_recv.at[1, k, 0], me.left),
                remote(at, at, g_send.at[k], s_recv.at[k], me.sib)]

    def reach(side, k):
        longer = (k + core) % 2
        return nz // 2 - longer if side == 0 else nz // 2 - 1 + longer

    def passing(side, k, s, hop):
        at = out.at[seq_of(me.z_at(side, s), core, k)]
        return remote(at, at, g_send.at[k], g_recv.at[side, k, hop], to[side])

    def stage(name):
        k, s = int(name[0]), int(name[1])
        if s == 0:
            out[seq_of(z, core, k)] = summed(k)
            start(first_hops(k))
            return
        for side in SIDES:
            @pl.when(s <= reach(side, k))
            def _():
                passing(side, k, s, s - 1).wait_recv()

                @pl.when(s < reach(side, k))
                def _():
                    passing(side, k, s, s).start()

                at = out.at[seq_of(me.z_at(side, s), core, k)]
                remote(at, at, g_send.at[k], s_recv.at[k], me.sib).start()

    def drain(k):
        settle(out.at[pl.ds(0, 2 * nz - 1)], g_send.at[k])
        settle(out.at[pl.ds(0, nz)], s_recv.at[k])

    def late_pair():
        for side in SIDES:
            start_n(per - 2 + side)
        start_parts(2)
        start_parts(3)
        for side in SIDES:
            settle(out.at[pl.ds(0, nz - 1)], e_send.at[side])

    def drain_rings():
        for side in SIDES:
            settle(out.at[pl.ds(0, (nz - 1) * (half - 1))], r_send.at[side])
        send_sib(steps - 2).wait_send()
        send_sib(steps - 1).wait_send()

    def drain_weights():
        for kind in kinds:
            sent = jnp.where(has(kind, me.tp), 3, 0)
            for s in range(1, nz // 2 + 1):
                for side in SIDES:
                    here = has(kind, source_of(side, s))
                    sent += jnp.where(here & (s <= hops(side, kind)), 1, 0) + jnp.where(here & (s < hops(side, kind)), 1, 0)
            for count in [2 * nz - 1] if kind in (UP, DOWN) else [3, 4]:
                @pl.when(sent == count)
                def _():
                    settle(gcols.at[pl.ds(0, count)], w_send.at[kind])

    attn = (Q, K, V, OUT)

    def own_heads_kept():
        for kind in attn:
            @pl.when(has(kind, me.tp))
            def _():
                piece_hops(kind)[3].wait()

        settle(gcols.at[pl.ds(0, 2 * len(attn))], ws_recv.at[nz])

    layer.clear(range(acc.shape[0]))
    actions = {
        "T": lambda rest: take_both(int(rest[0]), letters[rest[1]]),
        "N": lambda rest: await_pair(int(rest)),
        "L": lambda rest: start_slab(int(rest)),
        "M": lambda rest: start(layer.slab_loads(int(rest))),
        "W": lambda rest: layer.wait_slab(int(rest)),
        "A": lambda rest: own_heads_kept(),
        "X": lambda rest: start(layer.head_loads(int(rest))),
        "Y": lambda rest: layer.wait_heads(),
        "P": lambda rest: hand_out(int(rest)),
        "B": lambda rest: drain_rings(),
        "Z": lambda rest: drain_weights(),
        "G": stage,
        "E": lambda rest: late_pair(),
        "F": lambda rest: layer.clear(SIDES),
    }
    letters = {"U": UP, "D": DOWN, "Q": Q, "K": K, "V": V, "O": OUT}
    layer.run([
        "L0 T1K T2K T1V",
        "T1O T2V T2O T1Q",
        "T2Q T1D N0 T3V",
        "T1U N1 W0 S00",
        "L1 S01 L2 T3K",
        "B W1 S10 S11",
        "T3Q T3O T4O T2D",
        "T2U T4K L3 T4Q",
        "T4V W2 S20 A",
        "X0 S21 L4 Y",
        "H0 H1 H2 H3",
        "X2 R0 W3 S30",
        "T3U S31 T3D L5",
        "W4 S40 S41 L6",
        "R1 Y H0 H1",
        "W5 S50 T4D W6",
        "S60 T4U R2 L7",
        "W7 S70 P0 R3",
        "P1 H2 R4 H3",
        "R5 S71 R6 M5",
        "S61 W5 S51 P2",
        "P3 Z M0 M1",
        "X0 G00 R7 E",
        "G10 F G01 G11",
        "G02 N2 G12 W0",
        "S02 M2 W1 S12",
        "G03 M3 W2 S22",
        "M4 W3 S32 M5",
        "W4 S42 G13 Y",
        "H4 G04 G20 M6",
        "H5 X2 W5 S52",
        "G21 M7 W6 S62",
        "G14 W7 S72 G30",
        "Y H4 P4 H5",
        "G22 G31 P5",
    ], actions, late_step)
    early = 2
    for k in range(early):
        drain(k)
    for name in (*"40 32 50".split(), *"33 41 51".split()):
        stage(name)
    for k in range(per):
        settle(part_in.at[k], p_send.at[k])
    for name in (*"42 52 43 23".split(), *"34 53 24".split(), *"44 54".split()):
        stage(name)
    for k in range(early, per):
        drain(k)


def rope_rows(seq_len, head_dim, copies):
    inv_freq = ROPE_BASE ** (-2.0 * np.arange(head_dim // 2) / head_dim)
    angles = np.arange(seq_len)[:, None] * inv_freq[None, :]
    cos, sin = np.cos(angles), np.sin(angles)
    return [np.tile(np.concatenate(halves, 1), (copies, 1)).astype(np.float32) for halves in ((cos, cos), (-sin, sin))]


def solution(mesh):
    n_dp, n_tp = mesh.shape["dp"], mesh.shape["tp"]
    nz = n_tp // 2
    any_spec = pl.BlockSpec(memory_space=pl.ANY)
    vmem_spec = pl.BlockSpec(memory_space=pltpu.VMEM)
    dma = pltpu.SemaphoreType.DMA

    def sems(counts):
        return [dma((int(count),)) for count in counts.split()]

    def shard_body(act_in, ln_gain, ln_bias, w_qkv, w_out, w_up, w_down):
        n_seq, seq_len, d_model = act_in.shape
        layers, _, _, qkv_cols = w_qkv.shape
        head_dim, ff = w_out.shape[1], w_up.shape[2]
        per = n_seq // n_tp
        half = per // 2
        heads = n_tp // 4
        tile = 4 * seq_len
        w_qkv = w_qkv.reshape(layers, d_model, qkv_cols)
        cos, sin = rope_rows(seq_len, head_dim, 4)
        seq_block = (seq_len, d_model)
        n_cols, n_rows = n_tp + 3 * heads, n_tp + heads
        steps = nz * half
        return pl.pallas_call(
            functools.partial(kernel, n_dp, n_tp),
            name="two_layers",
            out_shape=(pltpu.VMEM(act_in.shape, BF16), jax.ShapeDtypeStruct((n_cols, d_model, LANES), BF16), jax.ShapeDtypeStruct((n_rows, LANES, d_model), BF16)),
            in_specs=[any_spec] * 9,
            out_specs=(vmem_spec, any_spec, any_spec),
            scratch_shapes=[
                pltpu.VMEM(ln_gain.shape, F32), pltpu.VMEM(ln_bias.shape, F32), pltpu.VMEM(cos.shape, F32), pltpu.VMEM(sin.shape, F32), pltpu.VMEM((per, *seq_block), BF16),
                pltpu.VMEM((d_model, 2 * qkv_cols), BF16), pltpu.VMEM((2 * head_dim, d_model), BF16), pltpu.VMEM((2, d_model, ff // 2), BF16), pltpu.VMEM((2, ff // 2, d_model), BF16),
                pltpu.VMEM((tile, d_model), BF16), pltpu.VMEM((tile, head_dim), BF16), pltpu.VMEM((tile, ff), BF16), pltpu.VMEM((2, 2 * seq_len, d_model), F32),
                pltpu.VMEM((per, tile, d_model), BF16), pltpu.VMEM((4, tile, d_model), F32), pltpu.VMEM((per, 3, *seq_block), BF16),
                pltpu.VMEM((4, d_model, LANES), BF16), pltpu.VMEM((2, LANES, d_model), BF16),
                *sems("6 3 2 4"), dma((2,)), dma((2, (nz - 1) * (half - 1))), dma((2,)), dma((2, nz - 1, 2)),
                *sems("6 6 6"), dma((2, nz // 2, 6)), dma((nz + 1,)), *sems("6 3"), dma((3, 2)), *sems("6 6 4 6"), dma((2, per, nz // 2)), dma((per,)),
            ],
            compiler_params=pltpu.CompilerParams(collective_id=1, has_side_effects=True, vmem_limit_bytes=39 * MIB),
        )(act_in, ln_gain, ln_bias, cos, sin, w_qkv, w_out, w_up, w_down)[0]

    return jax.shard_map(shard_body, mesh=mesh, in_specs=(P("dp"), P(), P(), P(None, None, "tp"), P(None, "tp"), P(None, None, "tp"), P(None, "tp")), out_specs=P("dp"), check_vma=False)
```

time: 394 us -> 390 us (0.990)
  Pallas kernels: 385 us -> 381 us
    pallas_call x2 -> x1, Pallas kernels: 385 us -> 381 us  [shard_body(): pl.pallas_call(functools.partial(kernel, n_dp, n_tp), name='two_layers',...]
where the time goes in v5:
time: 390 us
  Pallas kernels  381 us (98%)
  local copies, waits for them, and re-layouts  8.92 us (2%)
    pallas_call x1, Pallas kernels, shard_body(): pl.pallas_call(functools.partial(kernel, n_dp, n_tp), name='two_layers',...  381 us
    unnamed x1, local copies, waits for them, and re-layouts  8.92 us

profile of v5, /device:TPU:21, one launch (start us, length us, event | category | flops | bytes accessed | tf_op | source)
XLA Modules:
  0.0 389.6 jit_solution(3290643030007039082)
XLA Ops:
  0.0 380.7 %two_layers.1 = (bf16[96,64,2048]{2,1,0:T(8,128)(2,1)S(1)}, bf16[28,2048,128]{2,1,0:T(8,128)(2,1)}, bf16[20,128,2048]{2,1,0:T(8,128)(2,1)}) custom-call(bf16[96,64,2048]{2,1,0:T(8,128)(2,1)} %x.1, f32[2,2048]{1,0:T(2,128)} %gains_h.1, f32[2,2048]{1,0:T(2,128)} %biases_h.1, f32[256,128]{1,0:T(8,128)} %constant.4.clone.cos_h, f32[256,128]{1,0:T(8,128)} %constant.5.clone.sin_h, ...), custom_call_target="tpu_custom_call" | custom-call | tf_op jit(solution)/shard_map/two_layers/pallas_call | solution.py:741
  380.7 8.9 %copy.11 = bf16[96,64,2048]{2,1,0:T(8,128)(2,1)} copy(bf16[96,64,2048]{2,1,0:T(8,128)(2,1)S(1)} %get-tuple-element.6) | data formatting | bytes 50331648

commit v6 on v5

--- a/solution.py
+++ b/solution.py
@@ -357,9 +357,12 @@
     def rows_of(member):
         return pl.ds(pl.multiple_of(member * seq_len, seq_len), seq_len)
 
+    def rows_sem(tile):
+        return n_recv.at[tile - 2] if isinstance(tile, int) and tile >= per - 2 else n_recv.at[tile // 2]
+
     def send_n(tile, peer):
         at = nall.at[tile, rows_of(q)]
-        return remote(at, at, n_send.at[tile], n_recv.at[tile // 2], me.peers[peer])
+        return remote(at, at, n_send.at[tile], rows_sem(tile), me.peers[peer])
 
     def compute(i, waits=(), then=None):
         slot = i % 3
@@ -542,8 +545,11 @@
                 piece_hops(kind)[3].wait()
         start(layer.slab_loads(number))
 
-    def await_pair(p):
-        settle(nall.at[pl.ds(2 * p, 2), pl.ds(0, 3 * seq_len)], n_recv.at[p])
+    def await_rows(which):
+        if which < 2:
+            settle(nall.at[pl.ds(2 * which, 2), pl.ds(0, 3 * seq_len)], n_recv.at[which])
+        else:
+            settle(nall.at[which, pl.ds(0, 3 * seq_len)], n_recv.at[which - 2])
 
     def send_part(k, peer):
         return remote(nall.at[k, rows_of(me.peer_q[peer])], part_in.at[k, peer], p_send.at[k], p_recv.at[k], me.peers[peer])
@@ -605,9 +611,9 @@
         settle(out.at[pl.ds(0, nz)], s_recv.at[k])
 
     def late_pair():
+        start_parts(2)
         for side in SIDES:
             start_n(per - 2 + side)
-        start_parts(2)
         start_parts(3)
         for side in SIDES:
             settle(out.at[pl.ds(0, nz - 1)], e_send.at[side])
@@ -643,7 +649,7 @@
     layer.clear(range(acc.shape[0]))
     actions = {
         "T": lambda rest: take_both(int(rest[0]), letters[rest[1]]),
-        "N": lambda rest: await_pair(int(rest)),
+        "N": lambda rest: await_rows(int(rest)),
         "L": lambda rest: start_slab(int(rest)),
         "M": lambda rest: start(layer.slab_loads(int(rest))),
         "W": lambda rest: layer.wait_slab(int(rest)),
@@ -682,27 +688,29 @@
         "S61 W5 S51 P2",
         "P3 Z M0 M1",
         "X0 G00 R7 E",
-        "G10 F G01 G11",
-        "G02 N2 G12 W0",
-        "S02 M2 W1 S12",
-        "G03 M3 W2 S22",
+        "G10 F G01 G20",
+        "G11 G02 G12 N4",
+        "G21 Y H4 G03",
+        "N5 H5 X2 W0",
+        "S02 M2 G13 W1",
+        "S12 M3 W2 S22",
         "M4 W3 S32 M5",
-        "W4 S42 G13 Y",
-        "H4 G04 G20 M6",
-        "H5 X2 W5 S52",
-        "G21 M7 W6 S62",
-        "G14 W7 S72 G30",
-        "Y H4 P4 H5",
-        "G22 G31 P5",
+        "G22 W4 S42 M6",
+        "W5 S52 M7 W6",
+        "S62 W7 S72 G30",
+        "Y H4 P4 G23",
+        "G31 H5 G14 P5",
     ], actions, late_step)
+    for name in "04 24".split():
+        stage(name)
     early = 2
     for k in range(early):
         drain(k)
-    for name in (*"40 32 50".split(), *"33 41 51".split()):
+    for name in (*"40 32 50".split(), *"41 51 33".split()):
         stage(name)
     for k in range(per):
         settle(part_in.at[k], p_send.at[k])
-    for name in (*"42 52 43 23".split(), *"34 53 24".split(), *"44 54".split()):
+    for name in (*"52 42 53".split(), *"43 44 34 54".split()):
         stage(name)
     for k in range(early, per):
         drain(k)
@@ -751,7 +759,7 @@
                 pltpu.VMEM((per, tile, d_model), BF16), pltpu.VMEM((4, tile, d_model), F32), pltpu.VMEM((per, 3, *seq_block), BF16),
                 pltpu.VMEM((4, d_model, LANES), BF16), pltpu.VMEM((2, LANES, d_model), BF16),
                 *sems("6 3 2 4"), dma((2,)), dma((2, (nz - 1) * (half - 1))), dma((2,)), dma((2, nz - 1, 2)),
-                *sems("6 6 6"), dma((2, nz // 2, 6)), dma((nz + 1,)), *sems("6 3"), dma((3, 2)), *sems("6 6 4 6"), dma((2, per, nz // 2)), dma((per,)),
+                *sems("6 6 6"), dma((2, nz // 2, 6)), dma((nz + 1,)), *sems("6 4"), dma((3, 2)), *sems("6 6 4 6"), dma((2, per, nz // 2)), dma((per,)),
             ],
             compiler_params=pltpu.CompilerParams(collective_id=1, has_side_effects=True, vmem_limit_bytes=39 * MIB),
         )(act_in, ln_gain, ln_bias, cos, sin, w_qkv, w_out, w_up, w_down)[0]

time: 390 us -> 390 us (level)
  no operation moved by 1% of the time
where the time goes in v6:
time: 390 us
  Pallas kernels  381 us (98%)
  local copies, waits for them, and re-layouts  8.92 us (2%)
    pallas_call x1, Pallas kernels, shard_body(): pl.pallas_call(functools.partial(kernel, n_dp, n_tp), name='two_layers',...  381 us
    unnamed x1, local copies, waits for them, and re-layouts  8.92 us

profile of v6, /device:TPU:21, one launch (start us, length us, event | category | flops | bytes accessed | tf_op | source)
XLA Modules:
  0.0 389.8 jit_solution(12248934567947837559)
XLA Ops:
  0.0 380.9 %two_layers.1 = (bf16[96,64,2048]{2,1,0:T(8,128)(2,1)S(1)}, bf16[28,2048,128]{2,1,0:T(8,128)(2,1)}, bf16[20,128,2048]{2,1,0:T(8,128)(2,1)}) custom-call(bf16[96,64,2048]{2,1,0:T(8,128)(2,1)} %x.1, f32[2,2048]{1,0:T(2,128)} %gains_h.1, f32[2,2048]{1,0:T(2,128)} %biases_h.1, f32[256,128]{1,0:T(8,128)} %constant.4.clone.cos_h, f32[256,128]{1,0:T(8,128)} %constant.5.clone.sin_h, ...), custom_call_target="tpu_custom_call" | custom-call | tf_op jit(solution)/shard_map/two_layers/pallas_call | solution.py:749
  380.9 8.9 %copy.11 = bf16[96,64,2048]{2,1,0:T(8,128)(2,1)} copy(bf16[96,64,2048]{2,1,0:T(8,128)(2,1)S(1)} %get-tuple-element.6) | data formatting | bytes 50331648

commit v7 on v6

--- a/solution.py
+++ b/solution.py
@@ -254,8 +254,8 @@
 def kernel(n_dp, n_tp, x, gains_h, biases_h, cos_h, sin_h, qkv, out_w, up, down,
            out, gcols, grows,
            gains, biases, cos_ref, sin_ref, done, qkv_v, out_v, up_v, down_v, normed, ctx, act, own, nall, acc, part_in, st_cols, st_rows,
-           w_sem, x_sem, sib_send, sib_recv, r_send, r_recv, e_send, e_recv,
-           st_sem, loc_sem, w_send, wr_recv, ws_recv, n_send, n_recv, slab_sem, p_send, p_recv, small_sem, g_send, g_recv, s_recv):
+           w_sem, x_sem, sib_send, sib_recv, r_send, r_recv, e_send,
+           st_sem, loc_sem, w_send, wr_recv, ws_recv, n_send, n_recv, slab_sem, p_send, p_recv, small_sem, g_send, s_recv):
     me = Place(n_dp, n_tp)
     me.greet()
     nz, core, z, q = me.nz, me.core, me.z, me.q
@@ -510,7 +510,7 @@
 
     def late_send(side, s, h):
         at, i = pl.ds(h * cut, cut), half * s + half - 1
-        return remote(out.at[ring_at(side, i), at], out.at[ring_at(side, i + half), at], e_send.at[side], e_recv.at[side, s, h], to[side])
+        return remote(out.at[ring_at(side, i), at], out.at[ring_at(side, i + half), at], e_send.at[side], r_recv.at[side, 2 * s + h], to[side])
 
     def late_step(s):
         for h in SIDES:
@@ -576,8 +576,8 @@
 
     def first_hops(k):
         at = out.at[seq_of(z, core, k)]
-        return [remote(at, at, g_send.at[k], g_recv.at[0, k, 0], me.right),
-                remote(at, at, g_send.at[k], g_recv.at[1, k, 0], me.left),
+        return [remote(at, at, g_send.at[k], wr_recv.at[0, 0, k], me.right),
+                remote(at, at, g_send.at[k], wr_recv.at[1, 0, k], me.left),
                 remote(at, at, g_send.at[k], s_recv.at[k], me.sib)]
 
     def reach(side, k):
@@ -586,7 +586,7 @@
 
     def passing(side, k, s, hop):
         at = out.at[seq_of(me.z_at(side, s), core, k)]
-        return remote(at, at, g_send.at[k], g_recv.at[side, k, hop], to[side])
+        return remote(at, at, g_send.at[k], wr_recv.at[side, hop, k], to[side])
 
     def stage(name):
         k, s = int(name[0]), int(name[1])
@@ -716,6 +716,13 @@
         drain(k)
 
 
+def store_kernel(src, dst, sem):
+    blocks = src.shape[0] // sem.shape[0]
+    copies = [pltpu.make_async_copy(src.at[pl.ds(i * blocks, blocks)], dst.at[pl.ds(i * blocks, blocks)], sem.at[i]) for i in range(sem.shape[0])]
+    start(copies)
+    wait(copies)
+
+
 def rope_rows(seq_len, head_dim, copies):
     inv_freq = ROPE_BASE ** (-2.0 * np.arange(head_dim // 2) / head_dim)
     angles = np.arange(seq_len)[:, None] * inv_freq[None, :]
@@ -746,7 +753,7 @@
         seq_block = (seq_len, d_model)
         n_cols, n_rows = n_tp + 3 * heads, n_tp + heads
         steps = nz * half
-        return pl.pallas_call(
+        gathered = pl.pallas_call(
             functools.partial(kernel, n_dp, n_tp),
             name="two_layers",
             out_shape=(pltpu.VMEM(act_in.shape, BF16), jax.ShapeDtypeStruct((n_cols, d_model, LANES), BF16), jax.ShapeDtypeStruct((n_rows, LANES, d_model), BF16)),
@@ -758,10 +765,19 @@
                 pltpu.VMEM((tile, d_model), BF16), pltpu.VMEM((tile, head_dim), BF16), pltpu.VMEM((tile, ff), BF16), pltpu.VMEM((2, 2 * seq_len, d_model), F32),
                 pltpu.VMEM((per, tile, d_model), BF16), pltpu.VMEM((4, tile, d_model), F32), pltpu.VMEM((per, 3, *seq_block), BF16),
                 pltpu.VMEM((4, d_model, LANES), BF16), pltpu.VMEM((2, LANES, d_model), BF16),
-                *sems("6 3 2 4"), dma((2,)), dma((2, (nz - 1) * (half - 1))), dma((2,)), dma((2, nz - 1, 2)),
-                *sems("6 6 6"), dma((2, nz // 2, 6)), dma((nz + 1,)), *sems("6 4"), dma((3, 2)), *sems("6 6 4 6"), dma((2, per, nz // 2)), dma((per,)),
+                *sems("6 3 2 4"), dma((2,)), dma((2, (nz - 1) * (half - 1))), dma((2,)),
+                *sems("6 6 6"), dma((2, nz // 2, 6)), dma((nz + 1,)), *sems("6 4"), dma((3, 2)), *sems("6 6 4 6"), dma((per,)),
             ],
             compiler_params=pltpu.CompilerParams(collective_id=1, has_side_effects=True, vmem_limit_bytes=39 * MIB),
         )(act_in, ln_gain, ln_bias, cos, sin, w_qkv, w_out, w_up, w_down)[0]
+        return pl.pallas_call(
+            store_kernel,
+            name="store",
+            out_shape=jax.ShapeDtypeStruct(act_in.shape, BF16),
+            in_specs=[vmem_spec],
+            out_specs=any_spec,
+            scratch_shapes=[dma((n_tp,))],
+            compiler_params=pltpu.CompilerParams(vmem_limit_bytes=MIB),
+        )(pltpu.with_memory_space_constraint(gathered, pltpu.VMEM))
 
     return jax.shard_map(shard_body, mesh=mesh, in_specs=(P("dp"), P(), P(), P(None, None, "tp"), P(None, "tp"), P(None, None, "tp"), P(None, "tp")), out_specs=P("dp"), check_vma=False)

time: 390 us -> 389 us (level)
  local copies, waits for them, and re-layouts: 8.92 us -> 0 us
  Pallas kernels: 381 us -> 389 us
    unnamed x1 -> x0, local copies, waits for them, and re-layouts: 8.92 us -> none
    pallas_call x0 -> x1, Pallas kernels: none -> 8.51 us  [shard_body(): pl.pallas_call(store_kernel, name='store', out_shape=jax.ShapeDtypeStruct...]
where the time goes in v7:
time: 389 us
  Pallas kernels  389 us (100%)
    pallas_call x1, Pallas kernels, shard_body(): pl.pallas_call(functools.partial(kernel, n_dp, n_tp), name='two_layers',...  380 us
    pallas_call x1, Pallas kernels, shard_body(): pl.pallas_call(store_kernel, name='store', out_shape=jax.ShapeDtypeStruct...  8.51 us

profile of v7, /device:TPU:21, one launch (start us, length us, event | category | flops | bytes accessed | tf_op | source)
XLA Modules:
  0.0 388.9 jit_solution(6796524171629695537)
XLA Ops:
  0.0 380.2 %two_layers.1 = (bf16[96,64,2048]{2,1,0:T(8,128)(2,1)S(1)}, bf16[28,2048,128]{2,1,0:T(8,128)(2,1)}, bf16[20,128,2048]{2,1,0:T(8,128)(2,1)}) custom-call(bf16[96,64,2048]{2,1,0:T(8,128)(2,1)} %x.1, f32[2,2048]{1,0:T(2,128)} %gains_h.1, f32[2,2048]{1,0:T(2,128)} %biases_h.1, f32[256,128]{1,0:T(8,128)} %constant.4.clone.cos_h, f32[256,128]{1,0:T(8,128)} %constant.5.clone.sin_h, ...), custom_call_target="tpu_custom_call" | custom-call | tf_op jit(solution)/shard_map/two_layers/pallas_call | solution.py:756
  380.2 8.5 %store.1 = bf16[96,64,2048]{2,1,0:T(8,128)(2,1)} custom-call(bf16[96,64,2048]{2,1,0:T(8,128)(2,1)S(1)} %get-tuple-element.6.src), custom_call_target="tpu_custom_call" | custom-call | tf_op jit(solution)/shard_map/store/pallas_call | solution.py:773

commit v8 on v7

--- a/solution.py
+++ b/solution.py
@@ -561,8 +561,7 @@
     def hand_out(k):
         settle(nall.at[k, pl.ds(0, 3 * seq_len)], n_send.at[k])
         layer.round_off(k)
-        if k not in (2, 3):
-            start_parts(k)
+        start_parts(k)
 
     def summed(k):
         settle(part_in.at[k], p_recv.at[k])
@@ -611,10 +610,7 @@
         settle(out.at[pl.ds(0, nz)], s_recv.at[k])
 
     def late_pair():
-        start_parts(2)
-        for side in SIDES:
-            start_n(per - 2 + side)
-        start_parts(3)
+        start_n(per - 2)
         for side in SIDES:
             settle(out.at[pl.ds(0, nz - 1)], e_send.at[side])
 
@@ -662,6 +658,7 @@
         "G": stage,
         "E": lambda rest: late_pair(),
         "F": lambda rest: layer.clear(SIDES),
+        "I": lambda rest: start_n(per - 1),
     }
     letters = {"U": UP, "D": DOWN, "Q": Q, "K": K, "V": V, "O": OUT}
     layer.run([
@@ -684,33 +681,33 @@
         "S60 T4U R2 L7",
         "W7 S70 P0 R3",
         "P1 H2 R4 H3",
-        "R5 S71 R6 M5",
-        "S61 W5 S51 P2",
-        "P3 Z M0 M1",
-        "X0 G00 R7 E",
-        "G10 F G01 G20",
-        "G11 G02 G12 N4",
-        "G21 Y H4 G03",
-        "N5 H5 X2 W0",
-        "S02 M2 G13 W1",
+        "R5 S71 M5 X0",
+        "R6 G00 R7 E",
+        "G10 S61 M0 W5",
+        "S51 M1 P2 I",
+        "P3 F G01 G11",
+        "G02 G20 N4 Y",
+        "H4 G12 G21 G03",
+        "N5 H5 X2 Z",
+        "W0 S02 M2 W1",
         "S12 M3 W2 S22",
         "M4 W3 S32 M5",
         "G22 W4 S42 M6",
-        "W5 S52 M7 W6",
-        "S62 W7 S72 G30",
-        "Y H4 P4 G23",
-        "G31 H5 G14 P5",
+        "W5 S52 G30 M7",
+        "W6 S62 W7 S72",
+        "G13 Y H4 P4",
+        "G04 G14 H5 G31",
+        "P5",
     ], actions, late_step)
-    for name in "04 24".split():
-        stage(name)
+    stage("23")
     early = 2
     for k in range(early):
         drain(k)
-    for name in (*"40 32 50".split(), *"41 51 33".split()):
+    for name in (*"40 32 50".split(), *"41 51 42".split()):
         stage(name)
     for k in range(per):
         settle(part_in.at[k], p_send.at[k])
-    for name in (*"52 42 53".split(), *"43 44 34 54".split()):
+    for name in (*"52 33 43 53".split(), *"54 24 44 34".split()):
         stage(name)
     for k in range(early, per):
         drain(k)

time: 389 us -> 391 us (level)
  no operation moved by 1% of the time
where the time goes in v8:
time: 391 us; the launch traced here: 390 us
  Pallas kernels  390 us (100%)
    pallas_call x1, Pallas kernels, shard_body(): pl.pallas_call(functools.partial(kernel, n_dp, n_tp), name='two_layers',...  381 us
    pallas_call x1, Pallas kernels, shard_body(): pl.pallas_call(store_kernel, name='store', out_shape=jax.ShapeDtypeStruct...  8.51 us

profile of v8, /device:TPU:21, one launch (start us, length us, event | category | flops | bytes accessed | tf_op | source)
XLA Modules:
  0.0 389.9 jit_solution(1825734385970419988)
XLA Ops:
  0.0 381.2 %two_layers.1 = (bf16[96,64,2048]{2,1,0:T(8,128)(2,1)S(1)}, bf16[28,2048,128]{2,1,0:T(8,128)(2,1)}, bf16[20,128,2048]{2,1,0:T(8,128)(2,1)}) custom-call(bf16[96,64,2048]{2,1,0:T(8,128)(2,1)} %x.1, f32[2,2048]{1,0:T(2,128)} %gains_h.1, f32[2,2048]{1,0:T(2,128)} %biases_h.1, f32[256,128]{1,0:T(8,128)} %constant.4.clone.cos_h, f32[256,128]{1,0:T(8,128)} %constant.5.clone.sin_h, ...), custom_call_target="tpu_custom_call" | custom-call | tf_op jit(solution)/shard_map/two_layers/pallas_call | solution.py:753
  381.2 8.5 %store.1 = bf16[96,64,2048]{2,1,0:T(8,128)(2,1)} custom-call(bf16[96,64,2048]{2,1,0:T(8,128)(2,1)S(1)} %get-tuple-element.6.src), custom_call_target="tpu_custom_call" | custom-call | tf_op jit(solution)/shard_map/store/pallas_call | solution.py:770

commit v9 on v7

--- a/solution.py
+++ b/solution.py
@@ -684,10 +684,10 @@
         "S60 T4U R2 L7",
         "W7 S70 P0 R3",
         "P1 H2 R4 H3",
-        "R5 S71 R6 M5",
-        "S61 W5 S51 P2",
-        "P3 Z M0 M1",
-        "X0 G00 R7 E",
+        "R5 S71 M5 S61",
+        "R6 W5 S51 P2",
+        "P3 G00 R7 E",
+        "Z M0 M1 X0",
         "G10 F G01 G20",
         "G11 G02 G12 N4",
         "G21 Y H4 G03",

time: 389 us -> 390 us (level)
  no operation moved by 1% of the time
where the time goes in v9:
time: 390 us
  Pallas kernels  390 us (100%)
    pallas_call x1, Pallas kernels, shard_body(): pl.pallas_call(functools.partial(kernel, n_dp, n_tp), name='two_layers',...  381 us
    pallas_call x1, Pallas kernels, shard_body(): pl.pallas_call(store_kernel, name='store', out_shape=jax.ShapeDtypeStruct...  8.51 us

profile of v9, /device:TPU:21, one launch (start us, length us, event | category | flops | bytes accessed | tf_op | source)
XLA Modules:
  0.0 389.7 jit_solution(14020267752354269536)
XLA Ops:
  0.0 381.0 %two_layers.1 = (bf16[96,64,2048]{2,1,0:T(8,128)(2,1)S(1)}, bf16[28,2048,128]{2,1,0:T(8,128)(2,1)}, bf16[20,128,2048]{2,1,0:T(8,128)(2,1)}) custom-call(bf16[96,64,2048]{2,1,0:T(8,128)(2,1)} %x.1, f32[2,2048]{1,0:T(2,128)} %gains_h.1, f32[2,2048]{1,0:T(2,128)} %biases_h.1, f32[256,128]{1,0:T(8,128)} %constant.4.clone.cos_h, f32[256,128]{1,0:T(8,128)} %constant.5.clone.sin_h, ...), custom_call_target="tpu_custom_call" | custom-call | tf_op jit(solution)/shard_map/two_layers/pallas_call | solution.py:756
  381.0 8.5 %store.1 = bf16[96,64,2048]{2,1,0:T(8,128)(2,1)} custom-call(bf16[96,64,2048]{2,1,0:T(8,128)(2,1)S(1)} %get-tuple-element.6.src), custom_call_target="tpu_custom_call" | custom-call | tf_op jit(solution)/shard_map/store/pallas_call | solution.py:773
